TPU v7x, 256 devices: a whole 4x4x8 slice. The times are simulated.
256 devices in a mesh: ent: 128 (over x, y, z_lo, core), grp: 2 (over z_hi).
Axes of the slice: x: 4, y: 4, z: 8 (z_hi: 2, z_lo: 4; z = z_hi * 4 + z_lo), core: 2. Of those that a mesh axis runs over, the one named last changes fastest.
Arguments:
- entity_table: bfloat16 [65536, 1024], P('ent'), may hold values from -2.5 to 2.5
- rel_phases: float32 [822, 512], replicated, may hold values from -3.1416 to 3.1416
- head_ids: int32 [65536], P(('ent', 'grp')), may hold values from 0 to 511
- rel_ids: int32 [65536], P(('ent', 'grp')), may hold values from 0 to 821
- target_pos: int32 [65536], P(('ent', 'grp')), may hold values from 0 to 511
- block_owner: int32 [4], replicated, may hold values from 0 to 127
- block_local: int32 [4], replicated, may hold values from 0 to 3
Outputs:
- losses: float32 [65536], P(('ent', 'grp'))
- head_grad: bfloat16 [65536, 1024], P(('ent', 'grp'))
- table_grad: bfloat16 [65536, 1024], P('ent')
- rel_grad: float32 [822, 512], replicated
Inputs may be any that keep to these rules, and one draw needn't show every extreme that they name: query q on device d (ent then grp) has head row (d // 2) * 512 + head_ids[q]. `target_pos`: position among the 512 candidates, block after block. Block b covers table rows from (block_owner[b] * 4 + block_local[b]) * 128 on; blocks may repeat.
All inputs are finite; a program needn't handle non-finite values.
Results may differ from a plain program's by a relative error of at most 0.0057.
Values may be sent and summed in bfloat16 or wider, within the bound.
No kernel may reach another device: no remote copies, remote signals or barrier semaphores. Data moves between devices by JAX's collectives and lax.ppermute only.
A program may use at most 64 MiB of HBM per device.

v0:
```python
import jax
import jax.numpy as jnp
from jax import lax
from jax.sharding import Mesh
from jax.sharding import PartitionSpec as P

BLK = 128
ENT = ("ent_0", "ent_1", "ent_2", "ent_3")
ENT_GRP = ("ent_0", "ent_1", "ent_2", "ent_3", "grp")


SOFTMAX_TEMPER = 2.0


def broadcast_by_axis(value, axes, root):
    value = jnp.where(lax.axis_index(axes) == root, value, jnp.zeros_like(value))
    for axis in axes:
        value = lax.psum(value, axis)
    return value


def joined_along(parts, dim):
    parts = jnp.moveaxis(parts, 0, dim)
    dims = parts.shape
    return parts.reshape(*dims[:dim], dims[dim] * dims[dim + 1], *dims[dim + 2 :])


def copy_for_each(value, axis):
    copies = jnp.broadcast_to(value, (lax.axis_size(axis), *value.shape))
    return lax.all_to_all(copies, axis, split_axis=0, concat_axis=0, tiled=True)


def gather_directly(value, axis, dim):
    return joined_along(copy_for_each(value, axis), dim)


def body(entity_table, rel_phases, head_ids, rel_ids, target_pos, block_owner, block_local):
    half_dim = rel_phases.shape[1]
    rel_count = rel_phases.shape[0]
    shard_rows = entity_table.shape[0]
    blocks_total = block_owner.shape[0]
    blank = jnp.zeros((blocks_total, BLK, 2 * half_dim), jnp.bfloat16)
    share = blocks_total // lax.axis_size("grp")
    offset = lax.axis_index("grp") * share

    def fetch_share(position, buffer):
        wanted = offset + position
        own_block = lax.dynamic_slice_in_dim(entity_table, block_local[wanted] * BLK, BLK, 0)
        arrived = broadcast_by_axis(own_block, ENT, block_owner[wanted])
        return lax.dynamic_update_slice_in_dim(buffer, arrived[None], position, 0)

    halves = lax.fori_loop(0, share, fetch_share, blank[:share])
    fetched = gather_directly(halves, "grp", 0)
    candidate_block = fetched.reshape(blocks_total * BLK, 2 * half_dim)
    heads = jnp.take(entity_table, head_ids, axis=0).astype(jnp.float32)
    angles = jnp.take(rel_phases, rel_ids, axis=0)
    cosine = jnp.cos(angles)
    sine = jnp.sin(angles)
    real_head = heads[:, :half_dim]
    imag_head = heads[:, half_dim:]
    real_query = real_head * cosine - imag_head * sine
    imag_query = real_head * sine + imag_head * cosine
    query_reduced_precision = jnp.concatenate([real_query, imag_query], axis=1).astype(jnp.bfloat16)
    candidate_norm = jnp.sum(jnp.square(candidate_block.astype(jnp.float32)), axis=1)
    inner_products = lax.dot_general(
        query_reduced_precision,
        candidate_block,
        (((1,), (1,)), ((), ())),
        preferred_element_type=jnp.float32,
    )
    logit_scores = (2.0 * inner_products - candidate_norm[None, :]) / SOFTMAX_TEMPER
    top = jnp.max(logit_scores, axis=1, keepdims=True)
    log_total = top[:, 0] + jnp.log(jnp.sum(jnp.exp(logit_scores - top), axis=1))
    picked = jnp.take_along_axis(logit_scores, target_pos[:, None], axis=1)[:, 0]
    losses = log_total - picked
    columns = jnp.arange(logit_scores.shape[1], dtype=jnp.int32)
    onehot = (columns[None, :] == target_pos[:, None]).astype(jnp.float32)
    softmax_weights = jnp.exp(logit_scores - log_total[:, None]) - onehot
    weights_reduced_precision = softmax_weights.astype(jnp.bfloat16)
    query_gradient = (
        2.0
        / SOFTMAX_TEMPER
        * jnp.dot(weights_reduced_precision, candidate_block, preferred_element_type=jnp.float32)
    )
    back_products = lax.dot_general(
        weights_reduced_precision,
        query_reduced_precision,
        (((0,), (0,)), ((), ())),
        preferred_element_type=jnp.float32,
    )
    candidate_gradient = (
        2.0
        / SOFTMAX_TEMPER
        * (
            back_products
            - jnp.sum(softmax_weights, axis=0)[:, None] * candidate_block.astype(jnp.float32)
        )
    )
    real_grad = query_gradient[:, :half_dim]
    imag_grad = query_gradient[:, half_dim:]
    head_grad = jnp.concatenate(
        [real_grad * cosine + imag_grad * sine, imag_grad * cosine - real_grad * sine], axis=1
    ).astype(jnp.bfloat16)
    angle_grad = imag_grad * real_query - real_grad * imag_query
    rel_part = jax.ops.segment_sum(angle_grad, rel_ids, num_segments=rel_count)
    summed, rel_grad = lax.psum((candidate_gradient, rel_part), ENT_GRP)
    block_numbers = jnp.arange(shard_rows // BLK, dtype=jnp.int32)
    selector = (
        (block_owner == lax.axis_index(ENT))[:, None]
        & (block_local[:, None] == block_numbers[None, :])
    ).astype(jnp.float32)
    placed = jnp.einsum(
        "jb,jrk->brk",
        selector,
        summed.reshape(blocks_total, BLK, 2 * half_dim),
        precision=lax.Precision.HIGHEST,
    )
    table_grad = placed.reshape(shard_rows, 2 * half_dim).astype(jnp.bfloat16)
    return (losses, head_grad, table_grad, rel_grad)


def solution(mesh):
    finer = Mesh(
        mesh.devices.reshape(4, 4, 4, 2, mesh.shape["grp"]),
        ("ent_0", "ent_1", "ent_2", "ent_3", "grp"),
    )
    placed = (P(ENT, None), P(), P(ENT_GRP), P(ENT_GRP), P(ENT_GRP), P(), P())
    return jax.shard_map(
        body,
        mesh=finer,
        in_specs=placed,
        out_specs=(P(ENT_GRP), P(ENT_GRP, None), P(ENT, None), P()),
        check_vma=False,
    )
```

profile of v0, /device:TPU:33, one launch (start us, length us, event | category | flops | bytes accessed | tf_op | source)
XLA Modules:
  0.0 715.9 jit_solution(12075199189034619199)
XLA Ops:
  8.0 377.7 %while.13 = (s32[]{:T(128)}, bf16[2,128,1024]{2,1,0:T(8,128)(2,1)S(1)}, s32[]{:T(128)}, s32[4]{0:T(128)}, s32[4]{0:T(128)}, /*index=5*/bf16[512,1024]{1,0:T(8,12...) while((s32[]{:T(128)}, ...), condition=%wide.region_5.6_spmd, body=%wide.region_0.5_spmd.sunk | while | flops 655389 | bytes 7340707 | solution.py:52
  8.1 1.3 dynamic_slice.27
  9.5 1.2 dynamic_slice.26
  12.0 1.7 dynamic-slice_select_fusion.2
  13.8 47.5 %all-reduce.9.cloned.1.call-done = bf16[128,1024]{1,0:T(8,128)(2,1)} async-done(((bf16[128,1024]{1,0:T(8,128)(2,1)}), bf16[128,1024]{1,0:T(8,128)(2,1)}) %all-reduce.9.cloned.1.call-update) | async-done | bytes 262160 | tf_op jit(solution)/shard_map/while/body/eval_jaxpr/psum | solution.py:18
  61.4 49.8 %all-reduce.11.cloned.1.call-done = bf16[128,1024]{1,0:T(8,128)(2,1)} async-done(((bf16[128,1024]{1,0:T(8,128)(2,1)}), bf16[128,1024]{1,0:T(8,128)(2,1)}) %all-reduce.11.cloned.1.call-update) | async-done | bytes 262160 | tf_op jit(solution)/shard_map/while/body/eval_jaxpr/psum | solution.py:18
  111.3 50.8 %all-reduce.13.cloned.1.call-done = bf16[128,1024]{1,0:T(8,128)(2,1)} async-done(((bf16[128,1024]{1,0:T(8,128)(2,1)}), bf16[128,1024]{1,0:T(8,128)(2,1)}) %all-reduce.13.cloned.1.call-update) | async-done | bytes 262160 | tf_op jit(solution)/shard_map/while/body/eval_jaxpr/psum | solution.py:18
  162.1 34.7 %all-reduce.15.cloned.1.call-done = bf16[1,128,1024]{2,1,0:T(8,128)(2,1)} async-done(((bf16[1,128,1024]{2,1,0:T(8,128)(2,1)}), bf16[1,128,1024]{2,1,0:T(8,128)(2,1)}) %all-reduce.15.cloned.1.call-update) | async-done | bytes 262160 | tf_op jit(solution)/shard_map/while/body/eval_jaxpr/psum | solution.py:18
  197.9 1.2 dynamic_slice.27
  199.1 1.2 dynamic_slice.26
  201.7 1.7 dynamic-slice_select_fusion.2
  203.5 45.8 %all-reduce.9.cloned.1.call-done = bf16[128,1024]{1,0:T(8,128)(2,1)} async-done(((bf16[128,1024]{1,0:T(8,128)(2,1)}), bf16[128,1024]{1,0:T(8,128)(2,1)}) %all-reduce.9.cloned.1.call-update) | async-done | bytes 262160 | tf_op jit(solution)/shard_map/while/body/eval_jaxpr/psum | solution.py:18
  249.3 49.6 %all-reduce.11.cloned.1.call-done = bf16[128,1024]{1,0:T(8,128)(2,1)} async-done(((bf16[128,1024]{1,0:T(8,128)(2,1)}), bf16[128,1024]{1,0:T(8,128)(2,1)}) %all-reduce.11.cloned.1.call-update) | async-done | bytes 262160 | tf_op jit(solution)/shard_map/while/body/eval_jaxpr/psum | solution.py:18
  299.0 50.8 %all-reduce.13.cloned.1.call-done = bf16[128,1024]{1,0:T(8,128)(2,1)} async-done(((bf16[128,1024]{1,0:T(8,128)(2,1)}), bf16[128,1024]{1,0:T(8,128)(2,1)}) %all-reduce.13.cloned.1.call-update) | async-done | bytes 262160 | tf_op jit(solution)/shard_map/while/body/eval_jaxpr/psum | solution.py:18
  349.9 34.9 %all-reduce.15.cloned.1.call-done = bf16[1,128,1024]{2,1,0:T(8,128)(2,1)} async-done(((bf16[1,128,1024]{2,1,0:T(8,128)(2,1)}), bf16[1,128,1024]{2,1,0:T(8,128)(2,1)}) %all-reduce.15.cloned.1.call-update) | async-done | bytes 262160 | tf_op jit(solution)/shard_map/while/body/eval_jaxpr/psum | solution.py:18
  385.8 1.1 broadcast_in_dim.60
  386.9 5.8 all-to-all-start
  392.8 1.2 gather_fusion
  395.2 3.2 fusion.25
  398.3 23.0 %all-to-all-done = bf16[2,2,128,1024]{3,2,1,0:T(8,128)(2,1)} async-done(((bf16[2,2,128,1024]{3,2,1,0:T(8,128)(2,1)}), bf16[2,2,128,1024]{3,2,1,0:T(8,128)(2,1)}, u32[]{:S(2)}, u32[]{:S(2)}) %all-to-all-start) | async-done | bytes 1048608 | tf_op jit(solution)/shard_map/all_to_all | solution.py:30
  421.3 1.5 multiply_reduce_fusion
  422.8 1.8 fusion.27
  424.6 2.3 gather_fusion.2
  428.0 1.7 fusion.23
  429.7 1.8 multiply_subtract_fusion
  431.6 2.7 copy.12
  434.3 3.9 scatter_custom_fusion
  439.3 2.3 add_convert_fusion
  442.4 259.7 %all-reduce.7.cloned.1.call-done = (f32[4,128,1024]{2,0,1:T(4,128)}, f32[822,512]{1,0:T(8,128)}) async-done(((f32[4,128,1024]{2,0,1:T(4,128)}, f32[822,512]{1,0:T(8,128)}), (f32[4,128,1024]{2,0,1:T(4,128)}, f32[822,512]{1,0:T(8,128)})) %all-reduce.7.cloned.1.call-update) | async-done | bytes 3780624 | tf_op jit(solution)/shard_map/psum | solution.py:106
  702.1 3.8 convolution_convert_fusion
  706.0 1.3 copy.13
  707.3 1.2 copy.27
  (64 shorter events, 6.5 us)
Async XLA Ops:
  8.0 386.0 %copy-start = (f32[822,512]{1,0:T(8,128)S(1)}, f32[822,512]{1,0:T(8,128)}, u32[]{:S(2)}) copy-start(f32[822,512]{1,0:T(8,128)} %param.10) | copy-start | bytes 5050372
  8.0 53.3 %all-reduce.9.cloned.1.call-start = ((), (), s32[]{:S(2)}) async-start(), calls=%async_computation.2 | async-start | bytes 524288 | tf_op jit(solution)/shard_map/while/body/eval_jaxpr/psum | solution.py:18
  13.7 97.4 %all-reduce.11.cloned.1.call-start = ((), (), s32[]{:S(2)}) async-start(), calls=%async_computation.3 | async-start | bytes 524288 | tf_op jit(solution)/shard_map/while/body/eval_jaxpr/psum | solution.py:18
  61.3 100.7 %all-reduce.13.cloned.1.call-start = ((), (), s32[]{:S(2)}) async-start(), calls=%async_computation.4 | async-start | bytes 524288 | tf_op jit(solution)/shard_map/while/body/eval_jaxpr/psum | solution.py:18
  111.2 85.6 %all-reduce.15.cloned.1.call-start = ((), (), s32[]{:S(2)}) async-start(), calls=%async_computation.5 | async-start | bytes 524288 | tf_op jit(solution)/shard_map/while/body/eval_jaxpr/psum | solution.py:18
  197.8 51.4 %all-reduce.9.cloned.1.call-start = ((), (), s32[]{:S(2)}) async-start(), calls=%async_computation.2 | async-start | bytes 524288 | tf_op jit(solution)/shard_map/while/body/eval_jaxpr/psum | solution.py:18
  203.4 95.5 %all-reduce.11.cloned.1.call-start = ((), (), s32[]{:S(2)}) async-start(), calls=%async_computation.3 | async-start | bytes 524288 | tf_op jit(solution)/shard_map/while/body/eval_jaxpr/psum | solution.py:18
  249.3 100.6 %all-reduce.13.cloned.1.call-start = ((), (), s32[]{:S(2)}) async-start(), calls=%async_computation.4 | async-start | bytes 524288 | tf_op jit(solution)/shard_map/while/body/eval_jaxpr/psum | solution.py:18
  299.0 85.8 %all-reduce.15.cloned.1.call-start = ((), (), s32[]{:S(2)}) async-start(), calls=%async_computation.5 | async-start | bytes 524288 | tf_op jit(solution)/shard_map/while/body/eval_jaxpr/psum | solution.py:18
  385.7 7.0 copy-start.10
  385.7 7.0 copy-start.9
  385.7 7.0 copy-start.8
  385.7 7.1 copy-start.1
  386.9 34.4 %all-to-all-start = ((bf16[2,2,128,1024]{3,2,1,0:T(8,128)(2,1)}), bf16[2,2,128,1024]{3,2,1,0:T(8,128)(2,1)}, u32[]{:S(2)}, u32[]{:S(2)}) async-start(bf16[2,2,128,1024]{3,2,1,0:T(8,128)(2,1)} %broadcast_in_dim.60), calls=%async_computation | async-start | bytes 2097152 | tf_op jit(solution)/shard_map/all_to_all | solution.py:30
  392.7 309.4 %all-reduce.7.cloned.1.call-start = ((), (), s32[]{:S(2)}) async-start(), calls=%async_computation.1 | async-start | bytes 7569408 | tf_op jit(solution)/shard_map/psum | solution.py:106
  395.0 3.3 copy-start.2
  398.3 28.6 %copy-start.6 = (bf16[256,512]{1,0:T(8,128)(2,1)}, bf16[256,512]{1,0:T(8,128)(2,1)S(1)}, u32[]{:S(2)}) copy-start(bf16[256,512]{1,0:T(8,128)(2,1)S(1)} %get-tuple-element.136) | copy-start | bytes 786436
  426.9 2.8 copy-start.7
  431.6 2.7 copy-start.4
  438.2 0.7 copy-start.12
  438.2 1.1 copy-start.3
  438.2 263.9 %copy-start.11 = (s32[4]{0:T(128)S(1)}, s32[4]{0:T(128)}, u32[]{:S(2)}) copy-start(s32[4]{0:T(128)} %get-tuple-element.267) | copy-start | bytes 52
  702.1 5.1 copy-start.5
Sparse Core Ops, SparseCore 0:
  13.9 47.4 all-reduce.8
  63.6 47.4 all-reduce.10
  113.8 48.2 all-reduce.12
  164.5 32.2 all-reduce.14
  203.5 45.6 all-reduce.8
  251.4 47.4 all-reduce.10
  301.6 48.2 all-reduce.12
  352.4 32.2 all-reduce.14
Sparse Core Ops, SparseCore 1:
  438.3 263.8 all-reduce.6
where the time goes:
time: 719 us; the launch traced here: 716 us
  waiting for transfers between devices  647 us (90%)
  local copies, waits for them, and re-layouts  18.8 us (3%)
  other arithmetic  16.4 us (2%)
  between operations  15.7 us (2%)
  matrix products  9.19 us (1%)
    psum x8, waiting for transfers between devices, broadcast_by_axis(): value = lax.psum(value, axis)  364 us
    psum x1, waiting for transfers between devices, body(): summed, rel_grad = lax.psum((candidate_gradient, rel_part), ENT_GRP)  260 us
    all_to_all x1, waiting for transfers between devices, copy_for_each(): return lax.all_to_all(copies, axis, split_axis=0, concat_axis=0, tiled=True)  23 us
  transfers between devices with their start and end apart: 10, of which 10 were waited for; matrix products, arithmetic and copies ran while one was open for 1% of the time, Pallas kernels for 0%

commit v1 on v0

v1 whole, which is shorter than its diff:
```python
import jax
import jax.numpy as jnp
from jax import lax
from jax.experimental import pallas as pl
from jax.experimental.pallas import tpu as pltpu
from jax.sharding import Mesh
from jax.sharding import PartitionSpec as P

BLK = 128
ENT = ("x", "y", "zl", "core")
ENT_GRP = ("x", "y", "zl", "core", "grp")
PLANE = ("x", "y")
LINE = ("zl", "grp")
SWAP = [(0, 1), (1, 0)]
BF = jnp.bfloat16
F32 = jnp.float32
NT = (((1,), (1,)), ((), ()))
TN = (((0,), (0,)), ((), ()))
VMEM = pl.BlockSpec(memory_space=pltpu.VMEM)
SMEM = pl.BlockSpec(memory_space=pltpu.SMEM)
RELS = 64
LIMIT = 60 * 1024 * 1024


def dot(a, b, dims=(((1,), (0,)), ((), ()))):
    return lax.dot_general(a, b, dims, preferred_element_type=F32)


def split_sum(ones, x, dims, ones_first):
    hi = x.astype(BF)
    lo = (x - hi.astype(F32)).astype(BF)
    if ones_first:
        return dot(ones, hi, dims) + dot(ones, lo, dims)
    return dot(hi, ones, dims) + dot(lo, ones, dims)


def main_kernel(
    core_ref, heads_ref, query_ref, own_ref, other_ref, target_ref, cos_ref, sin_ref,
    loss_ref, head_ref, keep_ref, send_ref, ang_keep_ref, ang_send_ref,
):
    rows, half = cos_ref.shape
    n = own_ref.shape[0]
    query = query_ref[...]
    cands = (own_ref[...], other_ref[...])
    target = jnp.broadcast_to(target_ref[...], (128, rows)).T[:, :1]
    ones8 = jnp.ones((8, 2 * half), BF)
    scores = []
    for cand in cands:
        wide = cand.astype(F32)
        norm = split_sum(ones8, wide * wide, NT, True)[:1]
        scores.append(dot(query, cand, NT) - 0.5 * norm)
    top = jnp.maximum(
        jnp.max(scores[0], axis=1, keepdims=True), jnp.max(scores[1], axis=1, keepdims=True)
    )
    exps = [jnp.exp(s - top) for s in scores]
    total = jnp.sum(exps[0], axis=1, keepdims=True) + jnp.sum(exps[1], axis=1, keepdims=True)
    lanes = lax.broadcasted_iota(jnp.int32, (rows, n), 1)
    hits = [lanes == target, lanes + n == target]
    picked = sum(jnp.sum(jnp.where(h, s, 0.0), axis=1, keepdims=True) for h, s in zip(hits, scores))
    loss = top + jnp.log(total) - picked
    loss_ref[...] = jnp.broadcast_to(loss, (rows, 128)).T[:1]
    scale = 1.0 / total
    ones_q = jnp.ones((rows, 128), BF)
    dquery = None
    for k in range(2):
        weights = exps[k] * scale - hits[k].astype(F32)
        low = weights.astype(BF)
        part = dot(low, cands[k])
        dquery = part if dquery is None else dquery + part
        column = split_sum(ones_q, weights, TN, False)[:, :1]
        grad = dot(low, query, TN) - column * cands[k].astype(F32)
        if k == 0:
            keep_ref[...] = grad
        else:
            send_ref[...] = grad.astype(BF)
    cosine = cos_ref[...]
    sine = sin_ref[...]
    heads = heads_ref[...].astype(F32)
    hr, hi = heads[:, :half], heads[:, half:]
    qr = hr * cosine - hi * sine
    qi = hr * sine + hi * cosine
    dr, di = dquery[:, :half], dquery[:, half:]
    head_ref[:, :half] = (dr * cosine + di * sine).astype(BF)
    head_ref[:, half:] = (di * cosine - dr * sine).astype(BF)
    ang = di * qr - dr * qi
    a, b = ang[:, : half // 2], ang[:, half // 2 :]
    first = core_ref[0] == 0
    ang_keep_ref[...] = jnp.where(first, a, b)
    ang_send_ref[...] = jnp.where(first, b, a)


def pack_kernel(ids_ref, keep_ref, got_ref, ang_ref, ang_got_ref, out_ref):
    pieces, piece_rows, width = out_ref.shape
    cand_rows = keep_ref.shape[0] // pieces
    grad = keep_ref[...] + got_ref[...].astype(F32)
    out_ref[:, :cand_rows, :] = grad.astype(BF).reshape(pieces, cand_rows, width)
    used = 13 * RELS
    rel = lax.broadcasted_iota(jnp.int32, (used, ids_ref.shape[1]), 0)
    pick = (rel == ids_ref[...]).astype(F32).astype(BF)
    q = ang_ref.shape[0]
    total = None
    for k, ref in enumerate((ang_ref, ang_got_ref)):
        x = ref[...]
        hi = x.astype(BF)
        lo = (x - hi.astype(F32)).astype(BF)
        sel = pick[:, k * q : (k + 1) * q]
        part = dot(sel, hi) + dot(sel, lo)
        total = part if total is None else total + part
    w = ang_ref.shape[1]
    total = total.astype(BF)
    rr = piece_rows - cand_rows
    for j in range(pieces):
        for k in range(width // w):
            if j < 13:
                at = j * RELS + k * rr
                out_ref[j, cand_rows:, k * w : (k + 1) * w] = total[at : at + rr]
            else:
                out_ref[j, cand_rows:, k * w : (k + 1) * w] = jnp.zeros((rr, w), BF)


def place_kernel(core_ref, me_ref, owner_ref, local_ref, own_ref, other_ref, table_ref, rel_ref):
    pieces, piece_rows, width = own_ref.shape
    cand_rows = piece_rows // 2
    rels, rel_width = rel_ref.shape
    w = rel_width // 2
    table_ref[...] = jnp.zeros_like(table_ref)
    core = core_ref[0]
    for b in range(4):
        g, h = b // 2, b % 2

        @pl.when(owner_ref[b] == me_ref[0])
        def _():
            start = pl.multiple_of(local_ref[b] * BLK, BLK)
            for j in range(pieces):
                at = pl.ds(start + j * 8, 8)
                lo, hi = g * 8, g * 8 + 8
                block = jnp.where(
                    core == h,
                    own_ref[j, lo:hi, :].astype(F32),
                    other_ref[j, lo:hi, :].astype(F32),
                )
                table_ref[at, :] = (table_ref[at, :].astype(F32) + block).astype(BF)

    rr = piece_rows - cand_rows
    for h in range(2):
        for j in range(pieces):
            for k in range(width // w):
                at = j * RELS + k * rr
                size = min(rr, rels - at)
                if size > 0:
                    cols = slice(k * w, (k + 1) * w)
                    rel_ref[at : at + size, h * w : (h + 1) * w] = jnp.where(
                        core == h,
                        own_ref[j, cand_rows : cand_rows + size, cols].astype(F32),
                        other_ref[j, cand_rows : cand_rows + size, cols].astype(F32),
                    )


def exchange(x, axes):
    return lax.all_to_all(x, axes, split_axis=0, concat_axis=0, tiled=True)


def copies(x, n):
    return jnp.broadcast_to(x[None], (n, *x.shape))


def body(entity_table, rel_phases, head_ids, rel_ids, target_pos, block_owner, block_local):
    half = rel_phases.shape[1]
    rels = rel_phases.shape[0]
    width = 2 * half
    queries = head_ids.shape[0]
    core = lax.axis_index("core")
    grp = lax.axis_index("grp")
    me = lax.axis_index(ENT)
    plane = lax.axis_size(PLANE)
    line = lax.axis_size(LINE)
    rows = BLK // plane

    def mine(b):
        block = lax.dynamic_slice_in_dim(entity_table, block_local[b] * BLK, BLK, 0)
        return jnp.where(block_owner[b] == me, block, jnp.zeros_like(block))

    ids_other = lax.ppermute(rel_ids, "core", SWAP)
    kept = mine(2 * grp + core)
    passed = lax.ppermute(mine(2 * grp + 1 - core), "core", SWAP)
    block = (kept + passed).reshape(plane, rows, width)
    piece = jnp.sum(exchange(block, PLANE).astype(F32), axis=0).astype(BF)
    pieces = exchange(copies(piece, line), LINE).reshape(line // 2, 2, rows, width)
    piece = jnp.sum(pieces.astype(F32), axis=0).astype(BF).reshape(2 * rows, width)
    own = exchange(copies(piece, plane), PLANE).reshape(2 * BLK, width)
    other = lax.ppermute(own, "core", SWAP)

    heads = jnp.take(entity_table, head_ids, axis=0)
    angles = jnp.take(rel_phases, rel_ids, axis=0)
    cosine = jnp.cos(angles)
    sine = jnp.sin(angles)
    wide = heads.astype(F32)
    hr, hi = wide[:, :half], wide[:, half:]
    query = jnp.concatenate([hr * cosine - hi * sine, hr * sine + hi * cosine], axis=1).astype(BF)
    b, t = target_pos // BLK, target_pos % BLK
    place = ((b % 2) ^ core) * (2 * BLK) + (t // rows) * (2 * rows) + (b // 2) * rows + t % rows
    core_at = core.astype(jnp.int32).reshape(1)

    n = 2 * BLK
    loss, head_grad, keep, send, ang_keep, ang_send = pl.pallas_call(
        main_kernel,
        out_shape=(
            jax.ShapeDtypeStruct((1, queries), F32),
            jax.ShapeDtypeStruct((queries, width), BF),
            jax.ShapeDtypeStruct((n, width), F32),
            jax.ShapeDtypeStruct((n, width), BF),
            jax.ShapeDtypeStruct((queries, half // 2), F32),
            jax.ShapeDtypeStruct((queries, half // 2), F32),
        ),
        in_specs=[SMEM] + [VMEM] * 7,
        out_specs=(VMEM,) * 6,
        compiler_params=pltpu.CompilerParams(vmem_limit_bytes=LIMIT),
        cost_estimate=pl.CostEstimate(
            flops=6 * queries * 2 * n * width, bytes_accessed=6_000_000, transcendentals=queries * n
        ),
        name="main_kernel",
    )(core_at, heads, query, own, other, place.reshape(1, queries), cosine, sine)

    got = lax.ppermute(send, "core", SWAP)
    ang_got = lax.ppermute(ang_send, "core", SWAP)
    ids = jnp.concatenate([rel_ids, ids_other]).reshape(1, 2 * queries)
    packed = pl.pallas_call(
        pack_kernel,
        out_shape=jax.ShapeDtypeStruct((plane, 4 * rows, width), BF),
        in_specs=[VMEM] * 5,
        out_specs=VMEM,
        compiler_params=pltpu.CompilerParams(vmem_limit_bytes=LIMIT),
        cost_estimate=pl.CostEstimate(
            flops=4 * queries * 1024 * half, bytes_accessed=4_000_000, transcendentals=0
        ),
        name="pack_kernel",
    )(ids, keep, got, ang_keep, ang_got)
    part = jnp.sum(exchange(packed, PLANE).astype(F32), axis=0).astype(BF)
    part = jnp.sum(exchange(copies(part, line), LINE).astype(F32), axis=0).astype(BF)
    own_sum = exchange(copies(part, plane), PLANE)
    other_sum = lax.ppermute(own_sum, "core", SWAP)
    table_grad, rel_grad = pl.pallas_call(
        place_kernel,
        out_shape=(
            jax.ShapeDtypeStruct(entity_table.shape, BF),
            jax.ShapeDtypeStruct((rels, half), F32),
        ),
        in_specs=[SMEM] * 4 + [VMEM] * 2,
        out_specs=(VMEM, VMEM),
        compiler_params=pltpu.CompilerParams(vmem_limit_bytes=LIMIT),
        cost_estimate=pl.CostEstimate(flops=1_000_000, bytes_accessed=5_000_000, transcendentals=0),
        name="place_kernel",
    )(core_at, me.astype(jnp.int32).reshape(1), block_owner, block_local, own_sum, other_sum)
    return loss.reshape(queries), head_grad, table_grad, rel_grad


def solution(mesh):
    finer = Mesh(
        mesh.devices.reshape(4, 4, 4, 2, mesh.shape["grp"]),
        ENT_GRP,
    )
    placed = (P(ENT, None), P(), P(ENT_GRP), P(ENT_GRP), P(ENT_GRP), P(), P())
    return jax.shard_map(
        body,
        mesh=finer,
        in_specs=placed,
        out_specs=(P(ENT_GRP), P(ENT_GRP, None), P(ENT, None), P()),
        check_vma=False,
    )
```

time: 719 us -> 142 us (0.20)
  waiting for transfers between devices: 647 us -> 19.3 us
  blocking collectives: 0 us -> 58.6 us
  starting transfers between devices: 6.15 us -> 26.5 us
  between operations: 15.7 us -> 3.42 us
  Pallas kernels: 0 us -> 12 us
  local copies, waits for them, and re-layouts: 18.8 us -> 8.78 us
  matrix products: 9.19 us -> 0 us
    psum x9 -> x0, waiting for transfers between devices: 624 us -> none  [the longest x8 364 us: broadcast_by_axis(): value = lax.psum(value, axis)]
    all_to_all x0 -> x3, blocking collectives: none -> 58.6 us  [exchange(): return lax.all_to_all(x, axes, split_axis=0, concat_axis=0, tiled=True)]
    all_to_all x1 -> x3, starting transfers between devices: 5.82 us -> 19 us  [exchange(): return lax.all_to_all(x, axes, split_axis=0, concat_axis=0, tiled=True)]
    pallas_call x0 -> x3, Pallas kernels: none -> 12 us  [the longest x1 5.55 us: body(): pl.pallas_call(main_kernel, out_shape=(jax.ShapeDtypeStruct((1, queries),...]
    dot_general x4 -> x0, matrix products: 9.19 us -> none  [the longest x1 3.83 us: body(): jnp.einsum('jb,jrk->brk', selector, summed.reshape(blocks_total, BLK, 2 *...]
    all_to_all x1 -> x3, waiting for transfers between devices: 23 us -> 15.1 us  [exchange(): return lax.all_to_all(x, axes, split_axis=0, concat_axis=0, tiled=True)]
    ppermute x0 -> x6, starting transfers between devices: none -> 7.47 us  [the longest x1 4.25 us: body(): other = lax.ppermute(own, 'core', SWAP)]
  transfers between devices with their start and end apart: 10 -> 9, of which waited for: 10 -> 5; matrix products, arithmetic and copies ran while one was open for 1% -> 9% of each run, Pallas kernels for 0% -> 0%
where the time goes in v1:
time: 142 us; the launch traced here: 141 us
  blocking collectives  58.6 us (41%)
  starting transfers between devices  26.5 us (19%)
  waiting for transfers between devices  19.3 us (14%)
  other arithmetic  13 us (9%)
  Pallas kernels  12 us (8%)
  local copies, waits for them, and re-layouts  8.78 us (6%)
  between operations  3.42 us (2%)
    all_to_all x3, blocking collectives, exchange(): return lax.all_to_all(x, axes, split_axis=0, concat_axis=0, tiled=True)  58.6 us
    all_to_all x3, starting transfers between devices, exchange(): return lax.all_to_all(x, axes, split_axis=0, concat_axis=0, tiled=True)  19 us
    all_to_all x3, waiting for transfers between devices, exchange(): return lax.all_to_all(x, axes, split_axis=0, concat_axis=0, tiled=True)  15.1 us
    pallas_call x1, Pallas kernels, body(): pl.pallas_call(main_kernel, out_shape=(jax.ShapeDtypeStruct((1, queries),...  5.55 us
    another operation x2, other arithmetic  5.49 us
    ppermute x1, starting transfers between devices, body(): other = lax.ppermute(own, 'core', SWAP)  4.25 us
    pallas_call x1, Pallas kernels, body(): pl.pallas_call(pack_kernel, out_shape=jax.ShapeDtypeStruct((plane, 4 * ro...  3.25 us
    pallas_call x1, Pallas kernels, body(): pl.pallas_call(place_kernel, out_shape=(jax.ShapeDtypeStruct(entity_table...  3.17 us
  transfers between devices with their start and end apart: 9, of which 5 were waited for; matrix products, arithmetic and copies ran while one was open for 9% of the time, Pallas kernels for 0%

profile of v1, /device:TPU:33, one launch (start us, length us, event | category | flops | bytes accessed | tf_op | source)
XLA Modules:
  0.0 141.5 jit_solution(2337903992521291271)
XLA Ops:
  0.7 1.5 %fusion.3 = (s32[1]{0:T(128)}, s32[1]{0:T(128)}, s32[1]{0:T(128)}, s32[1]{0:T(128)}) fusion(s32[4]{0:T(128)} %owner_ref.1, s32[]{:T(128)S(6)} %select_n.74, s32[]{:T(128)S(6)} %select_n.78, s32[4]{0:T(128)} %local_ref.1), kind=kLoop, calls=%fused_computation.35 | loop fusion | bytes 40 | tf_op jit(solution)/shard_map/dynamic_slice | solution.py:181
  3.4 1.0 dynamic-slice_select_fusion
  4.5 0.8 collective-permute-start
  5.2 0.7 compare_select_fusion.1
  7.2 0.7 compare_select_fusion
  7.9 1.7 %add_bitcast_fusion = bf16[16,8,1024]{2,1,0:T(8,128)(2,1)} fusion(bf16[128,1024]{1,0:T(8,128)(2,1)S(1)} %collective-permute-done, bf16[512,1024]{1,0:T(8,128)(2,1)} %param.7, s32[]{:T(128)S(6)} %select_n.76, pred[]{:T(512)S(6)} %eq.10), kind=kLoop, calls=%fused_computation.8 | loop fusion | flops 655360 | bytes 786437 | tf_op jit(solution)/shard_map/reshape | solution.py:186
  9.6 6.8 %all-to-all-start = ((bf16[16,8,1024]{2,1,0:T(8,128)(2,1)}), bf16[16,8,1024]{2,1,0:T(8,128)(2,1)S(1)}, u32[]{:S(2)}, u32[]{:S(2)}) async-start(bf16[16,8,1024]{2,1,0:T(8,128)(2,1)} %add_bitcast_fusion), calls=%async_computation | async-start | bytes 524288 | tf_op jit(solution)/shard_map/all_to_all | solution.py:160
  16.4 1.2 gather_fusion
  17.6 1.8 %gather_fusion.1 = f32[256,512]{1,0:T(8,128)} fusion(f32[822,512]{1,0:T(8,128)S(1)} %copy-done, s32[1024]{0:T(1024)S(1)} %pad_clamp_fusion), kind=kCustom, calls=%fused_computation.1 | custom fusion | bytes 1049600 | tf_op jit(solution)/shard_map/jit(_take)/gather | solution.py:194
  19.4 4.8 %all-to-all-done = bf16[16,8,1024]{2,1,0:T(8,128)(2,1)S(1)} async-done(((bf16[16,8,1024]{2,1,0:T(8,128)(2,1)}), bf16[16,8,1024]{2,1,0:T(8,128)(2,1)S(1)}, u32[]{:S(2)}, u32[]{:S(2)}) %all-to-all-start) | async-done | bytes 262176 | tf_op jit(solution)/shard_map/all_to_all | solution.py:160
  24.9 8.0 %all-to-all-start.1 = ((bf16[8,8,1024]{2,1,0:T(8,128)(2,1)}), bf16[8,8,1024]{2,1,0:T(8,128)(2,1)S(1)}, u32[]{:S(2)}, u32[]{:S(2)}) async-start(bf16[8,8,1024]{2,1,0:T(8,128)(2,1)} %broadcast_in_dim.55), calls=%async_computation.1 | async-start | bytes 262144 | tf_op jit(solution)/shard_map/all_to_all | solution.py:160
  32.9 1.0 fusion.2
  33.9 5.6 %all-to-all-done.1 = bf16[8,8,1024]{2,1,0:T(8,128)(2,1)S(1)} async-done(((bf16[8,8,1024]{2,1,0:T(8,128)(2,1)}), bf16[8,8,1024]{2,1,0:T(8,128)(2,1)S(1)}, u32[]{:S(2)}, u32[]{:S(2)}) %all-to-all-start.1) | async-done | bytes 131104 | tf_op jit(solution)/shard_map/all_to_all | solution.py:160
  39.5 0.9 broadcast_in_dim.57
  40.4 4.2 %all-to-all-start.2 = ((bf16[16,16,1024]{2,1,0:T(8,128)(2,1)}), bf16[16,16,1024]{2,1,0:T(8,128)(2,1)}, u32[]{:S(2)}, u32[]{:S(2)}) async-start(bf16[16,16,1024]{2,1,0:T(8,128)(2,1)} %broadcast_in_dim.57), calls=%async_computation.2 | async-start | bytes 1048576 | tf_op jit(solution)/shard_map/all_to_all | solution.py:160
  44.6 4.3 %subtract_convert_fusion = (bf16[256,512]{1,0:T(8,128)(2,1)S(1)}, f32[256,512]{1,0:T(8,128)S(1)}, f32[256,512]{1,0:T(8,128)}) fusion(f32[256,1024]{1,0:T(8,128)S(1)} %get-tuple-element.23, f32[256,512]{1,0:T(8,128)} %gather_fusion.1, pred[256]{0:T(512)(128)(4,1)S(1)} %compare_and_fusion), kind=kLoop, calls=%fused_computation.4 | loop fusion | flops 655360 | bytes 2883840 | tf_op jit(solution)/shard_map/convert.4
  48.9 4.7 %all-to-all-done.2 = bf16[16,16,1024]{2,1,0:T(8,128)(2,1)} async-done(((bf16[16,16,1024]{2,1,0:T(8,128)(2,1)}), bf16[16,16,1024]{2,1,0:T(8,128)(2,1)}, u32[]{:S(2)}, u32[]{:S(2)}) %all-to-all-start.2) | async-done | bytes 524320 | tf_op jit(solution)/shard_map/all_to_all | solution.py:160
  53.6 4.2 %collective-permute-start.1 = (bf16[256,1024]{1,0:T(8,128)(2,1)}, bf16[256,1024]{1,0:T(8,128)(2,1)S(1)}, u32[]{:S(2)}, u32[]{:S(2)}) collective-permute-start(bf16[256,1024]{1,0:T(8,128)(2,1)} %bitcast.8.own_ref), channel_id=1, source_target_pairs={{0,2},{2,0},{1,3},{3,1},{4,6},{6,4},{5,7},{7,5},{8,10},{10,8},{9,1... | collective-permute-start | bytes 1572872 | tf_op jit(solution)/shard_map/ppermute | solution.py:191
  57.8 1.2 add_convert_fusion
  59.1 0.9 pad_maximum_fusion.query_ref
  60.5 0.8 copy-done.5
  61.3 5.5 %main_kernel.1 = (f32[1,256]{1,0:T(1,128)}, bf16[256,1024]{1,0:T(8,128)(2,1)}, f32[256,1024]{1,0:T(8,128)}, bf16[256,1024]{1,0:T(8,128)(2,1)}, f32[256,256]{1,0:T(8,128)}, /*index=5*/f32[256,256]{1,0:T(8,128)}) custom-call(s32[1]{0:T(128)} %bitcast.core_ref, bf16[256,1024]{1,0:T(8,128)(2,1)} %get-tuple-element.24.heads_ref, ...), custom_call_target="tpu_custom_call" | custom-call | flops 805306368 | bytes 6000000 | tf_op jit(solution)/shard_map/main_kernel/pallas_call | solution.py:205
  67.5 1.9 %collective-permute-done.2 = s32[256]{0:T(256)S(1)} collective-permute-done((s32[256]{0:T(256)S(1)}, s32[256]{0:T(256)S(1)}, u32[]{:S(2)}, u32[]{:S(2)}) %collective-permute-start.2) | collective-permute-done | bytes 1056 | tf_op jit(solution)/shard_map/ppermute | solution.py:183
  70.0 0.7 copy-done.7
  70.9 3.3 %pack_kernel.1 = bf16[16,32,1024]{2,1,0:T(8,128)(2,1)} custom-call(s32[1,512]{1,0:T(1,128)} %bitcast.16, f32[256,1024]{1,0:T(8,128)} %get-tuple-element.14.keep_ref, bf16[256,1024]{1,0:T(8,128)(2,1)} %copy-done.6, f32[256,256]{1,0:T(8,128)} %get-tuple-element.16.ang_ref, f32[256,256]{1,0:T(8,128)} %copy-done.7), custom_call_target="tpu_custom_call" | custom-call | flops 536870912 | bytes 4000000 | tf_op jit(solution)/shard_map/pack_kernel/pallas_call | solution.py:227
  74.1 19.4 %all_to_all.30 = bf16[16,32,1024]{2,1,0:T(8,128)(2,1)S(1)} all-to-all(bf16[16,32,1024]{2,1,0:T(8,128)(2,1)} %pack_kernel.1), channel_id=1, replica_groups=mesh['x'=4,'y'=4,'zl'=4,'core'=2,'grp'=2] {'x','y'}, dimensions={0} | all-to-all | bytes 2097152 | tf_op jit(solution)/shard_map/all_to_all | solution.py:160
  93.8 16.2 %all_to_all.31 = bf16[8,32,1024]{2,1,0:T(8,128)(2,1)S(1)} all-to-all(bf16[8,32,1024]{2,1,0:T(8,128)(2,1)S(1)} %broadcast_in_dim.58), channel_id=1, replica_groups=mesh['x'=4,'y'=4,'zl'=4,'core'=2,'grp'=2] {'zl','grp'}, dimensions={0} | all-to-all | bytes 1048576 | tf_op jit(solution)/shard_map/all_to_all | solution.py:160
  110.3 22.9 %all_to_all.32.own_ref = bf16[16,32,1024]{2,1,0:T(8,128)(2,1)S(1)} all-to-all(bf16[16,32,1024]{2,1,0:T(8,128)(2,1)S(1)} %broadcast_in_dim.59), channel_id=1, replica_groups=mesh['x'=4,'y'=4,'zl'=4,'core'=2,'grp'=2] {'x','y'}, dimensions={0} | all-to-all | bytes 2097152 | tf_op jit(solution)/shard_map/all_to_all | solution.py:160
  133.2 1.9 %collective-permute-start.5 = (bf16[16,32,1024]{2,1,0:T(8,128)(2,1)S(1)}, bf16[16,32,1024]{2,1,0:T(8,128)(2,1)S(1)}, u32[]{:S(2)}, u32[]{:S(2)}) collective-permute-start(bf16[16,32,1024]{2,1,0:T(8,128)(2,1)S(1)} %all_to_all.32.own_ref), channel_id=1, source_target_pairs={{0,2},{2,0},{1,3},{3,1},{4,6},{6,4},{5,7},{7,5},{8,10},{10,8},{9,1... | collective-permute-start | bytes 3145736 | tf_op jit(solution)/shard_map/ppermute | solution.py:241
  135.0 2.3 %collective-permute-done.5.other_ref = bf16[16,32,1024]{2,1,0:T(8,128)(2,1)S(1)} collective-permute-done((bf16[16,32,1024]{2,1,0:T(8,128)(2,1)S(1)}, bf16[16,32,1024]{2,1,0:T(8,128)(2,1)S(1)}, u32[]{:S(2)}, u32[]{:S(2)}) %collective-permute-start.5) | collective-permute-done | bytes 1048608 | tf_op jit(solution)/shard_map/ppermute | solution.py:241
  137.3 1.0 copy-done.4
  138.3 3.2 %place_kernel.1 = (bf16[512,1024]{1,0:T(8,128)(2,1)}, f32[822,512]{1,0:T(8,128)}) custom-call(s32[1]{0:T(128)} %bitcast.core_ref, s32[1]{0:T(128)} %bitcast.11.me_ref, s32[4]{0:T(128)} %owner_ref.1, s32[4]{0:T(128)} %local_ref.1, bf16[16,32,1024]{2,1,0:T(8,128)(2,1)} %copy-done.3, bf16[16,32,1024]{2,1,0:T(8,128)(2,1)} %copy-done.4), custom_call_target="tpu_custom_call" | custom-call | flops 1000000 | bytes 5000000 | tf_op jit(solution)/shard_map/place_kernel/pallas_call | solution.py:242
  (39 shorter events, 3.2 us)
Async XLA Ops:
  0.6 17.0 %copy-start = (f32[822,512]{1,0:T(8,128)S(1)}, f32[822,512]{1,0:T(8,128)}, u32[]{:S(2)}) copy-start(f32[822,512]{1,0:T(8,128)} %param.8) | copy-start | bytes 5050372
  0.6 15.8 %copy-start.1 = (bf16[512,1024]{1,0:T(8,128)(2,1)S(1)}, bf16[512,1024]{1,0:T(8,128)(2,1)}, u32[]{:S(2)}) copy-start(bf16[512,1024]{1,0:T(8,128)(2,1)} %param.7) | copy-start | bytes 3145732
  4.5 3.4 %collective-permute-start = (bf16[128,1024]{1,0:T(8,128)(2,1)S(1)}, bf16[128,1024]{1,0:T(8,128)(2,1)S(1)}, u32[]{:S(2)}, u32[]{:S(2)}) collective-permute-start(bf16[128,1024]{1,0:T(8,128)(2,1)S(1)} %dynamic-slice_select_fusion), channel_id=1, source_target_pairs={{0,2},{2,0},{1,3},{3,1},{4,6},{6,4},{5,7},{7,5},{8,10},{10,8},{9,1... | collective-permute-start | bytes 786440 | tf_op jit(solution)/shard_map/ppermute | solution.py:185
  9.6 14.5 %all-to-all-start = ((bf16[16,8,1024]{2,1,0:T(8,128)(2,1)}), bf16[16,8,1024]{2,1,0:T(8,128)(2,1)S(1)}, u32[]{:S(2)}, u32[]{:S(2)}) async-start(bf16[16,8,1024]{2,1,0:T(8,128)(2,1)} %add_bitcast_fusion), calls=%async_computation | async-start | bytes 524288 | tf_op jit(solution)/shard_map/all_to_all | solution.py:160
  17.6 1.8 %copy-start.9 = (s32[256]{0:T(256)S(1)}, s32[256]{0:T(256)}, u32[]{:S(2)}) copy-start(s32[256]{0:T(256)} %param.9) | copy-start | bytes 3076
  24.9 14.6 %all-to-all-start.1 = ((bf16[8,8,1024]{2,1,0:T(8,128)(2,1)}), bf16[8,8,1024]{2,1,0:T(8,128)(2,1)S(1)}, u32[]{:S(2)}, u32[]{:S(2)}) async-start(bf16[8,8,1024]{2,1,0:T(8,128)(2,1)} %broadcast_in_dim.55), calls=%async_computation.1 | async-start | bytes 262144 | tf_op jit(solution)/shard_map/all_to_all | solution.py:160
  32.9 11.7 %copy-start.8 = (s32[256]{0:T(256)S(1)}, s32[256]{0:T(256)}, u32[]{:S(2)}) copy-start(s32[256]{0:T(256)} %param.10) | copy-start | bytes 3076
  40.4 13.2 %all-to-all-start.2 = ((bf16[16,16,1024]{2,1,0:T(8,128)(2,1)}), bf16[16,16,1024]{2,1,0:T(8,128)(2,1)}, u32[]{:S(2)}, u32[]{:S(2)}) async-start(bf16[16,16,1024]{2,1,0:T(8,128)(2,1)} %broadcast_in_dim.57), calls=%async_computation.2 | async-start | bytes 1048576 | tf_op jit(solution)/shard_map/all_to_all | solution.py:160
  48.9 11.1 %copy-start.2 = (f32[256,512]{1,0:T(8,128)}, f32[256,512]{1,0:T(8,128)S(1)}, u32[]{:S(2)}) copy-start(f32[256,512]{1,0:T(8,128)S(1)} %get-tuple-element.21.sin_ref) | copy-start | bytes 1572868
  53.6 7.0 %collective-permute-start.1 = (bf16[256,1024]{1,0:T(8,128)(2,1)}, bf16[256,1024]{1,0:T(8,128)(2,1)S(1)}, u32[]{:S(2)}, u32[]{:S(2)}) collective-permute-start(bf16[256,1024]{1,0:T(8,128)(2,1)} %bitcast.8.own_ref), channel_id=1, source_target_pairs={{0,2},{2,0},{1,3},{3,1},{4,6},{6,4},{5,7},{7,5},{8,10},{10,8},{9,1... | collective-permute-start | bytes 1572872 | tf_op jit(solution)/shard_map/ppermute | solution.py:191
  57.8 2.1 %copy-start.10 = (s32[256]{0:T(256)S(1)}, s32[256]{0:T(256)}, u32[]{:S(2)}) copy-start(s32[256]{0:T(256)} %param.11) | copy-start | bytes 3076
  60.5 0.8 copy-start.5
  66.9 3.1 %collective-permute-start.3 = (bf16[256,1024]{1,0:T(8,128)(2,1)}, bf16[256,1024]{1,0:T(8,128)(2,1)S(1)}, u32[]{:S(2)}, u32[]{:S(2)}) collective-permute-start(bf16[256,1024]{1,0:T(8,128)(2,1)} %get-tuple-element.15), channel_id=1, source_target_pairs={{0,2},{2,0},{1,3},{3,1},{4,6},{6,4},{5,7},{7,5},{8,10},{10,8},{9,1... | collective-permute-start | bytes 1572872 | tf_op jit(solution)/shard_map/ppermute | solution.py:224
  66.9 3.1 %collective-permute-start.4 = (f32[256,256]{1,0:T(8,128)}, f32[256,256]{1,0:T(8,128)S(1)}, u32[]{:S(2)}, u32[]{:S(2)}) collective-permute-start(f32[256,256]{1,0:T(8,128)} %get-tuple-element.17), channel_id=1, source_target_pairs={{0,2},{2,0},{1,3},{3,1},{4,6},{6,4},{5,7},{7,5},{8,10},{10,8},{9,1... | collective-permute-start | bytes 786440 | tf_op jit(solution)/shard_map/ppermute | solution.py:225
  67.4 2.0 %collective-permute-start.2 = (s32[256]{0:T(256)S(1)}, s32[256]{0:T(256)S(1)}, u32[]{:S(2)}, u32[]{:S(2)}) collective-permute-start(s32[256]{0:T(256)S(1)} %copy-done.8), channel_id=1, source_target_pairs={{0,2},{2,0},{1,3},{3,1},{4,6},{6,4},{5,7},{7,5},{8,10},{10,8},{9,1... | collective-permute-start | bytes 3080 | tf_op jit(solution)/shard_map/ppermute | solution.py:183
  70.0 0.7 copy-start.7
  70.0 0.9 copy-start.6
  133.2 4.2 %copy-start.3 = (bf16[16,32,1024]{2,1,0:T(8,128)(2,1)}, bf16[16,32,1024]{2,1,0:T(8,128)(2,1)S(1)}, u32[]{:S(2)}) copy-start(bf16[16,32,1024]{2,1,0:T(8,128)(2,1)S(1)} %all_to_all.32.own_ref) | copy-start | bytes 3145732
  133.2 4.2 %collective-permute-start.5 = (bf16[16,32,1024]{2,1,0:T(8,128)(2,1)S(1)}, bf16[16,32,1024]{2,1,0:T(8,128)(2,1)S(1)}, u32[]{:S(2)}, u32[]{:S(2)}) collective-permute-start(bf16[16,32,1024]{2,1,0:T(8,128)(2,1)S(1)} %all_to_all.32.own_ref), channel_id=1, source_target_pairs={{0,2},{2,0},{1,3},{3,1},{4,6},{6,4},{5,7},{7,5},{8,10},{10,8},{9,1... | collective-permute-start | bytes 3145736 | tf_op jit(solution)/shard_map/ppermute | solution.py:241
  137.3 1.0 copy-start.4

commit v2 on v1

v2 whole, which is shorter than its diff:
```python
import jax
import jax.numpy as jnp
from jax import lax
from jax.experimental import pallas as pl
from jax.experimental.pallas import tpu as pltpu
from jax.sharding import Mesh
from jax.sharding import PartitionSpec as P


BLK = 128
LANES = 128
ENT = ("x", "y", "zl", "core")
ENT_GRP = ("x", "y", "zl", "core", "grp")
PLANE = ("x", "y")
LINE = ("zl", "grp")
SWAP = [(0, 1), (1, 0)]
BF = jnp.bfloat16
F32 = jnp.float32
NT = (((1,), (1,)), ((), ()))
TN = (((0,), (0,)), ((), ()))
VMEM = pl.BlockSpec(memory_space=pltpu.VMEM)
SMEM = pl.BlockSpec(memory_space=pltpu.SMEM)
HBM = pl.BlockSpec(memory_space=pltpu.HBM)
MIB = 1024 * 1024


def dot(a, b, dims=(((1,), (0,)), ((), ()))):
    return lax.dot_general(a, b, dims, preferred_element_type=F32)


def halves(x):
    hi = x.astype(BF)
    return hi, (x - hi.astype(F32)).astype(BF)


def own_shard():
    place = lax.axis_index(ENT[0])
    for axis in ENT[1:]:
        place = place * lax.axis_size(axis) + lax.axis_index(axis)
    return place


def fetch_kernel(owner_ref, local_ref, table_ref, keep_ref, pass_ref, sem):
    core = lax.axis_index("core")
    grp = lax.axis_index("grp")
    me = own_shard()
    for b, out_ref in ((2 * grp + core, keep_ref), (2 * grp + 1 - core, pass_ref)):

        @pl.when(owner_ref[b] == me)
        def _():
            start = pl.multiple_of(local_ref[b] * BLK, BLK)
            copy = pltpu.make_async_copy(table_ref.at[pl.ds(start, BLK)], out_ref, sem)
            copy.start()
            copy.wait()

        @pl.when(owner_ref[b] != me)
        def _():
            out_ref[...] = jnp.zeros_like(out_ref)


def prep_kernel(
    heads_ref, angles_ref, target_ref, ids_ref, ids_other_ref,
    query_ref, cos_ref, sin_ref, spot_ref, pick_ref,
):
    half = cos_ref.shape[1]
    rows = query_ref.shape[0]
    angles = angles_ref[...]
    cosine = jnp.cos(angles)
    sine = jnp.sin(angles)
    cos_ref[...] = cosine
    sin_ref[...] = sine
    hr = heads_ref[:, :half].astype(F32)
    hi = heads_ref[:, half:].astype(F32)
    query_ref[:, :half] = (hr * cosine - hi * sine).astype(BF)
    query_ref[:, half:] = (hr * sine + hi * cosine).astype(BF)
    t = target_ref[...]
    core = lax.axis_index("core")
    block, row = t >> 7, t & 127
    spot = (((block & 1) ^ core) << 8) + ((row >> 3) << 4) + ((block >> 1) << 3) + (row & 7)
    spot_ref[...] = jnp.broadcast_to(spot, (LANES, rows)).T
    rel = lax.broadcasted_iota(jnp.int32, (pick_ref.shape[0], rows), 0)
    pick_ref[:, :rows] = (rel == ids_ref[...]).astype(F32).astype(BF)
    pick_ref[:, rows:] = (rel == ids_other_ref[...]).astype(F32).astype(BF)


def main_kernel(
    heads_ref, query_ref, own_ref, other_ref, spot_ref, cos_ref, sin_ref,
    loss_ref, head_ref, keep_ref, send_ref, ang_keep_ref, ang_send_ref,
):
    rows, half = cos_ref.shape
    n = own_ref.shape[0]
    query = query_ref[...]
    cands = (own_ref[...], other_ref[...])
    spot = spot_ref[:, :1]
    ones8 = jnp.ones((8, 2 * half), BF)
    scores = []
    for cand in cands:
        wide = cand.astype(F32)
        hi, lo = halves(wide * wide)
        norm = (dot(ones8, hi, NT) + dot(ones8, lo, NT))[:1]
        scores.append(dot(query, cand, NT) - 0.5 * norm)
    top = jnp.maximum(
        jnp.max(scores[0], axis=1, keepdims=True), jnp.max(scores[1], axis=1, keepdims=True)
    )
    exps = [jnp.exp(s - top) for s in scores]
    total = jnp.sum(exps[0], axis=1, keepdims=True) + jnp.sum(exps[1], axis=1, keepdims=True)
    lanes = lax.broadcasted_iota(jnp.int32, (rows, n), 1)
    hits = [lanes == spot, lanes + n == spot]
    picked = sum(jnp.sum(jnp.where(h, s, 0.0), axis=1, keepdims=True) for h, s in zip(hits, scores))
    loss = top + jnp.log(total) - picked
    loss_ref[...] = jnp.broadcast_to(loss, (rows, LANES)).T[:1]
    scale = 1.0 / total
    ones_q = jnp.ones((rows, LANES), BF)
    dquery = None
    for k in (1, 0):
        weights = exps[k] * scale - hits[k].astype(F32)
        low, rest = halves(weights)
        part = dot(low, cands[k])
        dquery = part if dquery is None else dquery + part
        column = (dot(low, ones_q, TN) + dot(rest, ones_q, TN))[:, :1]
        grad = dot(low, query, TN) - column * cands[k].astype(F32)
        if k == 0:
            keep_ref[...] = grad
        else:
            send_ref[...] = grad.astype(BF)
    cosine = cos_ref[...]
    sine = sin_ref[...]
    hr = heads_ref[:, :half].astype(F32)
    hi = heads_ref[:, half:].astype(F32)
    qr = hr * cosine - hi * sine
    qi = hr * sine + hi * cosine
    dr, di = dquery[:, :half], dquery[:, half:]
    head_ref[:, :half] = (dr * cosine + di * sine).astype(BF)
    head_ref[:, half:] = (di * cosine - dr * sine).astype(BF)
    ang = di * qr - dr * qi
    a, b = ang[:, : half // 2], ang[:, half // 2 :]
    first = lax.axis_index("core") == 0
    ang_keep_ref[...] = jnp.where(first, a, b)
    ang_send_ref[...] = jnp.where(first, b, a)


def pack_kernel(pick_ref, keep_ref, got_ref, ang_ref, ang_got_ref, out_ref):
    pieces = out_ref.shape[0]
    per = keep_ref.shape[0] // pieces
    groups = keep_ref.shape[1] // LANES
    for k in range(groups):
        cols = slice(k * LANES, (k + 1) * LANES)
        grad = keep_ref[:, cols] + got_ref[:, cols].astype(F32)
        out_ref[:, k * per : (k + 1) * per, :] = grad.astype(BF).reshape(pieces, per, LANES)
    q = ang_ref.shape[0]
    total = None
    for k, ref in enumerate((ang_ref, ang_got_ref)):
        sel = pick_ref[:, k * q : (k + 1) * q]
        hi, lo = halves(ref[...])
        part = dot(sel, hi) + dot(sel, lo)
        total = part if total is None else total + part
    total = total.astype(BF)
    base = groups * per
    size = out_ref.shape[1] - base
    row_groups = total.shape[0] // size
    for j in range(pieces):
        at = (j % row_groups) * size
        col = (j // row_groups) * LANES
        out_ref[j, base:, :] = total[at : at + size, col : col + LANES]


def place_kernel(owner_ref, local_ref, own_ref, other_ref, table_ref, rel_ref):
    pieces, piece_rows, _ = own_ref.shape
    groups = table_ref.shape[1] // LANES
    rels, rel_width = rel_ref.shape
    per = BLK // pieces
    table_ref[...] = jnp.zeros_like(table_ref)
    core = lax.axis_index("core")
    me = own_shard()
    for b in range(4):
        g, h = b // 2, b % 2

        def add(src_ref, g=g, b=b):
            start = pl.multiple_of(local_ref[b] * BLK, BLK)
            for k in range(groups):
                at = k * 2 * per + g * per
                block = src_ref[:, at : at + per, :].astype(F32).reshape(BLK, LANES)
                cols = slice(k * LANES, (k + 1) * LANES)
                old = table_ref[pl.ds(start, BLK), cols].astype(F32)
                table_ref[pl.ds(start, BLK), cols] = (old + block).astype(BF)

        mine = owner_ref[b] == me
        pl.when(mine & (core == h))(lambda add=add: add(own_ref))
        pl.when(mine & (core != h))(lambda add=add: add(other_ref))

    base = groups * 2 * per
    size = piece_rows - base
    row_groups = pieces * LANES * 2 // rel_width
    for h in range(2):

        def spread(src_ref, h=h):
            for j in range(pieces):
                at = (j % row_groups) * size
                rows = min(size, rels - at)
                col = h * (rel_width // 2) + (j // row_groups) * LANES
                rel_ref[at : at + rows, col : col + LANES] = src_ref[
                    j, base : base + rows, :
                ].astype(F32)

        pl.when(core == h)(lambda spread=spread: spread(own_ref))
        pl.when(core != h)(lambda spread=spread: spread(other_ref))


def exchange(x, axes):
    return lax.all_to_all(x, axes, split_axis=0, concat_axis=0, tiled=True)


def copies(x, n):
    return jnp.broadcast_to(x[None], (n, *x.shape))


def call(kernel, ins, specs, outs, grant, flops, nbytes, scratch=()):
    shapes = tuple(jax.ShapeDtypeStruct(s, d) for s, d in outs)
    single = len(shapes) == 1
    return pl.pallas_call(
        kernel,
        out_shape=shapes[0] if single else shapes,
        in_specs=specs,
        out_specs=VMEM if single else (VMEM,) * len(shapes),
        scratch_shapes=list(scratch),
        compiler_params=pltpu.CompilerParams(vmem_limit_bytes=grant),
        cost_estimate=pl.CostEstimate(flops=flops, bytes_accessed=nbytes, transcendentals=0),
    )(*ins)


def body(entity_table, rel_phases, head_ids, rel_ids, target_pos, block_owner, block_local):
    half = rel_phases.shape[1]
    rels = rel_phases.shape[0]
    width = 2 * half
    queries = head_ids.shape[0]
    plane = lax.axis_size(PLANE)
    line = lax.axis_size(LINE)
    rows = BLK // plane
    n = 2 * BLK
    rel_rows = -(-rels // 64) * 64
    piece_rows = n * width // (plane * LANES) + rel_rows * half // 2 // (plane * LANES)

    kept, passed = call(
        fetch_kernel, (block_owner, block_local, entity_table), [SMEM, SMEM, HBM],
        [((BLK, width), BF)] * 2, 2 * MIB, 100_000, 500_000, [pltpu.SemaphoreType.DMA],
    )
    passed = lax.ppermute(passed, "core", SWAP)
    ids_other = lax.ppermute(rel_ids, "core", SWAP)
    block = (kept + passed).reshape(plane, rows, width)
    block = exchange(block, PLANE)
    piece = jnp.sum(block.astype(F32), axis=0).astype(BF)
    pieces = exchange(copies(piece, line), LINE).reshape(line // 2, 2, rows, width)
    piece = jnp.sum(pieces.astype(F32), axis=0).astype(BF).reshape(2 * rows, width)
    own = exchange(copies(piece, plane), PLANE).reshape(n, width)
    other = lax.ppermute(own, "core", SWAP)

    heads = jnp.take(entity_table, head_ids, axis=0, mode="clip")
    angles = jnp.take(rel_phases, rel_ids, axis=0, mode="clip")
    query, cosine, sine, spot, pick = call(
        prep_kernel,
        (heads, angles, *(v.reshape(1, queries) for v in (target_pos, rel_ids, ids_other))),
        [VMEM] * 5,
        [((queries, width), BF), ((queries, half), F32), ((queries, half), F32),
         ((queries, LANES), jnp.int32), ((rel_rows, 2 * queries), BF)],
        12 * MIB, 100_000_000, 4_000_000,
    )

    loss, head_grad, keep, send, ang_keep, ang_send = call(
        main_kernel, (heads, query, own, other, spot, cosine, sine), [VMEM] * 7,
        [((1, queries), F32), ((queries, width), BF), ((n, width), F32), ((n, width), BF),
         ((queries, half // 2), F32), ((queries, half // 2), F32)],
        24 * MIB, 12 * queries * n * width, 6_000_000,
    )

    got = lax.ppermute(send, "core", SWAP)
    ang_got = lax.ppermute(ang_send, "core", SWAP)
    packed = call(
        pack_kernel, (pick, keep, got, ang_keep, ang_got), [VMEM] * 5,
        [((plane, piece_rows, LANES), BF)], 12 * MIB, 4 * rel_rows * queries * half, 4_000_000,
    )
    part = jnp.sum(exchange(packed, PLANE).astype(F32), axis=0).astype(BF)
    part = jnp.sum(exchange(copies(part, line), LINE).astype(F32), axis=0).astype(BF)
    own_sum = exchange(copies(part, plane), PLANE)
    other_sum = lax.ppermute(own_sum, "core", SWAP)
    table_grad, rel_grad = call(
        place_kernel, (block_owner, block_local, own_sum, other_sum), [SMEM, SMEM, VMEM, VMEM],
        [(entity_table.shape, BF), ((rels, half), F32)], 12 * MIB, 1_000_000, 5_000_000,
    )
    return loss.reshape(queries), head_grad, table_grad, rel_grad


def solution(mesh):
    finer = Mesh(mesh.devices.reshape(4, 4, 4, 2, mesh.shape["grp"]), ENT_GRP)
    placed = (P(ENT, None), P(), P(ENT_GRP), P(ENT_GRP), P(ENT_GRP), P(), P())
    return jax.shard_map(
        body,
        mesh=finer,
        in_specs=placed,
        out_specs=(P(ENT_GRP), P(ENT_GRP, None), P(ENT, None), P()),
        check_vma=False,
    )
```

time: 142 us -> 123 us (0.87)
  blocking collectives: 58.6 us -> 91.2 us
  starting transfers between devices: 26.5 us -> 9.77 us
  waiting for transfers between devices: 19.3 us -> 5.22 us
  other arithmetic: 13 us -> 0.3 us
  local copies, waits for them, and re-layouts: 8.78 us -> 5.09 us
  between operations: 3.42 us -> 0.81 us
  Pallas kernels: 12 us -> 10.5 us
    all_to_all x3 -> x6, blocking collectives: 58.6 us -> 91.2 us  [exchange(): return lax.all_to_all(x, axes, split_axis=0, concat_axis=0, tiled=True)]
    all_to_all x3 -> x0, starting transfers between devices: 19 us -> none  [exchange(): return lax.all_to_all(x, axes, split_axis=0, concat_axis=0, tiled=True)]
    all_to_all x3 -> x0, waiting for transfers between devices: 15.1 us -> none  [exchange(): return lax.all_to_all(x, axes, split_axis=0, concat_axis=0, tiled=True)]
    another operation x2 -> x0, other arithmetic: 5.49 us -> none
    select_n x3 -> x0, other arithmetic: 2.37 us -> none  [the longest x1 1 us: mine(): return jnp.where(block_owner[b] == me, block, jnp.zeros_like(block))]
    ppermute x1, starting transfers between devices: 1.87 us -> 4.12 us  [body(): other_sum = lax.ppermute(own_sum, 'core', SWAP)]
    ppermute x1, waiting for transfers between devices: 0.01 us -> 1.9 us  [body(): ang_got = lax.ppermute(ang_send, 'core', SWAP)]
    ppermute x1, waiting for transfers between devices: 1.9 us -> 0.01 us  [body(): ids_other = lax.ppermute(rel_ids, 'core', SWAP)]
  transfers between devices with their start and end apart: 9 -> 6, of which waited for: 5 -> 3; matrix products, arithmetic and copies ran while one was open for 9% -> 2% of each run, Pallas kernels for 0% -> 2%
where the time goes in v2:
time: 123 us
  blocking collectives  91.2 us (74%)
  Pallas kernels  10.5 us (9%)
  starting transfers between devices  9.77 us (8%)
  waiting for transfers between devices  5.22 us (4%)
  local copies, waits for them, and re-layouts  5.09 us (4%)
    all_to_all x6, blocking collectives, exchange(): return lax.all_to_all(x, axes, split_axis=0, concat_axis=0, tiled=True)  91.2 us
    pallas_call x5, Pallas kernels, call(): pl.pallas_call(kernel, out_shape=shapes[0] if single else shapes, in_spec...  10.5 us
    ppermute x1, starting transfers between devices, body(): other = lax.ppermute(own, 'core', SWAP)  4.37 us
    ppermute x1, starting transfers between devices, body(): other_sum = lax.ppermute(own_sum, 'core', SWAP)  4.12 us
    unnamed x20, local copies, waits for them, and re-layouts  2.7 us
  transfers between devices with their start and end apart: 6, of which 3 were waited for; matrix products, arithmetic and copies ran while one was open for 2% of the time, Pallas kernels for 2%

profile of v2, /device:TPU:33, one launch (start us, length us, event | category | flops | bytes accessed | tf_op | source)
XLA Modules:
  0.0 122.9 jit_solution(16505977196665798646)
XLA Ops:
  0.6 0.0 copy-start
  0.7 1.3 %copy-done.1 = bf16[512,1024]{1,0:T(8,128)(2,1)S(1)} copy-done((bf16[512,1024]{1,0:T(8,128)(2,1)S(1)}, bf16[512,1024]{1,0:T(8,128)(2,1)}, u32[]{:S(2)}) %copy-start.1) | copy-done | bytes 1048600
  2.0 0.7 copy-done.4
  2.7 0.7 copy-done.6
  3.3 0.6 shard_map.103
  3.9 0.8 collective-permute-start.1
  4.7 1.2 collective-permute-done.1
  5.9 0.0 copy-start.3
  5.9 14.2 %all_to_all.30 = bf16[16,8,1024]{2,1,0:T(8,128)(2,1)S(1)} all-to-all(bf16[16,8,1024]{2,1,0:T(8,128)(2,1)S(1)} %add_bitcast_fusion), channel_id=1, replica_groups=mesh['x'=4,'y'=4,'zl'=4,'core'=2,'grp'=2] {'x','y'}, dimensions={0} | all-to-all | bytes 524288 | tf_op jit(solution)/shard_map/all_to_all | solution.py:210
  20.2 14.4 %all_to_all.31 = bf16[8,8,1024]{2,1,0:T(8,128)(2,1)S(1)} all-to-all(bf16[8,8,1024]{2,1,0:T(8,128)(2,1)S(1)} %broadcast_in_dim.35), channel_id=1, replica_groups=mesh['x'=4,'y'=4,'zl'=4,'core'=2,'grp'=2] {'zl','grp'}, dimensions={0} | all-to-all | bytes 262144 | tf_op jit(solution)/shard_map/all_to_all | solution.py:210
  34.7 0.1 broadcast_in_dim.37
  34.7 12.6 %all_to_all.32 = bf16[16,16,1024]{2,1,0:T(8,128)(2,1)} all-to-all(bf16[16,16,1024]{2,1,0:T(8,128)(2,1)S(1)} %broadcast_in_dim.37), channel_id=1, replica_groups=mesh['x'=4,'y'=4,'zl'=4,'core'=2,'grp'=2] {'x','y'}, dimensions={0} | all-to-all | bytes 1048576 | tf_op jit(solution)/shard_map/all_to_all | solution.py:210
  47.3 4.4 %collective-permute-start.2 = (bf16[256,1024]{1,0:T(8,128)(2,1)}, bf16[256,1024]{1,0:T(8,128)(2,1)}, u32[]{:S(2)}, u32[]{:S(2)}) collective-permute-start(bf16[256,1024]{1,0:T(8,128)(2,1)} %bitcast.6.own_ref), channel_id=1, source_target_pairs={{0,2},{2,0},{1,3},{3,1},{4,6},{6,4},{5,7},{7,5},{8,10},{10,8},{9,1... | collective-permute-start | bytes 1572872 | tf_op jit(solution)/shard_map/ppermute | solution.py:255
  51.7 1.2 gather_fusion
  52.9 0.0 copy-start.8
  52.9 1.0 gather_fusion.1
  53.9 2.6 %shard_map.102 = (bf16[256,1024]{1,0:T(8,128)(2,1)S(1)}, f32[256,512]{1,0:T(8,128)S(1)}, f32[256,512]{1,0:T(8,128)S(1)}, s32[256,128]{1,0:T(8,128)S(1)}, bf16[832,512]{1,0:T(8,128)(2,1)S(1)}) custom-call(bf16[256,1024]{1,0:T(8,128)(2,1)S(1)} %gather_fusion, f32[256,512]{1,0:T(8,128)S(1)} %gather_fusion.1, s32[1,256]{1,0:T(1,128)S(1)} %bitcast.10, ...), custom_call_target="tpu_custom_call" | custom-call | flops 100000000 | bytes 4000000 | tf_op jit(solution)/shard_map/pallas_call | solution.py:220
  56.5 4.2 %shard_map.104 = (f32[1,256]{1,0:T(1,128)}, bf16[256,1024]{1,0:T(8,128)(2,1)}, f32[256,1024]{1,0:T(8,128)S(1)}, bf16[256,1024]{1,0:T(8,128)(2,1)S(1)}, f32[256,256]{1,0:T(8,128)S(1)}, /*index=5*/f32[256,256]{1,0:T(8,128)S(1)}) custom-call(bf16[256,1024]{1,0:T(8,128)(2,1)S(1)} %gather_fusion, bf16[256,1024]{1,0:T(8,128)(2,1)S(1)} %get-tuple-element.19.query_ref, ...), custom_call_target="tpu_custom_call" | custom-call | flops 805306368 | bytes 6000000 | tf_op jit(solution)/shard_map/pallas_call | solution.py:220
  60.7 0.5 collective-permute-start.3
  61.2 0.0 collective-permute-start.4
  61.2 1.9 %collective-permute-done.4.ang_got_ref = f32[256,256]{1,0:T(8,128)S(1)} collective-permute-done((f32[256,256]{1,0:T(8,128)S(1)}, f32[256,256]{1,0:T(8,128)S(1)}, u32[]{:S(2)}, u32[]{:S(2)}) %collective-permute-start.4) | collective-permute-done | bytes 262176 | tf_op jit(solution)/shard_map/ppermute | solution.py:276
  63.1 0.7 shard_map.105
  63.8 17.3 %all_to_all.33 = bf16[16,232,128]{2,1,0:T(8,128)(2,1)S(1)} all-to-all(bf16[16,232,128]{2,1,0:T(8,128)(2,1)S(1)} %shard_map.105), channel_id=1, replica_groups=mesh['x'=4,'y'=4,'zl'=4,'core'=2,'grp'=2] {'x','y'}, dimensions={0} | all-to-all | bytes 1900544 | tf_op jit(solution)/shard_map/all_to_all | solution.py:210
  81.1 0.1 reduce_sum.50
  81.3 0.1 broadcast_in_dim.38
  81.3 15.7 %all_to_all.34 = bf16[8,232,128]{2,1,0:T(8,128)(2,1)S(1)} all-to-all(bf16[8,232,128]{2,1,0:T(8,128)(2,1)S(1)} %broadcast_in_dim.38), channel_id=1, replica_groups=mesh['x'=4,'y'=4,'zl'=4,'core'=2,'grp'=2] {'zl','grp'}, dimensions={0} | all-to-all | bytes 950272 | tf_op jit(solution)/shard_map/all_to_all | solution.py:210
  97.0 0.1 reduce_sum.51
  97.1 0.1 broadcast_in_dim.39
  97.3 17.0 %all_to_all.35.own_ref = bf16[16,232,128]{2,1,0:T(8,128)(2,1)S(1)} all-to-all(bf16[16,232,128]{2,1,0:T(8,128)(2,1)S(1)} %broadcast_in_dim.39), channel_id=1, replica_groups=mesh['x'=4,'y'=4,'zl'=4,'core'=2,'grp'=2] {'x','y'}, dimensions={0} | all-to-all | bytes 1900544 | tf_op jit(solution)/shard_map/all_to_all | solution.py:210
  114.2 4.1 %collective-permute-start.5 = (bf16[16,232,128]{2,1,0:T(8,128)(2,1)S(1)}, bf16[16,232,128]{2,1,0:T(8,128)(2,1)S(1)}, u32[]{:S(2)}, u32[]{:S(2)}) collective-permute-start(bf16[16,232,128]{2,1,0:T(8,128)(2,1)S(1)} %all_to_all.35.own_ref), channel_id=1, source_target_pairs={{0,2},{2,0},{1,3},{3,1},{4,6},{6,4},{5,7},{7,5},{8,10},{10,8},{9,1... | collective-permute-start | bytes 2850824 | tf_op jit(solution)/shard_map/ppermute | solution.py:284
  118.3 2.1 %collective-permute-done.5.other_ref = bf16[16,232,128]{2,1,0:T(8,128)(2,1)S(1)} collective-permute-done((bf16[16,232,128]{2,1,0:T(8,128)(2,1)S(1)}, bf16[16,232,128]{2,1,0:T(8,128)(2,1)S(1)}, u32[]{:S(2)}, u32[]{:S(2)}) %collective-permute-start.5) | collective-permute-done | bytes 950304 | tf_op jit(solution)/shard_map/ppermute | solution.py:284
  120.5 2.4 %shard_map.106 = (bf16[512,1024]{1,0:T(8,128)(2,1)}, f32[822,512]{1,0:T(8,128)}) custom-call(s32[4]{0:T(128)S(1)} %copy-done.5, s32[4]{0:T(128)S(1)} %copy-done.7, bf16[16,232,128]{2,1,0:T(8,128)(2,1)S(1)} %all_to_all.35.own_ref, bf16[16,232,128]{2,1,0:T(8,128)(2,1)S(1)} %collective-permute-done.5.other_ref), custom_call_target="tpu_custom_call" | custom-call | flops 1000000 | bytes 5000000 | tf_op jit(solution)/shard_map/pallas_call | solution.py:220
  (24 shorter events, 0.2 us)
Async XLA Ops:
  0.6 52.3 %copy-start = (f32[822,512]{1,0:T(8,128)S(1)}, f32[822,512]{1,0:T(8,128)}, u32[]{:S(2)}) copy-start(f32[822,512]{1,0:T(8,128)} %param.8) | copy-start | bytes 5050372
  0.6 1.4 %copy-start.1 = (bf16[512,1024]{1,0:T(8,128)(2,1)S(1)}, bf16[512,1024]{1,0:T(8,128)(2,1)}, u32[]{:S(2)}) copy-start(bf16[512,1024]{1,0:T(8,128)(2,1)} %table_ref.1) | copy-start | bytes 3145732
  2.0 0.7 copy-start.4
  2.7 0.7 copy-start.6
  3.9 1.9 %collective-permute-start.1 = (bf16[128,1024]{1,0:T(8,128)(2,1)S(1)}, bf16[128,1024]{1,0:T(8,128)(2,1)S(1)}, u32[]{:S(2)}, u32[]{:S(2)}) collective-permute-start(bf16[128,1024]{1,0:T(8,128)(2,1)S(1)} %get-tuple-element.21), channel_id=1, source_target_pairs={{0,2},{2,0},{1,3},{3,1},{4,6},{6,4},{5,7},{7,5},{8,10},{10,8},{9,1... | collective-permute-start | bytes 786440 | tf_op jit(solution)/shard_map/ppermute | solution.py:247
  5.9 45.8 %copy-start.3 = (s32[256]{0:T(256)S(1)}, s32[256]{0:T(256)}, u32[]{:S(2)}) copy-start(s32[256]{0:T(256)} %param.10) | copy-start | bytes 3076
  5.9 45.8 %copy-start.9 = (s32[256]{0:T(256)S(1)}, s32[256]{0:T(256)}, u32[]{:S(2)}) copy-start(s32[256]{0:T(256)} %param.9) | copy-start | bytes 3076
  5.9 45.8 %copy-start.2 = (bf16[512,1024]{1,0:T(8,128)(2,1)S(1)}, bf16[512,1024]{1,0:T(8,128)(2,1)}, u32[]{:S(2)}) copy-start(bf16[512,1024]{1,0:T(8,128)(2,1)} %table_ref.1) | copy-start | bytes 3145732
  47.3 9.2 %collective-permute-start.2 = (bf16[256,1024]{1,0:T(8,128)(2,1)}, bf16[256,1024]{1,0:T(8,128)(2,1)}, u32[]{:S(2)}, u32[]{:S(2)}) collective-permute-start(bf16[256,1024]{1,0:T(8,128)(2,1)} %bitcast.6.own_ref), channel_id=1, source_target_pairs={{0,2},{2,0},{1,3},{3,1},{4,6},{6,4},{5,7},{7,5},{8,10},{10,8},{9,1... | collective-permute-start | bytes 1572872 | tf_op jit(solution)/shard_map/ppermute | solution.py:255
  51.7 2.2 %collective-permute-start = (s32[256]{0:T(256)S(1)}, s32[256]{0:T(256)S(1)}, u32[]{:S(2)}, u32[]{:S(2)}) collective-permute-start(s32[256]{0:T(256)S(1)} %copy-done.3), channel_id=1, source_target_pairs={{0,2},{2,0},{1,3},{3,1},{4,6},{6,4},{5,7},{7,5},{8,10},{10,8},{9,1... | collective-permute-start | bytes 3080 | tf_op jit(solution)/shard_map/ppermute | solution.py:248
  52.9 1.0 copy-start.8
  60.7 2.4 %collective-permute-start.3 = (bf16[256,1024]{1,0:T(8,128)(2,1)S(1)}, bf16[256,1024]{1,0:T(8,128)(2,1)S(1)}, u32[]{:S(2)}, u32[]{:S(2)}) collective-permute-start(bf16[256,1024]{1,0:T(8,128)(2,1)S(1)} %get-tuple-element.29), channel_id=1, source_target_pairs={{0,2},{2,0},{1,3},{3,1},{4,6},{6,4},{5,7},{7,5},{8,10},{10,8},{9,1... | collective-permute-start | bytes 1572872 | tf_op jit(solution)/shard_map/ppermute | solution.py:275
  61.2 1.9 %collective-permute-start.4 = (f32[256,256]{1,0:T(8,128)S(1)}, f32[256,256]{1,0:T(8,128)S(1)}, u32[]{:S(2)}, u32[]{:S(2)}) collective-permute-start(f32[256,256]{1,0:T(8,128)S(1)} %get-tuple-element.31), channel_id=1, source_target_pairs={{0,2},{2,0},{1,3},{3,1},{4,6},{6,4},{5,7},{7,5},{8,10},{10,8},{9,1... | collective-permute-start | bytes 786440 | tf_op jit(solution)/shard_map/ppermute | solution.py:276
  97.0 23.4 %copy-start.5 = (s32[4]{0:T(128)S(1)}, s32[4]{0:T(128)}, u32[]{:S(2)}) copy-start(s32[4]{0:T(128)} %owner_ref.3) | copy-start | bytes 52
  97.0 23.4 %copy-start.7 = (s32[4]{0:T(128)S(1)}, s32[4]{0:T(128)}, u32[]{:S(2)}) copy-start(s32[4]{0:T(128)} %local_ref.3) | copy-start | bytes 52
  114.2 6.3 %collective-permute-start.5 = (bf16[16,232,128]{2,1,0:T(8,128)(2,1)S(1)}, bf16[16,232,128]{2,1,0:T(8,128)(2,1)S(1)}, u32[]{:S(2)}, u32[]{:S(2)}) collective-permute-start(bf16[16,232,128]{2,1,0:T(8,128)(2,1)S(1)} %all_to_all.35.own_ref), channel_id=1, source_target_pairs={{0,2},{2,0},{1,3},{3,1},{4,6},{6,4},{5,7},{7,5},{8,10},{10,8},{9,1... | collective-permute-start | bytes 2850824 | tf_op jit(solution)/shard_map/ppermute | solution.py:284

commit v3 on v2

--- a/solution.py
+++ b/solution.py
@@ -12,7 +12,7 @@
 ENT = ("x", "y", "zl", "core")
 ENT_GRP = ("x", "y", "zl", "core", "grp")
 PLANE = ("x", "y")
-LINE = ("zl", "grp")
+LINE = ("grp", "zl")
 SWAP = [(0, 1), (1, 0)]
 BF = jnp.bfloat16
 F32 = jnp.float32
@@ -22,6 +22,7 @@
 SMEM = pl.BlockSpec(memory_space=pltpu.SMEM)
 HBM = pl.BlockSpec(memory_space=pltpu.HBM)
 MIB = 1024 * 1024
+FETCH = 56_000_000
 
 
 def dot(a, b, dims=(((1,), (0,)), ((), ()))):
@@ -58,21 +59,41 @@
             out_ref[...] = jnp.zeros_like(out_ref)
 
 
-def prep_kernel(
-    heads_ref, angles_ref, target_ref, ids_ref, ids_other_ref,
-    query_ref, cos_ref, sin_ref, spot_ref, pick_ref,
-):
-    half = cos_ref.shape[1]
-    rows = query_ref.shape[0]
-    angles = angles_ref[...]
-    cosine = jnp.cos(angles)
-    sine = jnp.sin(angles)
-    cos_ref[...] = cosine
-    sin_ref[...] = sine
+def turn_kernel(ids_ref, phases_ref, cos_ref, sin_ref):
+    def take(i, carry):
+        cos_ref[pl.ds(i, 1), :] = phases_ref[pl.ds(ids_ref[i], 1), :]
+        return carry
+
+    lax.fori_loop(0, cos_ref.shape[0], take, 0, unroll=8)
+    angles = cos_ref[...]
+    cos_ref[...] = jnp.cos(angles)
+    sin_ref[...] = jnp.sin(angles)
+
+
+def rotated(heads_ref, cosine, sine):
+    half = cosine.shape[1]
     hr = heads_ref[:, :half].astype(F32)
     hi = heads_ref[:, half:].astype(F32)
-    query_ref[:, :half] = (hr * cosine - hi * sine).astype(BF)
-    query_ref[:, half:] = (hr * sine + hi * cosine).astype(BF)
+    return hr * cosine - hi * sine, hr * sine + hi * cosine
+
+
+def scored(query, cand):
+    wide = cand.astype(F32)
+    hi, lo = halves(wide * wide)
+    ones = jnp.ones((8, cand.shape[1]), BF)
+    norm = (dot(ones, hi, NT) + dot(ones, lo, NT))[:1]
+    return dot(query, cand, NT) - 0.5 * norm
+
+
+def early_kernel(
+    heads_ref, cos_ref, sin_ref, target_ref, ids_ref, ids_other_ref, own_ref,
+    query_ref, spot_ref, pick_ref, scores_ref,
+):
+    rows, half = cos_ref.shape
+    qr, qi = rotated(heads_ref, cos_ref[...], sin_ref[...])
+    query_ref[:, :half] = qr.astype(BF)
+    query_ref[:, half:] = qi.astype(BF)
+    scores_ref[...] = scored(query_ref[...], own_ref[...])
     t = target_ref[...]
     core = lax.axis_index("core")
     block, row = t >> 7, t & 127
@@ -84,7 +105,7 @@
 
 
 def main_kernel(
-    heads_ref, query_ref, own_ref, other_ref, spot_ref, cos_ref, sin_ref,
+    heads_ref, query_ref, scores_ref, own_ref, other_ref, spot_ref, cos_ref, sin_ref,
     loss_ref, head_ref, keep_ref, send_ref, ang_keep_ref, ang_send_ref,
 ):
     rows, half = cos_ref.shape
@@ -92,13 +113,7 @@
     query = query_ref[...]
     cands = (own_ref[...], other_ref[...])
     spot = spot_ref[:, :1]
-    ones8 = jnp.ones((8, 2 * half), BF)
-    scores = []
-    for cand in cands:
-        wide = cand.astype(F32)
-        hi, lo = halves(wide * wide)
-        norm = (dot(ones8, hi, NT) + dot(ones8, lo, NT))[:1]
-        scores.append(dot(query, cand, NT) - 0.5 * norm)
+    scores = [scores_ref[...], scored(query, cands[1])]
     top = jnp.maximum(
         jnp.max(scores[0], axis=1, keepdims=True), jnp.max(scores[1], axis=1, keepdims=True)
     )
@@ -125,10 +140,7 @@
             send_ref[...] = grad.astype(BF)
     cosine = cos_ref[...]
     sine = sin_ref[...]
-    hr = heads_ref[:, :half].astype(F32)
-    hi = heads_ref[:, half:].astype(F32)
-    qr = hr * cosine - hi * sine
-    qi = hr * sine + hi * cosine
+    qr, qi = rotated(heads_ref, cosine, sine)
     dr, di = dquery[:, :half], dquery[:, half:]
     head_ref[:, :half] = (dr * cosine + di * sine).astype(BF)
     head_ref[:, half:] = (di * cosine - dr * sine).astype(BF)
@@ -164,46 +176,88 @@
         out_ref[j, base:, :] = total[at : at + size, col : col + LANES]
 
 
-def place_kernel(owner_ref, local_ref, own_ref, other_ref, table_ref, rel_ref):
-    pieces, piece_rows, _ = own_ref.shape
-    groups = table_ref.shape[1] // LANES
-    rels, rel_width = rel_ref.shape
-    per = BLK // pieces
-    table_ref[...] = jnp.zeros_like(table_ref)
+def block_of(src_ref, g, k):
+    per = BLK // src_ref.shape[0]
+    at = (k * 2 + g) * per
+    return src_ref[:, at : at + per, :].astype(F32).reshape(BLK, LANES)
+
+
+def spread(src_ref, part_ref):
+    pieces, piece_rows, _ = src_ref.shape
+    row_groups = pieces * LANES // part_ref.shape[1]
+    base = 2 * BLK * 8 // pieces
+    size = piece_rows - base
+    for j in range(pieces):
+        at = (j % row_groups) * size
+        rows = min(size, part_ref.shape[0] - at)
+        col = (j // row_groups) * LANES
+        part_ref[at : at + rows, col : col + LANES] = src_ref[j, base : base + rows, :].astype(F32)
+
+
+def half_columns(rel_ref, part_ref, half):
+    w = part_ref.shape[1]
+    return rel_ref.at[:, pl.ds(pl.multiple_of(half * w, w), w)]
+
+
+def place_own_kernel(owner_ref, local_ref, own_ref, table_ref, rel_ref, rows_ref, part_ref, sems):
     core = lax.axis_index("core")
     me = own_shard()
-    for b in range(4):
-        g, h = b // 2, b % 2
-
-        def add(src_ref, g=g, b=b):
-            start = pl.multiple_of(local_ref[b] * BLK, BLK)
+    rows_ref[...] = jnp.zeros_like(rows_ref)
+    for g in range(2):
+        b = 2 * g + core
+
+        @pl.when(owner_ref[b] == me)
+        def _():
+            at = pl.ds(pl.multiple_of(local_ref[b] * BLK, BLK), BLK)
+            for k in range(rows_ref.shape[1] // LANES):
+                cols = slice(k * LANES, (k + 1) * LANES)
+                old = rows_ref[at, cols].astype(F32)
+                rows_ref[at, cols] = (old + block_of(own_ref, g, k)).astype(BF)
+
+    table = pltpu.make_async_copy(rows_ref, table_ref, sems.at[0])
+    table.start()
+    spread(own_ref, part_ref)
+    part = pltpu.make_async_copy(part_ref, half_columns(rel_ref, part_ref, core), sems.at[1])
+    part.start()
+    table.wait()
+    part.wait()
+
+
+def place_other_kernel(
+    owner_ref, local_ref, own_ref, other_ref, table_in_ref, rel_in_ref,
+    table_ref, rel_ref, rows_ref, sum_ref, part_ref, sems,
+):
+    del table_in_ref, rel_in_ref
+    core = lax.axis_index("core")
+    me = own_shard()
+    spread(other_ref, part_ref)
+    part = pltpu.make_async_copy(part_ref, half_columns(rel_ref, part_ref, 1 - core), sems.at[2])
+    part.start()
+    groups = rows_ref.shape[2] // LANES
+    for g in range(2):
+        b = 2 * g + 1 - core
+
+        @pl.when(owner_ref[b] == me)
+        def _():
             for k in range(groups):
-                at = k * 2 * per + g * per
-                block = src_ref[:, at : at + per, :].astype(F32).reshape(BLK, LANES)
                 cols = slice(k * LANES, (k + 1) * LANES)
-                old = table_ref[pl.ds(start, BLK), cols].astype(F32)
-                table_ref[pl.ds(start, BLK), cols] = (old + block).astype(BF)
-
-        mine = owner_ref[b] == me
-        pl.when(mine & (core == h))(lambda add=add: add(own_ref))
-        pl.when(mine & (core != h))(lambda add=add: add(other_ref))
-
-    base = groups * 2 * per
-    size = piece_rows - base
-    row_groups = pieces * LANES * 2 // rel_width
-    for h in range(2):
-
-        def spread(src_ref, h=h):
-            for j in range(pieces):
-                at = (j % row_groups) * size
-                rows = min(size, rels - at)
-                col = h * (rel_width // 2) + (j // row_groups) * LANES
-                rel_ref[at : at + rows, col : col + LANES] = src_ref[
-                    j, base : base + rows, :
-                ].astype(F32)
-
-        pl.when(core == h)(lambda spread=spread: spread(own_ref))
-        pl.when(core != h)(lambda spread=spread: spread(other_ref))
+                sum_ref[:, cols] = block_of(other_ref, g, k)
+            twins = ((own_ref, core, 0), (own_ref, 2 + core, 1), (other_ref, 2 * (1 - g) + 1 - core, 1 - g))
+            for src_ref, c, h in twins:
+
+                @pl.when((owner_ref[c] == me) & (local_ref[c] == local_ref[b]))
+                def _():
+                    for k in range(groups):
+                        cols = slice(k * LANES, (k + 1) * LANES)
+                        sum_ref[:, cols] = sum_ref[:, cols] + block_of(src_ref, h, k)
+
+            rows_ref[g] = sum_ref[...].astype(BF)
+            at = pl.ds(pl.multiple_of(local_ref[b] * BLK, BLK), BLK)
+            copy = pltpu.make_async_copy(rows_ref.at[g], table_ref.at[at], sems.at[g])
+            copy.start()
+            copy.wait()
+
+    part.wait()
 
 
 def exchange(x, axes):
@@ -214,15 +268,16 @@
     return jnp.broadcast_to(x[None], (n, *x.shape))
 
 
-def call(kernel, ins, specs, outs, grant, flops, nbytes, scratch=()):
+def call(kernel, ins, specs, outs, grant, flops, nbytes, scratch=(), out=VMEM, aliases=None):
     shapes = tuple(jax.ShapeDtypeStruct(s, d) for s, d in outs)
     single = len(shapes) == 1
     return pl.pallas_call(
         kernel,
         out_shape=shapes[0] if single else shapes,
         in_specs=specs,
-        out_specs=VMEM if single else (VMEM,) * len(shapes),
+        out_specs=out if single else (out,) * len(shapes),
         scratch_shapes=list(scratch),
+        input_output_aliases=aliases or {},
         compiler_params=pltpu.CompilerParams(vmem_limit_bytes=grant),
         cost_estimate=pl.CostEstimate(flops=flops, bytes_accessed=nbytes, transcendentals=0),
     )(*ins)
@@ -242,34 +297,37 @@
 
     kept, passed = call(
         fetch_kernel, (block_owner, block_local, entity_table), [SMEM, SMEM, HBM],
-        [((BLK, width), BF)] * 2, 2 * MIB, 100_000, 500_000, [pltpu.SemaphoreType.DMA],
+        [((BLK, width), BF)] * 2, FETCH, 100_000, 500_000, [pltpu.SemaphoreType.DMA],
     )
     passed = lax.ppermute(passed, "core", SWAP)
     ids_other = lax.ppermute(rel_ids, "core", SWAP)
     block = (kept + passed).reshape(plane, rows, width)
     block = exchange(block, PLANE)
     piece = jnp.sum(block.astype(F32), axis=0).astype(BF)
-    pieces = exchange(copies(piece, line), LINE).reshape(line // 2, 2, rows, width)
-    piece = jnp.sum(pieces.astype(F32), axis=0).astype(BF).reshape(2 * rows, width)
+    pieces = exchange(copies(piece, line), LINE).reshape(2, line // 2, rows, width)
+    piece = jnp.sum(pieces.astype(F32), axis=1).astype(BF).reshape(2 * rows, width)
     own = exchange(copies(piece, plane), PLANE).reshape(n, width)
     other = lax.ppermute(own, "core", SWAP)
 
     heads = jnp.take(entity_table, head_ids, axis=0, mode="clip")
-    angles = jnp.take(rel_phases, rel_ids, axis=0, mode="clip")
-    query, cosine, sine, spot, pick = call(
-        prep_kernel,
-        (heads, angles, *(v.reshape(1, queries) for v in (target_pos, rel_ids, ids_other))),
-        [VMEM] * 5,
-        [((queries, width), BF), ((queries, half), F32), ((queries, half), F32),
-         ((queries, LANES), jnp.int32), ((rel_rows, 2 * queries), BF)],
-        12 * MIB, 100_000_000, 4_000_000,
+    cosine, sine = call(
+        turn_kernel, (rel_ids, rel_phases), [SMEM, VMEM], [((queries, half), F32)] * 2,
+        8 * MIB, 10_000_000, 2_000_000,
+    )
+    query, spot, pick, scores = call(
+        early_kernel,
+        (heads, cosine, sine, *(v.reshape(1, queries) for v in (target_pos, rel_ids, ids_other)), own),
+        [VMEM] * 7,
+        [((queries, width), BF), ((queries, LANES), jnp.int32), ((rel_rows, 2 * queries), BF),
+         ((queries, n), F32)],
+        12 * MIB, 4 * queries * n * width, 4_000_000,
     )
 
     loss, head_grad, keep, send, ang_keep, ang_send = call(
-        main_kernel, (heads, query, own, other, spot, cosine, sine), [VMEM] * 7,
+        main_kernel, (heads, query, scores, own, other, spot, cosine, sine), [VMEM] * 8,
         [((1, queries), F32), ((queries, width), BF), ((n, width), F32), ((n, width), BF),
          ((queries, half // 2), F32), ((queries, half // 2), F32)],
-        24 * MIB, 12 * queries * n * width, 6_000_000,
+        24 * MIB, 10 * queries * n * width, 6_000_000,
     )
 
     got = lax.ppermute(send, "core", SWAP)
@@ -282,9 +340,19 @@
     part = jnp.sum(exchange(copies(part, line), LINE).astype(F32), axis=0).astype(BF)
     own_sum = exchange(copies(part, plane), PLANE)
     other_sum = lax.ppermute(own_sum, "core", SWAP)
+    shapes = [(entity_table.shape, BF), ((rels, half), F32)]
+    part = pltpu.VMEM((rels, half // 2), F32)
+    partial = call(
+        place_own_kernel, (block_owner, block_local, own_sum), [SMEM, SMEM, VMEM], shapes,
+        8 * MIB, 1_000_000, 2_000_000,
+        [pltpu.VMEM(entity_table.shape, BF), part, pltpu.SemaphoreType.DMA((2,))], HBM,
+    )
     table_grad, rel_grad = call(
-        place_kernel, (block_owner, block_local, own_sum, other_sum), [SMEM, SMEM, VMEM, VMEM],
-        [(entity_table.shape, BF), ((rels, half), F32)], 12 * MIB, 1_000_000, 5_000_000,
+        place_other_kernel, (block_owner, block_local, own_sum, other_sum, *partial),
+        [SMEM, SMEM, VMEM, VMEM, HBM, HBM], shapes, 8 * MIB, 1_000_000, 2_000_000,
+        [pltpu.VMEM((2, BLK, width), BF), pltpu.VMEM((BLK, width), F32), part,
+         pltpu.SemaphoreType.DMA((3,))],
+        HBM, {4: 0, 5: 1},
     )
     return loss.reshape(queries), head_grad, table_grad, rel_grad
 

time: 123 us -> 125 us (1.016)
  the two profiles are of different devices: /device:TPU:33 before, /device:TPU:1 now
where the time goes in v3:
time: 125 us
  blocking collectives  91.6 us (73%)
  starting transfers between devices  12.4 us (10%)
  Pallas kernels  11.8 us (9%)
  local copies, waits for them, and re-layouts  4.63 us (4%)
  waiting for transfers between devices  3.32 us (3%)
    all_to_all x6, blocking collectives, exchange(): return lax.all_to_all(x, axes, split_axis=0, concat_axis=0, tiled=True)  91.6 us
    pallas_call x7, Pallas kernels, call(): pl.pallas_call(kernel, out_shape=shapes[0] if single else shapes, in_spec...  11.8 us
    ppermute x1, starting transfers between devices, body(): other = lax.ppermute(own, 'core', SWAP)  4.37 us
    ppermute x1, starting transfers between devices, body(): other_sum = lax.ppermute(own_sum, 'core', SWAP)  4.18 us
    ppermute x1, starting transfers between devices, body(): passed = lax.ppermute(passed, 'core', SWAP)  3.29 us
    gather x1, local copies, waits for them, and re-layouts, body(): heads = jnp.take(entity_table, head_ids, axis=0, mode='clip')  3.04 us
  transfers between devices with their start and end apart: 6, of which 3 were waited for; matrix products, arithmetic and copies ran while one was open for 2% of the time, Pallas kernels for 5%

profile of v3, /device:TPU:1, one launch (start us, length us, event | category | flops | bytes accessed | tf_op | source)
XLA Modules:
  0.0 124.9 jit_solution(6966044702872986927)
XLA Ops:
  0.6 0.0 copy-start.1
  0.6 0.6 copy-done.1
  1.3 0.7 copy-done.3
  1.9 0.6 shard_map.103
  2.6 3.3 %collective-permute-start.1 = (bf16[128,1024]{1,0:T(8,128)(2,1)S(1)}, bf16[128,1024]{1,0:T(8,128)(2,1)S(1)}, u32[]{:S(2)}, u32[]{:S(2)}) collective-permute-start(bf16[128,1024]{1,0:T(8,128)(2,1)S(1)} %get-tuple-element.25), channel_id=1, source_target_pairs={{0,2},{2,0},{1,3},{3,1},{4,6},{6,4},{5,7},{7,5},{8,10},{10,8},{9,1... | collective-permute-start | bytes 786440 | tf_op jit(solution)/shard_map/ppermute | solution.py:302
  5.9 1.2 collective-permute-done.1
  7.1 12.4 %all_to_all.30 = bf16[16,8,1024]{2,1,0:T(8,128)(2,1)S(1)} all-to-all(bf16[16,8,1024]{2,1,0:T(8,128)(2,1)S(1)} %add_bitcast_fusion), channel_id=1, replica_groups=mesh['x'=4,'y'=4,'zl'=4,'core'=2,'grp'=2] {'x','y'}, dimensions={0} | all-to-all | bytes 524288 | tf_op jit(solution)/shard_map/all_to_all | solution.py:264
  19.6 16.0 %all_to_all.31 = bf16[8,8,1024]{2,1,0:T(8,128)(2,1)S(1)} all-to-all(bf16[8,8,1024]{2,1,0:T(8,128)(2,1)S(1)} %broadcast_in_dim.15), channel_id=1, replica_groups=mesh['x'=4,'y'=4,'zl'=4,'core'=2,'grp'=2] {'grp','zl'}, dimensions={0} | all-to-all | bytes 262144 | tf_op jit(solution)/shard_map/all_to_all | solution.py:264
  35.6 0.1 broadcast_in_dim.32
  35.7 12.4 %all_to_all.32 = bf16[16,16,1024]{2,1,0:T(8,128)(2,1)S(1)} all-to-all(bf16[16,16,1024]{2,1,0:T(8,128)(2,1)S(1)} %broadcast_in_dim.32), channel_id=1, replica_groups=mesh['x'=4,'y'=4,'zl'=4,'core'=2,'grp'=2] {'x','y'}, dimensions={0} | all-to-all | bytes 1048576 | tf_op jit(solution)/shard_map/all_to_all | solution.py:264
  48.0 4.4 %collective-permute-start.2 = (bf16[256,1024]{1,0:T(8,128)(2,1)S(1)}, bf16[256,1024]{1,0:T(8,128)(2,1)S(1)}, u32[]{:S(2)}, u32[]{:S(2)}) collective-permute-start(bf16[256,1024]{1,0:T(8,128)(2,1)S(1)} %bitcast.10), channel_id=1, source_target_pairs={{0,2},{2,0},{1,3},{3,1},{4,6},{6,4},{5,7},{7,5},{8,10},{10,8},{9,1... | collective-permute-start | bytes 1572872 | tf_op jit(solution)/shard_map/ppermute | solution.py:310
  52.4 0.0 copy-start
  52.5 3.0 %gather_fusion = bf16[256,1024]{1,0:T(8,128)(2,1)S(1)} fusion(bf16[512,1024]{1,0:T(8,128)(2,1)} %table_ref.1, s32[1024]{0:T(1024)S(1)} %pad_clamp_fusion), kind=kCustom, calls=%fused_computation | custom fusion | bytes 1049600 | tf_op jit(solution)/shard_map/jit(_take)/gather | solution.py:312
  55.5 0.0 copy-start.6
  55.5 3.4 %shard_map.102 = (f32[256,512]{1,0:T(8,128)S(1)}, f32[256,512]{1,0:T(8,128)S(1)}) custom-call(s32[256]{0:T(256)S(1)} %copy-done.5, f32[822,512]{1,0:T(8,128)S(1)} %copy-done), custom_call_target="tpu_custom_call" | custom-call | flops 10000000 | bytes 2000000 | tf_op jit(solution)/shard_map/pallas_call | solution.py:274
  58.9 1.0 shard_map.104
  59.9 2.7 %shard_map.105 = (f32[1,256]{1,0:T(1,128)}, bf16[256,1024]{1,0:T(8,128)(2,1)}, f32[256,1024]{1,0:T(8,128)S(1)}, bf16[256,1024]{1,0:T(8,128)(2,1)S(1)}, f32[256,256]{1,0:T(8,128)S(1)}, /*index=5*/f32[256,256]{1,0:T(8,128)S(1)}) custom-call(bf16[256,1024]{1,0:T(8,128)(2,1)S(1)} %gather_fusion, bf16[256,1024]{1,0:T(8,128)(2,1)S(1)} %get-tuple-element.26.query_ref, ...), custom_call_target="tpu_custom_call" | custom-call | flops 671088640 | bytes 6000000 | tf_op jit(solution)/shard_map/pallas_call | solution.py:274
  62.7 0.5 collective-permute-start.3
  63.2 0.0 collective-permute-start.4
  63.2 1.9 %collective-permute-done.4.ang_got_ref = f32[256,256]{1,0:T(8,128)S(1)} collective-permute-done((f32[256,256]{1,0:T(8,128)S(1)}, f32[256,256]{1,0:T(8,128)S(1)}, u32[]{:S(2)}, u32[]{:S(2)}) %collective-permute-start.4) | collective-permute-done | bytes 262176 | tf_op jit(solution)/shard_map/ppermute | solution.py:334
  65.1 0.7 shard_map.106
  65.8 17.3 %all_to_all.33 = bf16[16,232,128]{2,1,0:T(8,128)(2,1)S(1)} all-to-all(bf16[16,232,128]{2,1,0:T(8,128)(2,1)S(1)} %shard_map.106), channel_id=1, replica_groups=mesh['x'=4,'y'=4,'zl'=4,'core'=2,'grp'=2] {'x','y'}, dimensions={0} | all-to-all | bytes 1900544 | tf_op jit(solution)/shard_map/all_to_all | solution.py:264
  83.1 0.1 reduce_sum.50
  83.3 0.1 broadcast_in_dim.33
  83.3 15.7 %all_to_all.34 = bf16[8,232,128]{2,1,0:T(8,128)(2,1)S(1)} all-to-all(bf16[8,232,128]{2,1,0:T(8,128)(2,1)S(1)} %broadcast_in_dim.33), channel_id=1, replica_groups=mesh['x'=4,'y'=4,'zl'=4,'core'=2,'grp'=2] {'grp','zl'}, dimensions={0} | all-to-all | bytes 950272 | tf_op jit(solution)/shard_map/all_to_all | solution.py:264
  99.0 0.1 reduce_sum.51
  99.1 0.1 broadcast_in_dim.34
  99.2 17.8 %all_to_all.35.own_ref = bf16[16,232,128]{2,1,0:T(8,128)(2,1)S(1)} all-to-all(bf16[16,232,128]{2,1,0:T(8,128)(2,1)S(1)} %broadcast_in_dim.34), channel_id=1, replica_groups=mesh['x'=4,'y'=4,'zl'=4,'core'=2,'grp'=2] {'x','y'}, dimensions={0} | all-to-all | bytes 1900544 | tf_op jit(solution)/shard_map/all_to_all | solution.py:264
  117.1 4.2 %collective-permute-start.5 = (bf16[16,232,128]{2,1,0:T(8,128)(2,1)S(1)}, bf16[16,232,128]{2,1,0:T(8,128)(2,1)S(1)}, u32[]{:S(2)}, u32[]{:S(2)}) collective-permute-start(bf16[16,232,128]{2,1,0:T(8,128)(2,1)S(1)} %all_to_all.35.own_ref), channel_id=1, source_target_pairs={{0,2},{2,0},{1,3},{3,1},{4,6},{6,4},{5,7},{7,5},{8,10},{10,8},{9,1... | collective-permute-start | bytes 2850824 | tf_op jit(solution)/shard_map/ppermute | solution.py:342
  121.2 1.9 %shard_map.107 = (bf16[512,1024]{1,0:T(8,128)(2,1)}, f32[822,512]{1,0:T(8,128)}) custom-call(s32[4]{0:T(128)S(1)} %copy-done.2, s32[4]{0:T(128)S(1)} %copy-done.4, bf16[16,232,128]{2,1,0:T(8,128)(2,1)S(1)} %all_to_all.35.own_ref), custom_call_target="tpu_custom_call" | custom-call | flops 1000000 | bytes 2000000 | tf_op jit(solution)/shard_map/pallas_call | solution.py:274
  123.1 0.3 collective-permute-done.5.other_ref
  123.4 1.5 %shard_map.108 = (bf16[512,1024]{1,0:T(8,128)(2,1)}, f32[822,512]{1,0:T(8,128)}) custom-call(s32[4]{0:T(128)S(1)} %copy-done.2, s32[4]{0:T(128)S(1)} %copy-done.4, bf16[16,232,128]{2,1,0:T(8,128)(2,1)S(1)} %all_to_all.35.own_ref, bf16[16,232,128]{2,1,0:T(8,128)(2,1)S(1)} %collective-permute-done.5.other_ref, ...), custom_call_target="tpu_custom_call", output_to_operand_aliasing={{0}: (4, {}), {1}: (5, {})} | custom-call | flops 1000000 | bytes 2000000 | tf_op jit(solution)/shard_map/pallas_call | solution.py:274
  (20 shorter events, 0.2 us)
Async XLA Ops:
  0.6 0.7 copy-start.1
  1.3 0.7 copy-start.3
  2.6 4.5 %collective-permute-start.1 = (bf16[128,1024]{1,0:T(8,128)(2,1)S(1)}, bf16[128,1024]{1,0:T(8,128)(2,1)S(1)}, u32[]{:S(2)}, u32[]{:S(2)}) collective-permute-start(bf16[128,1024]{1,0:T(8,128)(2,1)S(1)} %get-tuple-element.25), channel_id=1, source_target_pairs={{0,2},{2,0},{1,3},{3,1},{4,6},{6,4},{5,7},{7,5},{8,10},{10,8},{9,1... | collective-permute-start | bytes 786440 | tf_op jit(solution)/shard_map/ppermute | solution.py:302
  7.1 45.3 %copy-start.5 = (s32[256]{0:T(256)S(1)}, s32[256]{0:T(256)}, u32[]{:S(2)}) copy-start(s32[256]{0:T(256)} %ids_ref.1) | copy-start | bytes 3076
  7.1 45.3 %copy-start.7 = (s32[256]{0:T(256)S(1)}, s32[256]{0:T(256)}, u32[]{:S(2)}) copy-start(s32[256]{0:T(256)} %param.9) | copy-start | bytes 3076
  48.0 11.9 %collective-permute-start.2 = (bf16[256,1024]{1,0:T(8,128)(2,1)S(1)}, bf16[256,1024]{1,0:T(8,128)(2,1)S(1)}, u32[]{:S(2)}, u32[]{:S(2)}) collective-permute-start(bf16[256,1024]{1,0:T(8,128)(2,1)S(1)} %bitcast.10), channel_id=1, source_target_pairs={{0,2},{2,0},{1,3},{3,1},{4,6},{6,4},{5,7},{7,5},{8,10},{10,8},{9,1... | collective-permute-start | bytes 1572872 | tf_op jit(solution)/shard_map/ppermute | solution.py:310
  52.4 6.5 %collective-permute-start = (s32[256]{0:T(256)S(1)}, s32[256]{0:T(256)S(1)}, u32[]{:S(2)}, u32[]{:S(2)}) collective-permute-start(s32[256]{0:T(256)S(1)} %copy-done.5), channel_id=1, source_target_pairs={{0,2},{2,0},{1,3},{3,1},{4,6},{6,4},{5,7},{7,5},{8,10},{10,8},{9,1... | collective-permute-start | bytes 3080 | tf_op jit(solution)/shard_map/ppermute | solution.py:303
  52.4 3.1 %copy-start = (f32[822,512]{1,0:T(8,128)S(1)}, f32[822,512]{1,0:T(8,128)}, u32[]{:S(2)}) copy-start(f32[822,512]{1,0:T(8,128)} %phases_ref.1) | copy-start | bytes 5050372
  55.5 3.4 %copy-start.6 = (s32[256]{0:T(256)S(1)}, s32[256]{0:T(256)}, u32[]{:S(2)}) copy-start(s32[256]{0:T(256)} %param.11) | copy-start | bytes 3076
  62.7 2.4 %collective-permute-start.3 = (bf16[256,1024]{1,0:T(8,128)(2,1)S(1)}, bf16[256,1024]{1,0:T(8,128)(2,1)S(1)}, u32[]{:S(2)}, u32[]{:S(2)}) collective-permute-start(bf16[256,1024]{1,0:T(8,128)(2,1)S(1)} %get-tuple-element.33), channel_id=1, source_target_pairs={{0,2},{2,0},{1,3},{3,1},{4,6},{6,4},{5,7},{7,5},{8,10},{10,8},{9,1... | collective-permute-start | bytes 1572872 | tf_op jit(solution)/shard_map/ppermute | solution.py:333
  63.2 1.9 %collective-permute-start.4 = (f32[256,256]{1,0:T(8,128)S(1)}, f32[256,256]{1,0:T(8,128)S(1)}, u32[]{:S(2)}, u32[]{:S(2)}) collective-permute-start(f32[256,256]{1,0:T(8,128)S(1)} %get-tuple-element.35), channel_id=1, source_target_pairs={{0,2},{2,0},{1,3},{3,1},{4,6},{6,4},{5,7},{7,5},{8,10},{10,8},{9,1... | collective-permute-start | bytes 786440 | tf_op jit(solution)/shard_map/ppermute | solution.py:334
  99.0 22.2 %copy-start.2 = (s32[4]{0:T(128)S(1)}, s32[4]{0:T(128)}, u32[]{:S(2)}) copy-start(s32[4]{0:T(128)} %owner_ref.5) | copy-start | bytes 52
  99.0 22.2 %copy-start.4 = (s32[4]{0:T(128)S(1)}, s32[4]{0:T(128)}, u32[]{:S(2)}) copy-start(s32[4]{0:T(128)} %local_ref.5) | copy-start | bytes 52
  117.1 6.3 %collective-permute-start.5 = (bf16[16,232,128]{2,1,0:T(8,128)(2,1)S(1)}, bf16[16,232,128]{2,1,0:T(8,128)(2,1)S(1)}, u32[]{:S(2)}, u32[]{:S(2)}) collective-permute-start(bf16[16,232,128]{2,1,0:T(8,128)(2,1)S(1)} %all_to_all.35.own_ref), channel_id=1, source_target_pairs={{0,2},{2,0},{1,3},{3,1},{4,6},{6,4},{5,7},{7,5},{8,10},{10,8},{9,1... | collective-permute-start | bytes 2850824 | tf_op jit(solution)/shard_map/ppermute | solution.py:342

commit v4 on v3

--- a/solution.py
+++ b/solution.py
@@ -41,22 +41,39 @@
     return place
 
 
-def fetch_kernel(owner_ref, local_ref, table_ref, keep_ref, pass_ref, sem):
+def fetch_kernel(number_ref, table_ref, keep_ref, pass_ref, sem):
     core = lax.axis_index("core")
     grp = lax.axis_index("grp")
     me = own_shard()
+    per = table_ref.shape[0] // BLK
     for b, out_ref in ((2 * grp + core, keep_ref), (2 * grp + 1 - core, pass_ref)):
 
-        @pl.when(owner_ref[b] == me)
+        @pl.when(number_ref[b] // per == me)
         def _():
-            start = pl.multiple_of(local_ref[b] * BLK, BLK)
+            start = pl.multiple_of(number_ref[b] % per * BLK, BLK)
             copy = pltpu.make_async_copy(table_ref.at[pl.ds(start, BLK)], out_ref, sem)
             copy.start()
             copy.wait()
 
-        @pl.when(owner_ref[b] != me)
+        @pl.when(number_ref[b] // per != me)
         def _():
             out_ref[...] = jnp.zeros_like(out_ref)
+
+
+def cos_sin(x):
+    turns = jnp.floor(x * 0.6366197723675814 + 0.5)
+    rest = ((x - turns * 1.5703125) - turns * 4.837512969970703125e-4) - turns * 7.54978995489188e-8
+    z = rest * rest
+    s = ((-1.9515295891e-4 * z + 8.3321608736e-3) * z - 1.6666654611e-1) * z * rest + rest
+    c = ((2.443315711809948e-5 * z - 1.388731625493765e-3) * z + 4.166664568298827e-2) * z * z
+    c = c - 0.5 * z + 1.0
+    quarter = turns.astype(jnp.int32)
+    odd = (quarter & 1) != 0
+    cosine = jnp.where(odd, s, c)
+    sine = jnp.where(odd, c, s)
+    cosine = jnp.where(((quarter + 1) & 2) != 0, -cosine, cosine)
+    sine = jnp.where((quarter & 2) != 0, -sine, sine)
+    return cosine, sine
 
 
 def turn_kernel(ids_ref, phases_ref, cos_ref, sin_ref):
@@ -64,10 +81,10 @@
         cos_ref[pl.ds(i, 1), :] = phases_ref[pl.ds(ids_ref[i], 1), :]
         return carry
 
-    lax.fori_loop(0, cos_ref.shape[0], take, 0, unroll=8)
-    angles = cos_ref[...]
-    cos_ref[...] = jnp.cos(angles)
-    sin_ref[...] = jnp.sin(angles)
+    lax.fori_loop(0, cos_ref.shape[0], take, 0, unroll=16)
+    cosine, sine = cos_sin(cos_ref[...])
+    cos_ref[...] = cosine
+    sin_ref[...] = sine
 
 
 def rotated(heads_ref, cosine, sine):
@@ -199,16 +216,17 @@
     return rel_ref.at[:, pl.ds(pl.multiple_of(half * w, w), w)]
 
 
-def place_own_kernel(owner_ref, local_ref, own_ref, table_ref, rel_ref, rows_ref, part_ref, sems):
+def place_own_kernel(number_ref, own_ref, table_ref, rel_ref, rows_ref, part_ref, sems):
     core = lax.axis_index("core")
     me = own_shard()
+    per = table_ref.shape[0] // BLK
     rows_ref[...] = jnp.zeros_like(rows_ref)
     for g in range(2):
         b = 2 * g + core
 
-        @pl.when(owner_ref[b] == me)
+        @pl.when(number_ref[b] // per == me)
         def _():
-            at = pl.ds(pl.multiple_of(local_ref[b] * BLK, BLK), BLK)
+            at = pl.ds(pl.multiple_of(number_ref[b] % per * BLK, BLK), BLK)
             for k in range(rows_ref.shape[1] // LANES):
                 cols = slice(k * LANES, (k + 1) * LANES)
                 old = rows_ref[at, cols].astype(F32)
@@ -224,7 +242,7 @@
 
 
 def place_other_kernel(
-    owner_ref, local_ref, own_ref, other_ref, table_in_ref, rel_in_ref,
+    number_ref, own_ref, other_ref, table_in_ref, rel_in_ref,
     table_ref, rel_ref, rows_ref, sum_ref, part_ref, sems,
 ):
     del table_in_ref, rel_in_ref
@@ -233,11 +251,12 @@
     spread(other_ref, part_ref)
     part = pltpu.make_async_copy(part_ref, half_columns(rel_ref, part_ref, 1 - core), sems.at[2])
     part.start()
+    per = table_ref.shape[0] // BLK
     groups = rows_ref.shape[2] // LANES
     for g in range(2):
         b = 2 * g + 1 - core
 
-        @pl.when(owner_ref[b] == me)
+        @pl.when(number_ref[b] // per == me)
         def _():
             for k in range(groups):
                 cols = slice(k * LANES, (k + 1) * LANES)
@@ -245,14 +264,14 @@
             twins = ((own_ref, core, 0), (own_ref, 2 + core, 1), (other_ref, 2 * (1 - g) + 1 - core, 1 - g))
             for src_ref, c, h in twins:
 
-                @pl.when((owner_ref[c] == me) & (local_ref[c] == local_ref[b]))
+                @pl.when(number_ref[c] == number_ref[b])
                 def _():
                     for k in range(groups):
                         cols = slice(k * LANES, (k + 1) * LANES)
                         sum_ref[:, cols] = sum_ref[:, cols] + block_of(src_ref, h, k)
 
             rows_ref[g] = sum_ref[...].astype(BF)
-            at = pl.ds(pl.multiple_of(local_ref[b] * BLK, BLK), BLK)
+            at = pl.ds(pl.multiple_of(number_ref[b] % per * BLK, BLK), BLK)
             copy = pltpu.make_async_copy(rows_ref.at[g], table_ref.at[at], sems.at[g])
             copy.start()
             copy.wait()
@@ -295,8 +314,9 @@
     rel_rows = -(-rels // 64) * 64
     piece_rows = n * width // (plane * LANES) + rel_rows * half // 2 // (plane * LANES)
 
+    numbers = block_owner * (entity_table.shape[0] // BLK) + block_local
     kept, passed = call(
-        fetch_kernel, (block_owner, block_local, entity_table), [SMEM, SMEM, HBM],
+        fetch_kernel, (numbers, entity_table), [SMEM, HBM],
         [((BLK, width), BF)] * 2, FETCH, 100_000, 500_000, [pltpu.SemaphoreType.DMA],
     )
     passed = lax.ppermute(passed, "core", SWAP)
@@ -343,16 +363,16 @@
     shapes = [(entity_table.shape, BF), ((rels, half), F32)]
     part = pltpu.VMEM((rels, half // 2), F32)
     partial = call(
-        place_own_kernel, (block_owner, block_local, own_sum), [SMEM, SMEM, VMEM], shapes,
+        place_own_kernel, (numbers, own_sum), [SMEM, VMEM], shapes,
         8 * MIB, 1_000_000, 2_000_000,
         [pltpu.VMEM(entity_table.shape, BF), part, pltpu.SemaphoreType.DMA((2,))], HBM,
     )
     table_grad, rel_grad = call(
-        place_other_kernel, (block_owner, block_local, own_sum, other_sum, *partial),
-        [SMEM, SMEM, VMEM, VMEM, HBM, HBM], shapes, 8 * MIB, 1_000_000, 2_000_000,
+        place_other_kernel, (numbers, own_sum, other_sum, *partial),
+        [SMEM, VMEM, VMEM, HBM, HBM], shapes, 8 * MIB, 1_000_000, 2_000_000,
         [pltpu.VMEM((2, BLK, width), BF), pltpu.VMEM((BLK, width), F32), part,
          pltpu.SemaphoreType.DMA((3,))],
-        HBM, {4: 0, 5: 1},
+        HBM, {3: 0, 4: 1},
     )
     return loss.reshape(queries), head_grad, table_grad, rel_grad
 

time: 125 us -> 124 us (level)
  local copies, waits for them, and re-layouts: 4.63 us -> 3.32 us
    unnamed x16 -> x8, local copies, waits for them, and re-layouts: 1.34 us -> 0.02 us
  transfers between devices with their start and end apart: 6 -> 6, of which waited for: 3 -> 3; matrix products, arithmetic and copies ran while one was open for 2% -> 2% of each run, Pallas kernels for 5% -> 4%
where the time goes in v4:
time: 124 us; the launch traced here: 123 us
  blocking collectives  91.6 us (74%)
  starting transfers between devices  12.4 us (10%)
  Pallas kernels  10.9 us (9%)
  waiting for transfers between devices  3.33 us (3%)
  local copies, waits for them, and re-layouts  3.32 us (3%)
    all_to_all x6, blocking collectives, exchange(): return lax.all_to_all(x, axes, split_axis=0, concat_axis=0, tiled=True)  91.6 us
    pallas_call x7, Pallas kernels, call(): pl.pallas_call(kernel, out_shape=shapes[0] if single else shapes, in_spec...  10.9 us
    ppermute x1, starting transfers between devices, body(): other = lax.ppermute(own, 'core', SWAP)  4.37 us
    ppermute x1, starting transfers between devices, body(): other_sum = lax.ppermute(own_sum, 'core', SWAP)  4.18 us
    ppermute x1, starting transfers between devices, body(): passed = lax.ppermute(passed, 'core', SWAP)  3.29 us
    gather x1, local copies, waits for them, and re-layouts, body(): heads = jnp.take(entity_table, head_ids, axis=0, mode='clip')  3.04 us
  transfers between devices with their start and end apart: 6, of which 3 were waited for; matrix products, arithmetic and copies ran while one was open for 2% of the time, Pallas kernels for 4%

profile of v4, /device:TPU:1, one launch (start us, length us, event | category | flops | bytes accessed | tf_op | source)
XLA Modules:
  0.0 123.3 jit_solution(2075917507579106903)
XLA Ops:
  0.6 0.7 multiply_add_fusion.number_ref
  1.3 0.7 shard_map.103
  2.0 3.3 %collective-permute-start.1 = (bf16[128,1024]{1,0:T(8,128)(2,1)S(1)}, bf16[128,1024]{1,0:T(8,128)(2,1)S(1)}, u32[]{:S(2)}, u32[]{:S(2)}) collective-permute-start(bf16[128,1024]{1,0:T(8,128)(2,1)S(1)} %get-tuple-element.25), channel_id=1, source_target_pairs={{0,2},{2,0},{1,3},{3,1},{4,6},{6,4},{5,7},{7,5},{8,10},{10,8},{9,1... | collective-permute-start | bytes 786440 | tf_op jit(solution)/shard_map/ppermute | solution.py:322
  5.3 1.2 collective-permute-done.1
  6.5 0.0 copy-start.3
  6.5 12.4 %all_to_all.30 = bf16[16,8,1024]{2,1,0:T(8,128)(2,1)S(1)} all-to-all(bf16[16,8,1024]{2,1,0:T(8,128)(2,1)S(1)} %add_bitcast_fusion), channel_id=1, replica_groups=mesh['x'=4,'y'=4,'zl'=4,'core'=2,'grp'=2] {'x','y'}, dimensions={0} | all-to-all | bytes 524288 | tf_op jit(solution)/shard_map/all_to_all | solution.py:283
  19.0 16.0 %all_to_all.31 = bf16[8,8,1024]{2,1,0:T(8,128)(2,1)S(1)} all-to-all(bf16[8,8,1024]{2,1,0:T(8,128)(2,1)S(1)} %broadcast_in_dim.15), channel_id=1, replica_groups=mesh['x'=4,'y'=4,'zl'=4,'core'=2,'grp'=2] {'grp','zl'}, dimensions={0} | all-to-all | bytes 262144 | tf_op jit(solution)/shard_map/all_to_all | solution.py:283
  35.0 0.1 broadcast_in_dim.32
  35.1 12.4 %all_to_all.32 = bf16[16,16,1024]{2,1,0:T(8,128)(2,1)S(1)} all-to-all(bf16[16,16,1024]{2,1,0:T(8,128)(2,1)S(1)} %broadcast_in_dim.32), channel_id=1, replica_groups=mesh['x'=4,'y'=4,'zl'=4,'core'=2,'grp'=2] {'x','y'}, dimensions={0} | all-to-all | bytes 1048576 | tf_op jit(solution)/shard_map/all_to_all | solution.py:283
  47.4 4.4 %collective-permute-start.2 = (bf16[256,1024]{1,0:T(8,128)(2,1)S(1)}, bf16[256,1024]{1,0:T(8,128)(2,1)S(1)}, u32[]{:S(2)}, u32[]{:S(2)}) collective-permute-start(bf16[256,1024]{1,0:T(8,128)(2,1)S(1)} %bitcast.10), channel_id=1, source_target_pairs={{0,2},{2,0},{1,3},{3,1},{4,6},{6,4},{5,7},{7,5},{8,10},{10,8},{9,1... | collective-permute-start | bytes 1572872 | tf_op jit(solution)/shard_map/ppermute | solution.py:330
  51.8 0.0 collective-permute-start
  51.8 0.0 copy-start
  51.8 3.0 %gather_fusion = bf16[256,1024]{1,0:T(8,128)(2,1)S(1)} fusion(bf16[512,1024]{1,0:T(8,128)(2,1)} %table_ref.1, s32[1024]{0:T(1024)S(1)} %pad_clamp_fusion), kind=kCustom, calls=%fused_computation | custom fusion | bytes 1049600 | tf_op jit(solution)/shard_map/jit(_take)/gather | solution.py:332
  54.9 0.0 copy-start.2
  54.9 2.2 %shard_map.102 = (f32[256,512]{1,0:T(8,128)S(1)}, f32[256,512]{1,0:T(8,128)S(1)}) custom-call(s32[256]{0:T(256)S(1)} %copy-done.1, f32[822,512]{1,0:T(8,128)S(1)} %copy-done), custom_call_target="tpu_custom_call" | custom-call | flops 10000000 | bytes 2000000 | tf_op jit(solution)/shard_map/pallas_call | solution.py:293
  57.1 1.1 shard_map.104
  58.2 2.8 %shard_map.105 = (f32[1,256]{1,0:T(1,128)}, bf16[256,1024]{1,0:T(8,128)(2,1)}, f32[256,1024]{1,0:T(8,128)S(1)}, bf16[256,1024]{1,0:T(8,128)(2,1)S(1)}, f32[256,256]{1,0:T(8,128)S(1)}, /*index=5*/f32[256,256]{1,0:T(8,128)S(1)}) custom-call(bf16[256,1024]{1,0:T(8,128)(2,1)S(1)} %gather_fusion, bf16[256,1024]{1,0:T(8,128)(2,1)S(1)} %get-tuple-element.26.query_ref, ...), custom_call_target="tpu_custom_call" | custom-call | flops 671088640 | bytes 6000000 | tf_op jit(solution)/shard_map/pallas_call | solution.py:293
  61.0 0.5 collective-permute-start.3
  61.5 0.0 collective-permute-start.4
  61.5 1.9 %collective-permute-done.4.ang_got_ref = f32[256,256]{1,0:T(8,128)S(1)} collective-permute-done((f32[256,256]{1,0:T(8,128)S(1)}, f32[256,256]{1,0:T(8,128)S(1)}, u32[]{:S(2)}, u32[]{:S(2)}) %collective-permute-start.4) | collective-permute-done | bytes 262176 | tf_op jit(solution)/shard_map/ppermute | solution.py:354
  63.4 0.8 shard_map.106
  64.2 17.3 %all_to_all.33 = bf16[16,232,128]{2,1,0:T(8,128)(2,1)S(1)} all-to-all(bf16[16,232,128]{2,1,0:T(8,128)(2,1)S(1)} %shard_map.106), channel_id=1, replica_groups=mesh['x'=4,'y'=4,'zl'=4,'core'=2,'grp'=2] {'x','y'}, dimensions={0} | all-to-all | bytes 1900544 | tf_op jit(solution)/shard_map/all_to_all | solution.py:283
  81.5 0.1 reduce_sum.50
  81.6 0.1 broadcast_in_dim.33
  81.7 15.7 %all_to_all.34 = bf16[8,232,128]{2,1,0:T(8,128)(2,1)S(1)} all-to-all(bf16[8,232,128]{2,1,0:T(8,128)(2,1)S(1)} %broadcast_in_dim.33), channel_id=1, replica_groups=mesh['x'=4,'y'=4,'zl'=4,'core'=2,'grp'=2] {'grp','zl'}, dimensions={0} | all-to-all | bytes 950272 | tf_op jit(solution)/shard_map/all_to_all | solution.py:283
  97.4 0.1 reduce_sum.51
  97.5 0.1 broadcast_in_dim.34
  97.6 17.8 %all_to_all.35.own_ref = bf16[16,232,128]{2,1,0:T(8,128)(2,1)S(1)} all-to-all(bf16[16,232,128]{2,1,0:T(8,128)(2,1)S(1)} %broadcast_in_dim.34), channel_id=1, replica_groups=mesh['x'=4,'y'=4,'zl'=4,'core'=2,'grp'=2] {'x','y'}, dimensions={0} | all-to-all | bytes 1900544 | tf_op jit(solution)/shard_map/all_to_all | solution.py:283
  115.4 4.2 %collective-permute-start.5 = (bf16[16,232,128]{2,1,0:T(8,128)(2,1)S(1)}, bf16[16,232,128]{2,1,0:T(8,128)(2,1)S(1)}, u32[]{:S(2)}, u32[]{:S(2)}) collective-permute-start(bf16[16,232,128]{2,1,0:T(8,128)(2,1)S(1)} %all_to_all.35.own_ref), channel_id=1, source_target_pairs={{0,2},{2,0},{1,3},{3,1},{4,6},{6,4},{5,7},{7,5},{8,10},{10,8},{9,1... | collective-permute-start | bytes 2850824 | tf_op jit(solution)/shard_map/ppermute | solution.py:362
  119.6 1.9 %shard_map.107 = (bf16[512,1024]{1,0:T(8,128)(2,1)}, f32[822,512]{1,0:T(8,128)}) custom-call(s32[4]{0:T(128)S(1)} %multiply_add_fusion.number_ref, bf16[16,232,128]{2,1,0:T(8,128)(2,1)S(1)} %all_to_all.35.own_ref), custom_call_target="tpu_custom_call" | custom-call | flops 1000000 | bytes 2000000 | tf_op jit(solution)/shard_map/pallas_call | solution.py:293
  121.5 0.3 collective-permute-done.5.other_ref
  121.8 1.5 %shard_map.108 = (bf16[512,1024]{1,0:T(8,128)(2,1)}, f32[822,512]{1,0:T(8,128)}) custom-call(s32[4]{0:T(128)S(1)} %multiply_add_fusion.number_ref, bf16[16,232,128]{2,1,0:T(8,128)(2,1)S(1)} %all_to_all.35.own_ref, bf16[16,232,128]{2,1,0:T(8,128)(2,1)S(1)} %collective-permute-done.5.other_ref, ...), custom_call_target="tpu_custom_call", output_to_operand_aliasing={{0}: (3, {}), {1}: (4, {})} | custom-call | flops 1000000 | bytes 2000000 | tf_op jit(solution)/shard_map/pallas_call | solution.py:293
  (13 shorter events, 0.1 us)
Async XLA Ops:
  2.0 4.5 %collective-permute-start.1 = (bf16[128,1024]{1,0:T(8,128)(2,1)S(1)}, bf16[128,1024]{1,0:T(8,128)(2,1)S(1)}, u32[]{:S(2)}, u32[]{:S(2)}) collective-permute-start(bf16[128,1024]{1,0:T(8,128)(2,1)S(1)} %get-tuple-element.25), channel_id=1, source_target_pairs={{0,2},{2,0},{1,3},{3,1},{4,6},{6,4},{5,7},{7,5},{8,10},{10,8},{9,1... | collective-permute-start | bytes 786440 | tf_op jit(solution)/shard_map/ppermute | solution.py:322
  6.5 45.3 %copy-start.1 = (s32[256]{0:T(256)S(1)}, s32[256]{0:T(256)}, u32[]{:S(2)}) copy-start(s32[256]{0:T(256)} %ids_ref.1) | copy-start | bytes 3076
  6.5 45.3 %copy-start.3 = (s32[256]{0:T(256)S(1)}, s32[256]{0:T(256)}, u32[]{:S(2)}) copy-start(s32[256]{0:T(256)} %param.9) | copy-start | bytes 3076
  47.4 10.8 %collective-permute-start.2 = (bf16[256,1024]{1,0:T(8,128)(2,1)S(1)}, bf16[256,1024]{1,0:T(8,128)(2,1)S(1)}, u32[]{:S(2)}, u32[]{:S(2)}) collective-permute-start(bf16[256,1024]{1,0:T(8,128)(2,1)S(1)} %bitcast.10), channel_id=1, source_target_pairs={{0,2},{2,0},{1,3},{3,1},{4,6},{6,4},{5,7},{7,5},{8,10},{10,8},{9,1... | collective-permute-start | bytes 1572872 | tf_op jit(solution)/shard_map/ppermute | solution.py:330
  51.8 5.3 %collective-permute-start = (s32[256]{0:T(256)S(1)}, s32[256]{0:T(256)S(1)}, u32[]{:S(2)}, u32[]{:S(2)}) collective-permute-start(s32[256]{0:T(256)S(1)} %copy-done.1), channel_id=1, source_target_pairs={{0,2},{2,0},{1,3},{3,1},{4,6},{6,4},{5,7},{7,5},{8,10},{10,8},{9,1... | collective-permute-start | bytes 3080 | tf_op jit(solution)/shard_map/ppermute | solution.py:323
  51.8 3.1 %copy-start = (f32[822,512]{1,0:T(8,128)S(1)}, f32[822,512]{1,0:T(8,128)}, u32[]{:S(2)}) copy-start(f32[822,512]{1,0:T(8,128)} %phases_ref.1) | copy-start | bytes 5050372
  54.9 2.2 %copy-start.2 = (s32[256]{0:T(256)S(1)}, s32[256]{0:T(256)}, u32[]{:S(2)}) copy-start(s32[256]{0:T(256)} %param.11) | copy-start | bytes 3076
  61.0 2.4 %collective-permute-start.3 = (bf16[256,1024]{1,0:T(8,128)(2,1)S(1)}, bf16[256,1024]{1,0:T(8,128)(2,1)S(1)}, u32[]{:S(2)}, u32[]{:S(2)}) collective-permute-start(bf16[256,1024]{1,0:T(8,128)(2,1)S(1)} %get-tuple-element.33), channel_id=1, source_target_pairs={{0,2},{2,0},{1,3},{3,1},{4,6},{6,4},{5,7},{7,5},{8,10},{10,8},{9,1... | collective-permute-start | bytes 1572872 | tf_op jit(solution)/shard_map/ppermute | solution.py:353
  61.5 1.9 %collective-permute-start.4 = (f32[256,256]{1,0:T(8,128)S(1)}, f32[256,256]{1,0:T(8,128)S(1)}, u32[]{:S(2)}, u32[]{:S(2)}) collective-permute-start(f32[256,256]{1,0:T(8,128)S(1)} %get-tuple-element.35), channel_id=1, source_target_pairs={{0,2},{2,0},{1,3},{3,1},{4,6},{6,4},{5,7},{7,5},{8,10},{10,8},{9,1... | collective-permute-start | bytes 786440 | tf_op jit(solution)/shard_map/ppermute | solution.py:354
  115.4 6.3 %collective-permute-start.5 = (bf16[16,232,128]{2,1,0:T(8,128)(2,1)S(1)}, bf16[16,232,128]{2,1,0:T(8,128)(2,1)S(1)}, u32[]{:S(2)}, u32[]{:S(2)}) collective-permute-start(bf16[16,232,128]{2,1,0:T(8,128)(2,1)S(1)} %all_to_all.35.own_ref), channel_id=1, source_target_pairs={{0,2},{2,0},{1,3},{3,1},{4,6},{6,4},{5,7},{7,5},{8,10},{10,8},{9,1... | collective-permute-start | bytes 2850824 | tf_op jit(solution)/shard_map/ppermute | solution.py:362

commit v5 on v4

--- a/solution.py
+++ b/solution.py
@@ -20,6 +20,7 @@
 TN = (((0,), (0,)), ((), ()))
 VMEM = pl.BlockSpec(memory_space=pltpu.VMEM)
 SMEM = pl.BlockSpec(memory_space=pltpu.SMEM)
+ANY = pl.BlockSpec(memory_space=pl.ANY)
 HBM = pl.BlockSpec(memory_space=pltpu.HBM)
 MIB = 1024 * 1024
 FETCH = 56_000_000
@@ -123,7 +124,7 @@
 
 def main_kernel(
     heads_ref, query_ref, scores_ref, own_ref, other_ref, spot_ref, cos_ref, sin_ref,
-    loss_ref, head_ref, keep_ref, send_ref, ang_keep_ref, ang_send_ref,
+    loss_ref, dquery_ref, send_ref, ang_keep_ref, ang_send_ref, low_ref, rest_ref,
 ):
     rows, half = cos_ref.shape
     n = own_ref.shape[0]
@@ -142,25 +143,22 @@
     loss = top + jnp.log(total) - picked
     loss_ref[...] = jnp.broadcast_to(loss, (rows, LANES)).T[:1]
     scale = 1.0 / total
-    ones_q = jnp.ones((rows, LANES), BF)
     dquery = None
     for k in (1, 0):
         weights = exps[k] * scale - hits[k].astype(F32)
         low, rest = halves(weights)
         part = dot(low, cands[k])
         dquery = part if dquery is None else dquery + part
-        column = (dot(low, ones_q, TN) + dot(rest, ones_q, TN))[:, :1]
-        grad = dot(low, query, TN) - column * cands[k].astype(F32)
         if k == 0:
-            keep_ref[...] = grad
+            low_ref[...] = low
+            rest_ref[...] = rest
         else:
-            send_ref[...] = grad.astype(BF)
+            send_ref[...] = pulled(low, rest, query, cands[k]).astype(BF)
     cosine = cos_ref[...]
     sine = sin_ref[...]
     qr, qi = rotated(heads_ref, cosine, sine)
     dr, di = dquery[:, :half], dquery[:, half:]
-    head_ref[:, :half] = (dr * cosine + di * sine).astype(BF)
-    head_ref[:, half:] = (di * cosine - dr * sine).astype(BF)
+    dquery_ref[...] = dquery
     ang = di * qr - dr * qi
     a, b = ang[:, : half // 2], ang[:, half // 2 :]
     first = lax.axis_index("core") == 0
@@ -168,7 +166,30 @@
     ang_send_ref[...] = jnp.where(first, b, a)
 
 
-def pack_kernel(pick_ref, keep_ref, got_ref, ang_ref, ang_got_ref, out_ref):
+def pulled(low, rest, query, cand):
+    ones = jnp.ones((low.shape[0], LANES), BF)
+    column = (dot(low, ones, TN) + dot(rest, ones, TN))[:, :1]
+    return dot(low, query, TN) - column * cand.astype(F32)
+
+
+def keep_kernel(
+    loss_in_ref, dquery_ref, cos_ref, sin_ref, low_ref, rest_ref, query_ref, own_ref, pick_ref, ang_ref,
+    loss_ref, head_ref, keep_ref, rel_ref,
+):
+    half = cos_ref.shape[1]
+    loss_ref[...] = loss_in_ref[...]
+    cosine = cos_ref[...]
+    sine = sin_ref[...]
+    dr, di = dquery_ref[:, :half], dquery_ref[:, half:]
+    head_ref[:, :half] = (dr * cosine + di * sine).astype(BF)
+    head_ref[:, half:] = (di * cosine - dr * sine).astype(BF)
+    keep_ref[...] = pulled(low_ref[...], rest_ref[...], query_ref[...], own_ref[...])
+    hi, lo = halves(ang_ref[...])
+    sel = pick_ref[:, : ang_ref.shape[0]]
+    rel_ref[...] = dot(sel, hi) + dot(sel, lo)
+
+
+def pack_kernel(pick_ref, keep_ref, got_ref, rel_ref, ang_got_ref, out_ref):
     pieces = out_ref.shape[0]
     per = keep_ref.shape[0] // pieces
     groups = keep_ref.shape[1] // LANES
@@ -176,14 +197,9 @@
         cols = slice(k * LANES, (k + 1) * LANES)
         grad = keep_ref[:, cols] + got_ref[:, cols].astype(F32)
         out_ref[:, k * per : (k + 1) * per, :] = grad.astype(BF).reshape(pieces, per, LANES)
-    q = ang_ref.shape[0]
-    total = None
-    for k, ref in enumerate((ang_ref, ang_got_ref)):
-        sel = pick_ref[:, k * q : (k + 1) * q]
-        hi, lo = halves(ref[...])
-        part = dot(sel, hi) + dot(sel, lo)
-        total = part if total is None else total + part
-    total = total.astype(BF)
+    hi, lo = halves(ang_got_ref[...])
+    sel = pick_ref[:, ang_got_ref.shape[0] :]
+    total = (rel_ref[...] + (dot(sel, hi) + dot(sel, lo))).astype(BF)
     base = groups * per
     size = out_ref.shape[1] - base
     row_groups = total.shape[0] // size
@@ -216,11 +232,19 @@
     return rel_ref.at[:, pl.ds(pl.multiple_of(half * w, w), w)]
 
 
-def place_own_kernel(number_ref, own_ref, table_ref, rel_ref, rows_ref, part_ref, sems):
+def place_own_kernel(
+    numbers_ref, own_ref, table_ref, rel_ref, rows_ref, part_ref, number_ref, sems
+):
     core = lax.axis_index("core")
     me = own_shard()
     per = table_ref.shape[0] // BLK
+    load = pltpu.make_async_copy(numbers_ref, number_ref, sems.at[2])
+    load.start()
+    spread(own_ref, part_ref)
+    part = pltpu.make_async_copy(part_ref, half_columns(rel_ref, part_ref, core), sems.at[1])
+    part.start()
     rows_ref[...] = jnp.zeros_like(rows_ref)
+    load.wait()
     for g in range(2):
         b = 2 * g + core
 
@@ -234,29 +258,36 @@
 
     table = pltpu.make_async_copy(rows_ref, table_ref, sems.at[0])
     table.start()
-    spread(own_ref, part_ref)
-    part = pltpu.make_async_copy(part_ref, half_columns(rel_ref, part_ref, core), sems.at[1])
-    part.start()
     table.wait()
     part.wait()
 
 
 def place_other_kernel(
-    number_ref, own_ref, other_ref, table_in_ref, rel_in_ref,
-    table_ref, rel_ref, rows_ref, sum_ref, part_ref, sems,
+    numbers_ref, own_ref, other_ref, table_in_ref, rel_in_ref,
+    table_ref, rel_ref, rows_ref, sum_ref, part_ref, number_ref, sems,
 ):
     del table_in_ref, rel_in_ref
     core = lax.axis_index("core")
     me = own_shard()
+    per = table_ref.shape[0] // BLK
+    groups = rows_ref.shape[2] // LANES
+    load = pltpu.make_async_copy(numbers_ref, number_ref, sems.at[3])
+    load.start()
     spread(other_ref, part_ref)
     part = pltpu.make_async_copy(part_ref, half_columns(rel_ref, part_ref, 1 - core), sems.at[2])
     part.start()
-    per = table_ref.shape[0] // BLK
-    groups = rows_ref.shape[2] // LANES
+    load.wait()
+    blocks = []
     for g in range(2):
         b = 2 * g + 1 - core
-
-        @pl.when(number_ref[b] // per == me)
+        at = pl.ds(pl.multiple_of(number_ref[b] % per * BLK, BLK), BLK)
+        copy = pltpu.make_async_copy(rows_ref.at[g], table_ref.at[at], sems.at[g])
+        mine = number_ref[b] // per == me
+        if g == 1:
+            mine = mine & (number_ref[b] != number_ref[1 - core])
+        blocks.append((mine, copy))
+
+        @pl.when(mine)
         def _():
             for k in range(groups):
                 cols = slice(k * LANES, (k + 1) * LANES)
@@ -271,11 +302,10 @@
                         sum_ref[:, cols] = sum_ref[:, cols] + block_of(src_ref, h, k)
 
             rows_ref[g] = sum_ref[...].astype(BF)
-            at = pl.ds(pl.multiple_of(number_ref[b] % per * BLK, BLK), BLK)
-            copy = pltpu.make_async_copy(rows_ref.at[g], table_ref.at[at], sems.at[g])
             copy.start()
-            copy.wait()
-
+
+    for mine, copy in blocks:
+        pl.when(mine)(copy.wait)
     part.wait()
 
 
@@ -343,18 +373,24 @@
         12 * MIB, 4 * queries * n * width, 4_000_000,
     )
 
-    loss, head_grad, keep, send, ang_keep, ang_send = call(
+    loss, dquery, send, ang_keep, ang_send, low, rest = call(
         main_kernel, (heads, query, scores, own, other, spot, cosine, sine), [VMEM] * 8,
-        [((1, queries), F32), ((queries, width), BF), ((n, width), F32), ((n, width), BF),
-         ((queries, half // 2), F32), ((queries, half // 2), F32)],
-        24 * MIB, 10 * queries * n * width, 6_000_000,
+        [((1, queries), F32), ((queries, width), F32), ((n, width), BF),
+         ((queries, half // 2), F32), ((queries, half // 2), F32),
+         ((queries, n), BF), ((queries, n), BF)],
+        24 * MIB, 8 * queries * n * width, 6_000_000,
     )
 
     got = lax.ppermute(send, "core", SWAP)
     ang_got = lax.ppermute(ang_send, "core", SWAP)
+    loss, head_grad, keep, rel_keep = call(
+        keep_kernel, (loss, dquery, cosine, sine, low, rest, query, own, pick, ang_keep), [VMEM] * 10,
+        [((1, queries), F32), ((queries, width), BF), ((n, width), F32), ((rel_rows, half // 2), F32)],
+        12 * MIB, 4 * queries * n * width, 3_000_000,
+    )
     packed = call(
-        pack_kernel, (pick, keep, got, ang_keep, ang_got), [VMEM] * 5,
-        [((plane, piece_rows, LANES), BF)], 12 * MIB, 4 * rel_rows * queries * half, 4_000_000,
+        pack_kernel, (pick, keep, got, rel_keep, ang_got), [VMEM] * 5,
+        [((plane, piece_rows, LANES), BF)], 12 * MIB, 2 * rel_rows * queries * half, 4_000_000,
     )
     part = jnp.sum(exchange(packed, PLANE).astype(F32), axis=0).astype(BF)
     part = jnp.sum(exchange(copies(part, line), LINE).astype(F32), axis=0).astype(BF)
@@ -362,16 +398,17 @@
     other_sum = lax.ppermute(own_sum, "core", SWAP)
     shapes = [(entity_table.shape, BF), ((rels, half), F32)]
     part = pltpu.VMEM((rels, half // 2), F32)
+    number = pltpu.SMEM(numbers.shape, jnp.int32)
     partial = call(
-        place_own_kernel, (numbers, own_sum), [SMEM, VMEM], shapes,
+        place_own_kernel, (numbers, own_sum), [ANY, VMEM], shapes,
         8 * MIB, 1_000_000, 2_000_000,
-        [pltpu.VMEM(entity_table.shape, BF), part, pltpu.SemaphoreType.DMA((2,))], HBM,
+        [pltpu.VMEM(entity_table.shape, BF), part, number, pltpu.SemaphoreType.DMA((3,))], HBM,
     )
     table_grad, rel_grad = call(
         place_other_kernel, (numbers, own_sum, other_sum, *partial),
-        [SMEM, VMEM, VMEM, HBM, HBM], shapes, 8 * MIB, 1_000_000, 2_000_000,
-        [pltpu.VMEM((2, BLK, width), BF), pltpu.VMEM((BLK, width), F32), part,
-         pltpu.SemaphoreType.DMA((3,))],
+        [ANY, VMEM, VMEM, HBM, HBM], shapes, 8 * MIB, 1_000_000, 2_000_000,
+        [pltpu.VMEM((2, BLK, width), BF), pltpu.VMEM((BLK, width), F32), part, number,
+         pltpu.SemaphoreType.DMA((4,))],
         HBM, {3: 0, 4: 1},
     )
     return loss.reshape(queries), head_grad, table_grad, rel_grad

time: 124 us -> 122 us (0.984)
  waiting for transfers between devices: 3.33 us -> 1.82 us
    ppermute x1, waiting for transfers between devices: 1.9 us -> 0.07 us  [body(): ang_got = lax.ppermute(ang_send, 'core', SWAP)]
    pallas_call x7 -> x8, Pallas kernels: 10.9 us -> 10.6 us  [call(): pl.pallas_call(kernel, out_shape=shapes[0] if single else shapes, in_spec...]
  transfers between devices with their start and end apart: 6 -> 6, of which waited for: 3 -> 3; matrix products, arithmetic and copies ran while one was open for 2% -> 3% of each run, Pallas kernels for 4% -> 5%
where the time goes in v5:
time: 122 us
  blocking collectives  91.6 us (75%)
  starting transfers between devices  12.5 us (10%)
  Pallas kernels  10.6 us (9%)
  local copies, waits for them, and re-layouts  3.32 us (3%)
  waiting for transfers between devices  1.82 us (1%)
    all_to_all x6, blocking collectives, exchange(): return lax.all_to_all(x, axes, split_axis=0, concat_axis=0, tiled=True)  91.6 us
    pallas_call x8, Pallas kernels, call(): pl.pallas_call(kernel, out_shape=shapes[0] if single else shapes, in_spec...  10.6 us
    ppermute x1, starting transfers between devices, body(): other = lax.ppermute(own, 'core', SWAP)  4.37 us
    ppermute x1, starting transfers between devices, body(): other_sum = lax.ppermute(own_sum, 'core', SWAP)  4.18 us
    ppermute x1, starting transfers between devices, body(): passed = lax.ppermute(passed, 'core', SWAP)  3.29 us
    gather x1, local copies, waits for them, and re-layouts, body(): heads = jnp.take(entity_table, head_ids, axis=0, mode='clip')  3.04 us
  transfers between devices with their start and end apart: 6, of which 3 were waited for; matrix products, arithmetic and copies ran while one was open for 3% of the time, Pallas kernels for 5%

profile of v5, /device:TPU:1, one launch (start us, length us, event | category | flops | bytes accessed | tf_op | source)
XLA Modules:
  0.0 121.7 jit_solution(7224226235820603607)
XLA Ops:
  0.6 0.7 multiply_add_fusion.number_ref.numbers_ref
  1.3 0.7 shard_map.103
  2.0 3.3 %collective-permute-start.1 = (bf16[128,1024]{1,0:T(8,128)(2,1)S(1)}, bf16[128,1024]{1,0:T(8,128)(2,1)S(1)}, u32[]{:S(2)}, u32[]{:S(2)}) collective-permute-start(bf16[128,1024]{1,0:T(8,128)(2,1)S(1)} %get-tuple-element.30), channel_id=1, source_target_pairs={{0,2},{2,0},{1,3},{3,1},{4,6},{6,4},{5,7},{7,5},{8,10},{10,8},{9,1... | collective-permute-start | bytes 786440 | tf_op jit(solution)/shard_map/ppermute | solution.py:352
  5.3 1.2 collective-permute-done.1
  6.5 0.0 copy-start.3
  6.5 12.4 %all_to_all.30 = bf16[16,8,1024]{2,1,0:T(8,128)(2,1)S(1)} all-to-all(bf16[16,8,1024]{2,1,0:T(8,128)(2,1)S(1)} %add_bitcast_fusion), channel_id=1, replica_groups=mesh['x'=4,'y'=4,'zl'=4,'core'=2,'grp'=2] {'x','y'}, dimensions={0} | all-to-all | bytes 524288 | tf_op jit(solution)/shard_map/all_to_all | solution.py:313
  19.0 16.0 %all_to_all.31 = bf16[8,8,1024]{2,1,0:T(8,128)(2,1)S(1)} all-to-all(bf16[8,8,1024]{2,1,0:T(8,128)(2,1)S(1)} %broadcast_in_dim.15), channel_id=1, replica_groups=mesh['x'=4,'y'=4,'zl'=4,'core'=2,'grp'=2] {'grp','zl'}, dimensions={0} | all-to-all | bytes 262144 | tf_op jit(solution)/shard_map/all_to_all | solution.py:313
  35.0 0.1 broadcast_in_dim.32
  35.1 12.4 %all_to_all.32 = bf16[16,16,1024]{2,1,0:T(8,128)(2,1)S(1)} all-to-all(bf16[16,16,1024]{2,1,0:T(8,128)(2,1)S(1)} %broadcast_in_dim.32), channel_id=1, replica_groups=mesh['x'=4,'y'=4,'zl'=4,'core'=2,'grp'=2] {'x','y'}, dimensions={0} | all-to-all | bytes 1048576 | tf_op jit(solution)/shard_map/all_to_all | solution.py:313
  47.4 4.4 %collective-permute-start.2 = (bf16[256,1024]{1,0:T(8,128)(2,1)S(1)}, bf16[256,1024]{1,0:T(8,128)(2,1)S(1)}, u32[]{:S(2)}, u32[]{:S(2)}) collective-permute-start(bf16[256,1024]{1,0:T(8,128)(2,1)S(1)} %bitcast.10), channel_id=1, source_target_pairs={{0,2},{2,0},{1,3},{3,1},{4,6},{6,4},{5,7},{7,5},{8,10},{10,8},{9,1... | collective-permute-start | bytes 1572872 | tf_op jit(solution)/shard_map/ppermute | solution.py:360
  51.8 0.0 copy-start
  51.8 3.0 %gather_fusion = bf16[256,1024]{1,0:T(8,128)(2,1)S(1)} fusion(bf16[512,1024]{1,0:T(8,128)(2,1)} %table_ref.1, s32[1024]{0:T(1024)S(1)} %pad_clamp_fusion), kind=kCustom, calls=%fused_computation | custom fusion | bytes 1049600 | tf_op jit(solution)/shard_map/jit(_take)/gather | solution.py:362
  54.9 0.0 copy-start.2
  54.9 2.2 %shard_map.102 = (f32[256,512]{1,0:T(8,128)S(1)}, f32[256,512]{1,0:T(8,128)S(1)}) custom-call(s32[256]{0:T(256)S(1)} %copy-done.1, f32[822,512]{1,0:T(8,128)S(1)} %copy-done), custom_call_target="tpu_custom_call" | custom-call | flops 10000000 | bytes 2000000 | tf_op jit(solution)/shard_map/pallas_call | solution.py:323
  57.1 1.0 shard_map.104
  58.2 1.9 %shard_map.105 = (f32[1,256]{1,0:T(1,128)S(1)}, f32[256,1024]{1,0:T(8,128)S(1)}, bf16[256,1024]{1,0:T(8,128)(2,1)S(1)}, f32[256,256]{1,0:T(8,128)S(1)}, f32[256,...) custom-call(bf16[256,1024]{1,0:T(8,128)(2,1)S(1)} %gather_fusion, ...), custom_call_target="tpu_custom_call" | custom-call | flops 536870912 | bytes 6000000 | tf_op jit(solution)/shard_map/pallas_call | solution.py:323
  60.0 0.6 collective-permute-start.3
  60.6 0.1 collective-permute-start.4
  60.7 1.7 %shard_map.106 = (f32[1,256]{1,0:T(1,128)}, bf16[256,1024]{1,0:T(8,128)(2,1)}, f32[256,1024]{1,0:T(8,128)S(1)}, f32[832,256]{1,0:T(8,128)S(1)}) custom-call(f32[1,256]{1,0:T(1,128)S(1)} %get-tuple-element.34.loss_in_ref, f32[256,1024]{1,0:T(8,128)S(1)} %get-tuple-element.35.dquery_ref, f32[256,512]{1,0:T(8,128)S(1)} %get-tuple-element.27.cos_ref, ...), custom_call_target="tpu_custom_call" | custom-call | flops 268435456 | bytes 3000000 | tf_op jit(solution)/shard_map/pallas_call | solution.py:323
  62.5 0.1 collective-permute-done.4.ang_got_ref
  62.5 0.5 shard_map.107
  63.1 17.3 %all_to_all.33 = bf16[16,232,128]{2,1,0:T(8,128)(2,1)S(1)} all-to-all(bf16[16,232,128]{2,1,0:T(8,128)(2,1)S(1)} %shard_map.107), channel_id=1, replica_groups=mesh['x'=4,'y'=4,'zl'=4,'core'=2,'grp'=2] {'x','y'}, dimensions={0} | all-to-all | bytes 1900544 | tf_op jit(solution)/shard_map/all_to_all | solution.py:313
  80.4 0.1 reduce_sum.50
  80.5 0.1 broadcast_in_dim.33
  80.6 15.7 %all_to_all.34 = bf16[8,232,128]{2,1,0:T(8,128)(2,1)S(1)} all-to-all(bf16[8,232,128]{2,1,0:T(8,128)(2,1)S(1)} %broadcast_in_dim.33), channel_id=1, replica_groups=mesh['x'=4,'y'=4,'zl'=4,'core'=2,'grp'=2] {'grp','zl'}, dimensions={0} | all-to-all | bytes 950272 | tf_op jit(solution)/shard_map/all_to_all | solution.py:313
  96.3 0.1 reduce_sum.51
  96.4 0.1 broadcast_in_dim.34
  96.5 17.8 %all_to_all.35.own_ref = bf16[16,232,128]{2,1,0:T(8,128)(2,1)S(1)} all-to-all(bf16[16,232,128]{2,1,0:T(8,128)(2,1)S(1)} %broadcast_in_dim.34), channel_id=1, replica_groups=mesh['x'=4,'y'=4,'zl'=4,'core'=2,'grp'=2] {'x','y'}, dimensions={0} | all-to-all | bytes 1900544 | tf_op jit(solution)/shard_map/all_to_all | solution.py:313
  114.3 4.2 %collective-permute-start.5 = (bf16[16,232,128]{2,1,0:T(8,128)(2,1)S(1)}, bf16[16,232,128]{2,1,0:T(8,128)(2,1)S(1)}, u32[]{:S(2)}, u32[]{:S(2)}) collective-permute-start(bf16[16,232,128]{2,1,0:T(8,128)(2,1)S(1)} %all_to_all.35.own_ref), channel_id=1, source_target_pairs={{0,2},{2,0},{1,3},{3,1},{4,6},{6,4},{5,7},{7,5},{8,10},{10,8},{9,1... | collective-permute-start | bytes 2850824 | tf_op jit(solution)/shard_map/ppermute | solution.py:398
  118.5 1.6 %shard_map.108 = (bf16[512,1024]{1,0:T(8,128)(2,1)}, f32[822,512]{1,0:T(8,128)}) custom-call(s32[4]{0:T(128)S(1)} %multiply_add_fusion.number_ref.numbers_ref, bf16[16,232,128]{2,1,0:T(8,128)(2,1)S(1)} %all_to_all.35.own_ref), custom_call_target="tpu_custom_call" | custom-call | flops 1000000 | bytes 2000000 | tf_op jit(solution)/shard_map/pallas_call | solution.py:323
  120.1 0.6 collective-permute-done.5.other_ref
  120.7 1.0 shard_map.109
  (14 shorter events, 0.1 us)
Async XLA Ops:
  2.0 4.5 %collective-permute-start.1 = (bf16[128,1024]{1,0:T(8,128)(2,1)S(1)}, bf16[128,1024]{1,0:T(8,128)(2,1)S(1)}, u32[]{:S(2)}, u32[]{:S(2)}) collective-permute-start(bf16[128,1024]{1,0:T(8,128)(2,1)S(1)} %get-tuple-element.30), channel_id=1, source_target_pairs={{0,2},{2,0},{1,3},{3,1},{4,6},{6,4},{5,7},{7,5},{8,10},{10,8},{9,1... | collective-permute-start | bytes 786440 | tf_op jit(solution)/shard_map/ppermute | solution.py:352
  6.5 45.3 %copy-start.1 = (s32[256]{0:T(256)S(1)}, s32[256]{0:T(256)}, u32[]{:S(2)}) copy-start(s32[256]{0:T(256)} %ids_ref.1) | copy-start | bytes 3076
  6.5 45.3 %copy-start.3 = (s32[256]{0:T(256)S(1)}, s32[256]{0:T(256)}, u32[]{:S(2)}) copy-start(s32[256]{0:T(256)} %param.9) | copy-start | bytes 3076
  47.4 10.7 %collective-permute-start.2 = (bf16[256,1024]{1,0:T(8,128)(2,1)S(1)}, bf16[256,1024]{1,0:T(8,128)(2,1)S(1)}, u32[]{:S(2)}, u32[]{:S(2)}) collective-permute-start(bf16[256,1024]{1,0:T(8,128)(2,1)S(1)} %bitcast.10), channel_id=1, source_target_pairs={{0,2},{2,0},{1,3},{3,1},{4,6},{6,4},{5,7},{7,5},{8,10},{10,8},{9,1... | collective-permute-start | bytes 1572872 | tf_op jit(solution)/shard_map/ppermute | solution.py:360
  51.8 5.3 %collective-permute-start = (s32[256]{0:T(256)S(1)}, s32[256]{0:T(256)S(1)}, u32[]{:S(2)}, u32[]{:S(2)}) collective-permute-start(s32[256]{0:T(256)S(1)} %copy-done.1), channel_id=1, source_target_pairs={{0,2},{2,0},{1,3},{3,1},{4,6},{6,4},{5,7},{7,5},{8,10},{10,8},{9,1... | collective-permute-start | bytes 3080 | tf_op jit(solution)/shard_map/ppermute | solution.py:353
  51.8 3.1 %copy-start = (f32[822,512]{1,0:T(8,128)S(1)}, f32[822,512]{1,0:T(8,128)}, u32[]{:S(2)}) copy-start(f32[822,512]{1,0:T(8,128)} %phases_ref.1) | copy-start | bytes 5050372
  54.9 2.2 %copy-start.2 = (s32[256]{0:T(256)S(1)}, s32[256]{0:T(256)}, u32[]{:S(2)}) copy-start(s32[256]{0:T(256)} %param.11) | copy-start | bytes 3076
  60.0 2.5 %collective-permute-start.3 = (bf16[256,1024]{1,0:T(8,128)(2,1)S(1)}, bf16[256,1024]{1,0:T(8,128)(2,1)S(1)}, u32[]{:S(2)}, u32[]{:S(2)}) collective-permute-start(bf16[256,1024]{1,0:T(8,128)(2,1)S(1)} %get-tuple-element.43), channel_id=1, source_target_pairs={{0,2},{2,0},{1,3},{3,1},{4,6},{6,4},{5,7},{7,5},{8,10},{10,8},{9,1... | collective-permute-start | bytes 1572872 | tf_op jit(solution)/shard_map/ppermute | solution.py:384
  60.6 1.9 %collective-permute-start.4 = (f32[256,256]{1,0:T(8,128)S(1)}, f32[256,256]{1,0:T(8,128)S(1)}, u32[]{:S(2)}, u32[]{:S(2)}) collective-permute-start(f32[256,256]{1,0:T(8,128)S(1)} %get-tuple-element.45), channel_id=1, source_target_pairs={{0,2},{2,0},{1,3},{3,1},{4,6},{6,4},{5,7},{7,5},{8,10},{10,8},{9,1... | collective-permute-start | bytes 786440 | tf_op jit(solution)/shard_map/ppermute | solution.py:385
  114.3 6.3 %collective-permute-start.5 = (bf16[16,232,128]{2,1,0:T(8,128)(2,1)S(1)}, bf16[16,232,128]{2,1,0:T(8,128)(2,1)S(1)}, u32[]{:S(2)}, u32[]{:S(2)}) collective-permute-start(bf16[16,232,128]{2,1,0:T(8,128)(2,1)S(1)} %all_to_all.35.own_ref), channel_id=1, source_target_pairs={{0,2},{2,0},{1,3},{3,1},{4,6},{6,4},{5,7},{7,5},{8,10},{10,8},{9,1... | collective-permute-start | bytes 2850824 | tf_op jit(solution)/shard_map/ppermute | solution.py:398

commit v6 on v5

--- a/solution.py
+++ b/solution.py
@@ -42,23 +42,42 @@
     return place
 
 
-def fetch_kernel(number_ref, table_ref, keep_ref, pass_ref, sem):
+def fetch_kernel(number_ref, table_ref, keep_ref, pass_ref, sems):
     core = lax.axis_index("core")
     grp = lax.axis_index("grp")
     me = own_shard()
     per = table_ref.shape[0] // BLK
-    for b, out_ref in ((2 * grp + core, keep_ref), (2 * grp + 1 - core, pass_ref)):
-
-        @pl.when(number_ref[b] // per == me)
+    parts = sems.shape[1]
+    size = BLK // parts
+    waits = []
+    for k, (b, out_ref) in enumerate(((2 * grp + core, keep_ref), (2 * grp + 1 - core, pass_ref))):
+        mine = number_ref[b] // per == me
+        start = pl.multiple_of(number_ref[b] % per * BLK, BLK)
+        loads = [
+            pltpu.make_async_copy(
+                table_ref.at[pl.ds(start + p * size, size)],
+                out_ref.at[pl.ds(p * size, size)],
+                sems.at[k, p],
+            )
+            for p in range(parts)
+        ]
+        waits.append((mine, loads))
+
+        @pl.when(mine)
         def _():
-            start = pl.multiple_of(number_ref[b] % per * BLK, BLK)
-            copy = pltpu.make_async_copy(table_ref.at[pl.ds(start, BLK)], out_ref, sem)
-            copy.start()
-            copy.wait()
-
-        @pl.when(number_ref[b] // per != me)
+            for load in loads:
+                load.start()
+
+        @pl.when(jnp.logical_not(mine))
         def _():
             out_ref[...] = jnp.zeros_like(out_ref)
+
+    for mine, loads in waits:
+
+        @pl.when(mine)
+        def _():
+            for load in loads:
+                load.wait()
 
 
 def cos_sin(x):
@@ -347,7 +366,7 @@
     numbers = block_owner * (entity_table.shape[0] // BLK) + block_local
     kept, passed = call(
         fetch_kernel, (numbers, entity_table), [SMEM, HBM],
-        [((BLK, width), BF)] * 2, FETCH, 100_000, 500_000, [pltpu.SemaphoreType.DMA],
+        [((BLK, width), BF)] * 2, FETCH, 100_000, 500_000, [pltpu.SemaphoreType.DMA((2, 4))],
     )
     passed = lax.ppermute(passed, "core", SWAP)
     ids_other = lax.ppermute(rel_ids, "core", SWAP)

time: 122 us -> 122 us (level)
  no operation moved by 1% of the time
where the time goes in v6:
time: 122 us
  blocking collectives  91.6 us (75%)
  starting transfers between devices  12.5 us (10%)
  Pallas kernels  10.6 us (9%)
  local copies, waits for them, and re-layouts  3.32 us (3%)
  waiting for transfers between devices  1.82 us (1%)
    all_to_all x6, blocking collectives, exchange(): return lax.all_to_all(x, axes, split_axis=0, concat_axis=0, tiled=True)  91.6 us
    pallas_call x8, Pallas kernels, call(): pl.pallas_call(kernel, out_shape=shapes[0] if single else shapes, in_spec...  10.6 us
    ppermute x1, starting transfers between devices, body(): other = lax.ppermute(own, 'core', SWAP)  4.37 us
    ppermute x1, starting transfers between devices, body(): other_sum = lax.ppermute(own_sum, 'core', SWAP)  4.18 us
    ppermute x1, starting transfers between devices, body(): passed = lax.ppermute(passed, 'core', SWAP)  3.29 us
    gather x1, local copies, waits for them, and re-layouts, body(): heads = jnp.take(entity_table, head_ids, axis=0, mode='clip')  3.04 us
  transfers between devices with their start and end apart: 6, of which 3 were waited for; matrix products, arithmetic and copies ran while one was open for 3% of the time, Pallas kernels for 5%

profile of v6, /device:TPU:1, one launch (start us, length us, event | category | flops | bytes accessed | tf_op | source)
XLA Modules:
  0.0 121.7 jit_solution(9879351105340183048)
XLA Ops:
  0.6 0.7 multiply_add_fusion.number_ref.numbers_ref
  1.3 0.7 shard_map.103
  2.0 3.3 %collective-permute-start.1 = (bf16[128,1024]{1,0:T(8,128)(2,1)S(1)}, bf16[128,1024]{1,0:T(8,128)(2,1)S(1)}, u32[]{:S(2)}, u32[]{:S(2)}) collective-permute-start(bf16[128,1024]{1,0:T(8,128)(2,1)S(1)} %get-tuple-element.30), channel_id=1, source_target_pairs={{0,2},{2,0},{1,3},{3,1},{4,6},{6,4},{5,7},{7,5},{8,10},{10,8},{9,1... | collective-permute-start | bytes 786440 | tf_op jit(solution)/shard_map/ppermute | solution.py:371
  5.3 1.2 collective-permute-done.1
  6.5 0.0 copy-start.3
  6.5 12.4 %all_to_all.30 = bf16[16,8,1024]{2,1,0:T(8,128)(2,1)S(1)} all-to-all(bf16[16,8,1024]{2,1,0:T(8,128)(2,1)S(1)} %add_bitcast_fusion), channel_id=1, replica_groups=mesh['x'=4,'y'=4,'zl'=4,'core'=2,'grp'=2] {'x','y'}, dimensions={0} | all-to-all | bytes 524288 | tf_op jit(solution)/shard_map/all_to_all | solution.py:332
  19.0 16.0 %all_to_all.31 = bf16[8,8,1024]{2,1,0:T(8,128)(2,1)S(1)} all-to-all(bf16[8,8,1024]{2,1,0:T(8,128)(2,1)S(1)} %broadcast_in_dim.15), channel_id=1, replica_groups=mesh['x'=4,'y'=4,'zl'=4,'core'=2,'grp'=2] {'grp','zl'}, dimensions={0} | all-to-all | bytes 262144 | tf_op jit(solution)/shard_map/all_to_all | solution.py:332
  35.0 0.1 broadcast_in_dim.32
  35.1 12.4 %all_to_all.32 = bf16[16,16,1024]{2,1,0:T(8,128)(2,1)S(1)} all-to-all(bf16[16,16,1024]{2,1,0:T(8,128)(2,1)S(1)} %broadcast_in_dim.32), channel_id=1, replica_groups=mesh['x'=4,'y'=4,'zl'=4,'core'=2,'grp'=2] {'x','y'}, dimensions={0} | all-to-all | bytes 1048576 | tf_op jit(solution)/shard_map/all_to_all | solution.py:332
  47.5 4.4 %collective-permute-start.2 = (bf16[256,1024]{1,0:T(8,128)(2,1)S(1)}, bf16[256,1024]{1,0:T(8,128)(2,1)S(1)}, u32[]{:S(2)}, u32[]{:S(2)}) collective-permute-start(bf16[256,1024]{1,0:T(8,128)(2,1)S(1)} %bitcast.10), channel_id=1, source_target_pairs={{0,2},{2,0},{1,3},{3,1},{4,6},{6,4},{5,7},{7,5},{8,10},{10,8},{9,1... | collective-permute-start | bytes 1572872 | tf_op jit(solution)/shard_map/ppermute | solution.py:379
  51.9 0.0 copy-start
  51.9 3.0 %gather_fusion = bf16[256,1024]{1,0:T(8,128)(2,1)S(1)} fusion(bf16[512,1024]{1,0:T(8,128)(2,1)} %table_ref.1, s32[1024]{0:T(1024)S(1)} %pad_clamp_fusion), kind=kCustom, calls=%fused_computation | custom fusion | bytes 1049600 | tf_op jit(solution)/shard_map/jit(_take)/gather | solution.py:381
  54.9 0.0 copy-start.2
  55.0 2.2 %shard_map.102 = (f32[256,512]{1,0:T(8,128)S(1)}, f32[256,512]{1,0:T(8,128)S(1)}) custom-call(s32[256]{0:T(256)S(1)} %copy-done.1, f32[822,512]{1,0:T(8,128)S(1)} %copy-done), custom_call_target="tpu_custom_call" | custom-call | flops 10000000 | bytes 2000000 | tf_op jit(solution)/shard_map/pallas_call | solution.py:342
  57.2 1.0 shard_map.104
  58.2 1.9 %shard_map.105 = (f32[1,256]{1,0:T(1,128)S(1)}, f32[256,1024]{1,0:T(8,128)S(1)}, bf16[256,1024]{1,0:T(8,128)(2,1)S(1)}, f32[256,256]{1,0:T(8,128)S(1)}, f32[256,...) custom-call(bf16[256,1024]{1,0:T(8,128)(2,1)S(1)} %gather_fusion, ...), custom_call_target="tpu_custom_call" | custom-call | flops 536870912 | bytes 6000000 | tf_op jit(solution)/shard_map/pallas_call | solution.py:342
  60.1 0.6 collective-permute-start.3
  60.7 0.1 collective-permute-start.4
  60.8 1.7 %shard_map.106 = (f32[1,256]{1,0:T(1,128)}, bf16[256,1024]{1,0:T(8,128)(2,1)}, f32[256,1024]{1,0:T(8,128)S(1)}, f32[832,256]{1,0:T(8,128)S(1)}) custom-call(f32[1,256]{1,0:T(1,128)S(1)} %get-tuple-element.34.loss_in_ref, f32[256,1024]{1,0:T(8,128)S(1)} %get-tuple-element.35.dquery_ref, f32[256,512]{1,0:T(8,128)S(1)} %get-tuple-element.27.cos_ref, ...), custom_call_target="tpu_custom_call" | custom-call | flops 268435456 | bytes 3000000 | tf_op jit(solution)/shard_map/pallas_call | solution.py:342
  62.5 0.1 collective-permute-done.4.ang_got_ref
  62.6 0.5 shard_map.107
  63.1 17.3 %all_to_all.33 = bf16[16,232,128]{2,1,0:T(8,128)(2,1)S(1)} all-to-all(bf16[16,232,128]{2,1,0:T(8,128)(2,1)S(1)} %shard_map.107), channel_id=1, replica_groups=mesh['x'=4,'y'=4,'zl'=4,'core'=2,'grp'=2] {'x','y'}, dimensions={0} | all-to-all | bytes 1900544 | tf_op jit(solution)/shard_map/all_to_all | solution.py:332
  80.5 0.1 reduce_sum.50
  80.6 0.1 broadcast_in_dim.33
  80.7 15.7 %all_to_all.34 = bf16[8,232,128]{2,1,0:T(8,128)(2,1)S(1)} all-to-all(bf16[8,232,128]{2,1,0:T(8,128)(2,1)S(1)} %broadcast_in_dim.33), channel_id=1, replica_groups=mesh['x'=4,'y'=4,'zl'=4,'core'=2,'grp'=2] {'grp','zl'}, dimensions={0} | all-to-all | bytes 950272 | tf_op jit(solution)/shard_map/all_to_all | solution.py:332
  96.4 0.1 reduce_sum.51
  96.4 0.1 broadcast_in_dim.34
  96.6 17.8 %all_to_all.35.own_ref = bf16[16,232,128]{2,1,0:T(8,128)(2,1)S(1)} all-to-all(bf16[16,232,128]{2,1,0:T(8,128)(2,1)S(1)} %broadcast_in_dim.34), channel_id=1, replica_groups=mesh['x'=4,'y'=4,'zl'=4,'core'=2,'grp'=2] {'x','y'}, dimensions={0} | all-to-all | bytes 1900544 | tf_op jit(solution)/shard_map/all_to_all | solution.py:332
  114.4 4.2 %collective-permute-start.5 = (bf16[16,232,128]{2,1,0:T(8,128)(2,1)S(1)}, bf16[16,232,128]{2,1,0:T(8,128)(2,1)S(1)}, u32[]{:S(2)}, u32[]{:S(2)}) collective-permute-start(bf16[16,232,128]{2,1,0:T(8,128)(2,1)S(1)} %all_to_all.35.own_ref), channel_id=1, source_target_pairs={{0,2},{2,0},{1,3},{3,1},{4,6},{6,4},{5,7},{7,5},{8,10},{10,8},{9,1... | collective-permute-start | bytes 2850824 | tf_op jit(solution)/shard_map/ppermute | solution.py:417
  118.6 1.6 %shard_map.108 = (bf16[512,1024]{1,0:T(8,128)(2,1)}, f32[822,512]{1,0:T(8,128)}) custom-call(s32[4]{0:T(128)S(1)} %multiply_add_fusion.number_ref.numbers_ref, bf16[16,232,128]{2,1,0:T(8,128)(2,1)S(1)} %all_to_all.35.own_ref), custom_call_target="tpu_custom_call" | custom-call | flops 1000000 | bytes 2000000 | tf_op jit(solution)/shard_map/pallas_call | solution.py:342
  120.1 0.6 collective-permute-done.5.other_ref
  120.7 1.0 shard_map.109
  (14 shorter events, 0.1 us)
Async XLA Ops:
  2.0 4.5 %collective-permute-start.1 = (bf16[128,1024]{1,0:T(8,128)(2,1)S(1)}, bf16[128,1024]{1,0:T(8,128)(2,1)S(1)}, u32[]{:S(2)}, u32[]{:S(2)}) collective-permute-start(bf16[128,1024]{1,0:T(8,128)(2,1)S(1)} %get-tuple-element.30), channel_id=1, source_target_pairs={{0,2},{2,0},{1,3},{3,1},{4,6},{6,4},{5,7},{7,5},{8,10},{10,8},{9,1... | collective-permute-start | bytes 786440 | tf_op jit(solution)/shard_map/ppermute | solution.py:371
  6.5 45.3 %copy-start.1 = (s32[256]{0:T(256)S(1)}, s32[256]{0:T(256)}, u32[]{:S(2)}) copy-start(s32[256]{0:T(256)} %ids_ref.1) | copy-start | bytes 3076
  6.5 45.3 %copy-start.3 = (s32[256]{0:T(256)S(1)}, s32[256]{0:T(256)}, u32[]{:S(2)}) copy-start(s32[256]{0:T(256)} %param.9) | copy-start | bytes 3076
  47.5 10.7 %collective-permute-start.2 = (bf16[256,1024]{1,0:T(8,128)(2,1)S(1)}, bf16[256,1024]{1,0:T(8,128)(2,1)S(1)}, u32[]{:S(2)}, u32[]{:S(2)}) collective-permute-start(bf16[256,1024]{1,0:T(8,128)(2,1)S(1)} %bitcast.10), channel_id=1, source_target_pairs={{0,2},{2,0},{1,3},{3,1},{4,6},{6,4},{5,7},{7,5},{8,10},{10,8},{9,1... | collective-permute-start | bytes 1572872 | tf_op jit(solution)/shard_map/ppermute | solution.py:379
  51.8 5.3 %collective-permute-start = (s32[256]{0:T(256)S(1)}, s32[256]{0:T(256)S(1)}, u32[]{:S(2)}, u32[]{:S(2)}) collective-permute-start(s32[256]{0:T(256)S(1)} %copy-done.1), channel_id=1, source_target_pairs={{0,2},{2,0},{1,3},{3,1},{4,6},{6,4},{5,7},{7,5},{8,10},{10,8},{9,1... | collective-permute-start | bytes 3080 | tf_op jit(solution)/shard_map/ppermute | solution.py:372
  51.9 3.1 %copy-start = (f32[822,512]{1,0:T(8,128)S(1)}, f32[822,512]{1,0:T(8,128)}, u32[]{:S(2)}) copy-start(f32[822,512]{1,0:T(8,128)} %phases_ref.1) | copy-start | bytes 5050372
  54.9 2.2 %copy-start.2 = (s32[256]{0:T(256)S(1)}, s32[256]{0:T(256)}, u32[]{:S(2)}) copy-start(s32[256]{0:T(256)} %param.11) | copy-start | bytes 3076
  60.1 2.5 %collective-permute-start.3 = (bf16[256,1024]{1,0:T(8,128)(2,1)S(1)}, bf16[256,1024]{1,0:T(8,128)(2,1)S(1)}, u32[]{:S(2)}, u32[]{:S(2)}) collective-permute-start(bf16[256,1024]{1,0:T(8,128)(2,1)S(1)} %get-tuple-element.43), channel_id=1, source_target_pairs={{0,2},{2,0},{1,3},{3,1},{4,6},{6,4},{5,7},{7,5},{8,10},{10,8},{9,1... | collective-permute-start | bytes 1572872 | tf_op jit(solution)/shard_map/ppermute | solution.py:403
  60.7 1.9 %collective-permute-start.4 = (f32[256,256]{1,0:T(8,128)S(1)}, f32[256,256]{1,0:T(8,128)S(1)}, u32[]{:S(2)}, u32[]{:S(2)}) collective-permute-start(f32[256,256]{1,0:T(8,128)S(1)} %get-tuple-element.45), channel_id=1, source_target_pairs={{0,2},{2,0},{1,3},{3,1},{4,6},{6,4},{5,7},{7,5},{8,10},{10,8},{9,1... | collective-permute-start | bytes 786440 | tf_op jit(solution)/shard_map/ppermute | solution.py:404
  114.4 6.3 %collective-permute-start.5 = (bf16[16,232,128]{2,1,0:T(8,128)(2,1)S(1)}, bf16[16,232,128]{2,1,0:T(8,128)(2,1)S(1)}, u32[]{:S(2)}, u32[]{:S(2)}) collective-permute-start(bf16[16,232,128]{2,1,0:T(8,128)(2,1)S(1)} %all_to_all.35.own_ref), channel_id=1, source_target_pairs={{0,2},{2,0},{1,3},{3,1},{4,6},{6,4},{5,7},{7,5},{8,10},{10,8},{9,1... | collective-permute-start | bytes 2850824 | tf_op jit(solution)/shard_map/ppermute | solution.py:417

commit v7 on v5

--- a/solution.py
+++ b/solution.py
@@ -124,7 +124,7 @@
 
 def main_kernel(
     heads_ref, query_ref, scores_ref, own_ref, other_ref, spot_ref, cos_ref, sin_ref,
-    loss_ref, dquery_ref, send_ref, ang_keep_ref, ang_send_ref, low_ref, rest_ref,
+    loss_ref, dquery_ref, send_ref, ang_keep_ref, low_ref, rest_ref,
 ):
     rows, half = cos_ref.shape
     n = own_ref.shape[0]
@@ -153,7 +153,7 @@
             low_ref[...] = low
             rest_ref[...] = rest
         else:
-            send_ref[...] = pulled(low, rest, query, cands[k]).astype(BF)
+            send_ref[:, : 2 * half] = pulled(low, rest, query, cands[k]).astype(BF)
     cosine = cos_ref[...]
     sine = sin_ref[...]
     qr, qi = rotated(heads_ref, cosine, sine)
@@ -163,7 +163,9 @@
     a, b = ang[:, : half // 2], ang[:, half // 2 :]
     first = lax.axis_index("core") == 0
     ang_keep_ref[...] = jnp.where(first, a, b)
-    ang_send_ref[...] = jnp.where(first, b, a)
+    hi, lo = halves(jnp.where(first, b, a))
+    send_ref[:, 2 * half : 2 * half + half // 2] = hi
+    send_ref[:, 2 * half + half // 2 :] = lo
 
 
 def pulled(low, rest, query, cand):
@@ -189,7 +191,7 @@
     rel_ref[...] = dot(sel, hi) + dot(sel, lo)
 
 
-def pack_kernel(pick_ref, keep_ref, got_ref, rel_ref, ang_got_ref, out_ref):
+def pack_kernel(pick_ref, keep_ref, got_ref, rel_ref, out_ref):
     pieces = out_ref.shape[0]
     per = keep_ref.shape[0] // pieces
     groups = keep_ref.shape[1] // LANES
@@ -197,8 +199,10 @@
         cols = slice(k * LANES, (k + 1) * LANES)
         grad = keep_ref[:, cols] + got_ref[:, cols].astype(F32)
         out_ref[:, k * per : (k + 1) * per, :] = grad.astype(BF).reshape(pieces, per, LANES)
-    hi, lo = halves(ang_got_ref[...])
-    sel = pick_ref[:, ang_got_ref.shape[0] :]
+    w = keep_ref.shape[1]
+    hi = got_ref[:, w : w + w // 4]
+    lo = got_ref[:, w + w // 4 :]
+    sel = pick_ref[:, got_ref.shape[0] :]
     total = (rel_ref[...] + (dot(sel, hi) + dot(sel, lo))).astype(BF)
     base = groups * per
     size = out_ref.shape[1] - base
@@ -373,23 +377,22 @@
         12 * MIB, 4 * queries * n * width, 4_000_000,
     )
 
-    loss, dquery, send, ang_keep, ang_send, low, rest = call(
+    loss, dquery, send, ang_keep, low, rest = call(
         main_kernel, (heads, query, scores, own, other, spot, cosine, sine), [VMEM] * 8,
-        [((1, queries), F32), ((queries, width), F32), ((n, width), BF),
-         ((queries, half // 2), F32), ((queries, half // 2), F32),
+        [((1, queries), F32), ((queries, width), F32), ((n, width + half), BF),
+         ((queries, half // 2), F32),
          ((queries, n), BF), ((queries, n), BF)],
         24 * MIB, 8 * queries * n * width, 6_000_000,
     )
 
     got = lax.ppermute(send, "core", SWAP)
-    ang_got = lax.ppermute(ang_send, "core", SWAP)
     loss, head_grad, keep, rel_keep = call(
         keep_kernel, (loss, dquery, cosine, sine, low, rest, query, own, pick, ang_keep), [VMEM] * 10,
         [((1, queries), F32), ((queries, width), BF), ((n, width), F32), ((rel_rows, half // 2), F32)],
         12 * MIB, 4 * queries * n * width, 3_000_000,
     )
     packed = call(
-        pack_kernel, (pick, keep, got, rel_keep, ang_got), [VMEM] * 5,
+        pack_kernel, (pick, keep, got, rel_keep), [VMEM] * 4,
         [((plane, piece_rows, LANES), BF)], 12 * MIB, 2 * rel_rows * queries * half, 4_000_000,
     )
     part = jnp.sum(exchange(packed, PLANE).astype(F32), axis=0).astype(BF)

time: 122 us -> 122 us (level)
  transfers between devices with their start and end apart: 6 -> 5, of which waited for: 3 -> 3; matrix products, arithmetic and copies ran while one was open for 3% -> 3% of each run, Pallas kernels for 5% -> 5%
where the time goes in v7:
time: 122 us
  blocking collectives  91.7 us (75%)
  starting transfers between devices  12.4 us (10%)
  Pallas kernels  10.6 us (9%)
  local copies, waits for them, and re-layouts  3.32 us (3%)
  waiting for transfers between devices  1.91 us (2%)
    all_to_all x6, blocking collectives, exchange(): return lax.all_to_all(x, axes, split_axis=0, concat_axis=0, tiled=True)  91.7 us
    pallas_call x8, Pallas kernels, call(): pl.pallas_call(kernel, out_shape=shapes[0] if single else shapes, in_spec...  10.6 us
    ppermute x1, starting transfers between devices, body(): other = lax.ppermute(own, 'core', SWAP)  4.37 us
    ppermute x1, starting transfers between devices, body(): other_sum = lax.ppermute(own_sum, 'core', SWAP)  4.18 us
    ppermute x1, starting transfers between devices, body(): passed = lax.ppermute(passed, 'core', SWAP)  3.29 us
    gather x1, local copies, waits for them, and re-layouts, body(): heads = jnp.take(entity_table, head_ids, axis=0, mode='clip')  3.04 us
  transfers between devices with their start and end apart: 5, of which 3 were waited for; matrix products, arithmetic and copies ran while one was open for 3% of the time, Pallas kernels for 5%

profile of v7, /device:TPU:1, one launch (start us, length us, event | category | flops | bytes accessed | tf_op | source)
XLA Modules:
  0.0 121.8 jit_solution(2048444144328960742)
XLA Ops:
  0.6 0.7 multiply_add_fusion.number_ref.numbers_ref
  1.3 0.7 shard_map.103
  2.0 3.3 %collective-permute-start.1 = (bf16[128,1024]{1,0:T(8,128)(2,1)S(1)}, bf16[128,1024]{1,0:T(8,128)(2,1)S(1)}, u32[]{:S(2)}, u32[]{:S(2)}) collective-permute-start(bf16[128,1024]{1,0:T(8,128)(2,1)S(1)} %get-tuple-element.29), channel_id=1, source_target_pairs={{0,2},{2,0},{1,3},{3,1},{4,6},{6,4},{5,7},{7,5},{8,10},{10,8},{9,1... | collective-permute-start | bytes 786440 | tf_op jit(solution)/shard_map/ppermute | solution.py:356
  5.3 1.2 collective-permute-done.1
  6.5 0.0 copy-start.3
  6.5 12.4 %all_to_all.30 = bf16[16,8,1024]{2,1,0:T(8,128)(2,1)S(1)} all-to-all(bf16[16,8,1024]{2,1,0:T(8,128)(2,1)S(1)} %add_bitcast_fusion), channel_id=1, replica_groups=mesh['x'=4,'y'=4,'zl'=4,'core'=2,'grp'=2] {'x','y'}, dimensions={0} | all-to-all | bytes 524288 | tf_op jit(solution)/shard_map/all_to_all | solution.py:317
  19.0 16.0 %all_to_all.31 = bf16[8,8,1024]{2,1,0:T(8,128)(2,1)S(1)} all-to-all(bf16[8,8,1024]{2,1,0:T(8,128)(2,1)S(1)} %broadcast_in_dim.15), channel_id=1, replica_groups=mesh['x'=4,'y'=4,'zl'=4,'core'=2,'grp'=2] {'grp','zl'}, dimensions={0} | all-to-all | bytes 262144 | tf_op jit(solution)/shard_map/all_to_all | solution.py:317
  35.0 0.1 broadcast_in_dim.32
  35.1 12.4 %all_to_all.32 = bf16[16,16,1024]{2,1,0:T(8,128)(2,1)S(1)} all-to-all(bf16[16,16,1024]{2,1,0:T(8,128)(2,1)S(1)} %broadcast_in_dim.32), channel_id=1, replica_groups=mesh['x'=4,'y'=4,'zl'=4,'core'=2,'grp'=2] {'x','y'}, dimensions={0} | all-to-all | bytes 1048576 | tf_op jit(solution)/shard_map/all_to_all | solution.py:317
  47.4 4.4 %collective-permute-start.2 = (bf16[256,1024]{1,0:T(8,128)(2,1)S(1)}, bf16[256,1024]{1,0:T(8,128)(2,1)S(1)}, u32[]{:S(2)}, u32[]{:S(2)}) collective-permute-start(bf16[256,1024]{1,0:T(8,128)(2,1)S(1)} %bitcast.10), channel_id=1, source_target_pairs={{0,2},{2,0},{1,3},{3,1},{4,6},{6,4},{5,7},{7,5},{8,10},{10,8},{9,1... | collective-permute-start | bytes 1572872 | tf_op jit(solution)/shard_map/ppermute | solution.py:364
  51.8 0.0 collective-permute-start
  51.8 0.0 copy-start
  51.8 3.0 %gather_fusion = bf16[256,1024]{1,0:T(8,128)(2,1)S(1)} fusion(bf16[512,1024]{1,0:T(8,128)(2,1)} %table_ref.1, s32[1024]{0:T(1024)S(1)} %pad_clamp_fusion), kind=kCustom, calls=%fused_computation | custom fusion | bytes 1049600 | tf_op jit(solution)/shard_map/jit(_take)/gather | solution.py:366
  54.9 0.0 copy-start.2
  54.9 2.2 %shard_map.102 = (f32[256,512]{1,0:T(8,128)S(1)}, f32[256,512]{1,0:T(8,128)S(1)}) custom-call(s32[256]{0:T(256)S(1)} %copy-done.1, f32[822,512]{1,0:T(8,128)S(1)} %copy-done), custom_call_target="tpu_custom_call" | custom-call | flops 10000000 | bytes 2000000 | tf_op jit(solution)/shard_map/pallas_call | solution.py:327
  57.1 1.0 shard_map.104
  58.2 1.9 %shard_map.105 = (f32[1,256]{1,0:T(1,128)S(1)}, f32[256,1024]{1,0:T(8,128)S(1)}, bf16[256,1536]{1,0:T(8,128)(2,1)S(1)}, f32[256,256]{1,0:T(8,128)S(1)}, bf16[256...) custom-call(bf16[256,1024]{1,0:T(8,128)(2,1)S(1)} %gather_fusion, bf16[256,1024]{1,0:T(8,128)(2,1)S(1)} %get-tuple-element.30.query_ref, ...), custom_call_target="tpu_custom_call" | custom-call | flops 536870912 | bytes 6000000 | tf_op jit(solution)/shard_map/pallas_call | solution.py:327
  60.1 0.6 collective-permute-start.3
  60.7 1.7 %shard_map.106 = (f32[1,256]{1,0:T(1,128)}, bf16[256,1024]{1,0:T(8,128)(2,1)}, f32[256,1024]{1,0:T(8,128)S(1)}, f32[832,256]{1,0:T(8,128)S(1)}) custom-call(f32[1,256]{1,0:T(1,128)S(1)} %get-tuple-element.33.loss_in_ref, f32[256,1024]{1,0:T(8,128)S(1)} %get-tuple-element.34.dquery_ref, f32[256,512]{1,0:T(8,128)S(1)} %get-tuple-element.26.cos_ref, ...), custom_call_target="tpu_custom_call" | custom-call | flops 268435456 | bytes 3000000 | tf_op jit(solution)/shard_map/pallas_call | solution.py:327
  62.4 0.2 collective-permute-done.3.got_ref
  62.6 0.5 shard_map.107
  63.1 17.4 %all_to_all.33 = bf16[16,232,128]{2,1,0:T(8,128)(2,1)S(1)} all-to-all(bf16[16,232,128]{2,1,0:T(8,128)(2,1)S(1)} %shard_map.107), channel_id=1, replica_groups=mesh['x'=4,'y'=4,'zl'=4,'core'=2,'grp'=2] {'x','y'}, dimensions={0} | all-to-all | bytes 1900544 | tf_op jit(solution)/shard_map/all_to_all | solution.py:317
  80.5 0.1 reduce_sum.50
  80.6 0.1 broadcast_in_dim.33
  80.7 15.7 %all_to_all.34 = bf16[8,232,128]{2,1,0:T(8,128)(2,1)S(1)} all-to-all(bf16[8,232,128]{2,1,0:T(8,128)(2,1)S(1)} %broadcast_in_dim.33), channel_id=1, replica_groups=mesh['x'=4,'y'=4,'zl'=4,'core'=2,'grp'=2] {'grp','zl'}, dimensions={0} | all-to-all | bytes 950272 | tf_op jit(solution)/shard_map/all_to_all | solution.py:317
  96.4 0.1 reduce_sum.51
  96.5 0.1 broadcast_in_dim.34
  96.6 17.8 %all_to_all.35.own_ref = bf16[16,232,128]{2,1,0:T(8,128)(2,1)S(1)} all-to-all(bf16[16,232,128]{2,1,0:T(8,128)(2,1)S(1)} %broadcast_in_dim.34), channel_id=1, replica_groups=mesh['x'=4,'y'=4,'zl'=4,'core'=2,'grp'=2] {'x','y'}, dimensions={0} | all-to-all | bytes 1900544 | tf_op jit(solution)/shard_map/all_to_all | solution.py:317
  114.4 4.2 %collective-permute-start.4 = (bf16[16,232,128]{2,1,0:T(8,128)(2,1)S(1)}, bf16[16,232,128]{2,1,0:T(8,128)(2,1)S(1)}, u32[]{:S(2)}, u32[]{:S(2)}) collective-permute-start(bf16[16,232,128]{2,1,0:T(8,128)(2,1)S(1)} %all_to_all.35.own_ref), channel_id=1, source_target_pairs={{0,2},{2,0},{1,3},{3,1},{4,6},{6,4},{5,7},{7,5},{8,10},{10,8},{9,1... | collective-permute-start | bytes 2850824 | tf_op jit(solution)/shard_map/ppermute | solution.py:401
  118.6 1.6 %shard_map.108 = (bf16[512,1024]{1,0:T(8,128)(2,1)}, f32[822,512]{1,0:T(8,128)}) custom-call(s32[4]{0:T(128)S(1)} %multiply_add_fusion.number_ref.numbers_ref, bf16[16,232,128]{2,1,0:T(8,128)(2,1)S(1)} %all_to_all.35.own_ref), custom_call_target="tpu_custom_call" | custom-call | flops 1000000 | bytes 2000000 | tf_op jit(solution)/shard_map/pallas_call | solution.py:327
  120.2 0.6 collective-permute-done.4.other_ref
  120.8 1.0 shard_map.109
  (12 shorter events, 0.1 us)
Async XLA Ops:
  2.0 4.5 %collective-permute-start.1 = (bf16[128,1024]{1,0:T(8,128)(2,1)S(1)}, bf16[128,1024]{1,0:T(8,128)(2,1)S(1)}, u32[]{:S(2)}, u32[]{:S(2)}) collective-permute-start(bf16[128,1024]{1,0:T(8,128)(2,1)S(1)} %get-tuple-element.29), channel_id=1, source_target_pairs={{0,2},{2,0},{1,3},{3,1},{4,6},{6,4},{5,7},{7,5},{8,10},{10,8},{9,1... | collective-permute-start | bytes 786440 | tf_op jit(solution)/shard_map/ppermute | solution.py:356
  6.5 45.3 %copy-start.1 = (s32[256]{0:T(256)S(1)}, s32[256]{0:T(256)}, u32[]{:S(2)}) copy-start(s32[256]{0:T(256)} %ids_ref.1) | copy-start | bytes 3076
  6.5 45.3 %copy-start.3 = (s32[256]{0:T(256)S(1)}, s32[256]{0:T(256)}, u32[]{:S(2)}) copy-start(s32[256]{0:T(256)} %param.9) | copy-start | bytes 3076
  47.4 10.7 %collective-permute-start.2 = (bf16[256,1024]{1,0:T(8,128)(2,1)S(1)}, bf16[256,1024]{1,0:T(8,128)(2,1)S(1)}, u32[]{:S(2)}, u32[]{:S(2)}) collective-permute-start(bf16[256,1024]{1,0:T(8,128)(2,1)S(1)} %bitcast.10), channel_id=1, source_target_pairs={{0,2},{2,0},{1,3},{3,1},{4,6},{6,4},{5,7},{7,5},{8,10},{10,8},{9,1... | collective-permute-start | bytes 1572872 | tf_op jit(solution)/shard_map/ppermute | solution.py:364
  51.8 5.3 %collective-permute-start = (s32[256]{0:T(256)S(1)}, s32[256]{0:T(256)S(1)}, u32[]{:S(2)}, u32[]{:S(2)}) collective-permute-start(s32[256]{0:T(256)S(1)} %copy-done.1), channel_id=1, source_target_pairs={{0,2},{2,0},{1,3},{3,1},{4,6},{6,4},{5,7},{7,5},{8,10},{10,8},{9,1... | collective-permute-start | bytes 3080 | tf_op jit(solution)/shard_map/ppermute | solution.py:357
  51.8 3.1 %copy-start = (f32[822,512]{1,0:T(8,128)S(1)}, f32[822,512]{1,0:T(8,128)}, u32[]{:S(2)}) copy-start(f32[822,512]{1,0:T(8,128)} %phases_ref.1) | copy-start | bytes 5050372
  54.9 2.2 %copy-start.2 = (s32[256]{0:T(256)S(1)}, s32[256]{0:T(256)}, u32[]{:S(2)}) copy-start(s32[256]{0:T(256)} %param.11) | copy-start | bytes 3076
  60.1 2.5 %collective-permute-start.3 = (bf16[256,1536]{1,0:T(8,128)(2,1)S(1)}, bf16[256,1536]{1,0:T(8,128)(2,1)S(1)}, u32[]{:S(2)}, u32[]{:S(2)}) collective-permute-start(bf16[256,1536]{1,0:T(8,128)(2,1)S(1)} %get-tuple-element.42), channel_id=1, source_target_pairs={{0,2},{2,0},{1,3},{3,1},{4,6},{6,4},{5,7},{7,5},{8,10},{10,8},{9,1... | collective-permute-start | bytes 2359304 | tf_op jit(solution)/shard_map/ppermute | solution.py:388
  114.4 6.3 %collective-permute-start.4 = (bf16[16,232,128]{2,1,0:T(8,128)(2,1)S(1)}, bf16[16,232,128]{2,1,0:T(8,128)(2,1)S(1)}, u32[]{:S(2)}, u32[]{:S(2)}) collective-permute-start(bf16[16,232,128]{2,1,0:T(8,128)(2,1)S(1)} %all_to_all.35.own_ref), channel_id=1, source_target_pairs={{0,2},{2,0},{1,3},{3,1},{4,6},{6,4},{5,7},{7,5},{8,10},{10,8},{9,1... | collective-permute-start | bytes 2850824 | tf_op jit(solution)/shard_map/ppermute | solution.py:401
